TPU v7x, 256 devices: a whole 4x4x8 slice. The times are simulated.
256 devices in a mesh: shot: 8 (over x_hi, y), rcv: 32 (over x_lo, z, core).
Axes of the slice: x: 4 (x_hi: 2, x_lo: 2; x = x_hi * 2 + x_lo), y: 4, z: 8, core: 2. Of those that a mesh axis runs over, the one named last changes fastest.
Arguments:
- modeled: bfloat16 [2, 64, 8, 256, 512], P(None, 'shot', None, 'rcv'), may hold values from -9 to 9
- observed: bfloat16 [2, 8, 64, 256, 512], P(None, 'shot', 'rcv'), may hold values from -60 to 60
- mask: int32 [64, 8, 256], P('shot', None, 'rcv'), may hold values 0 or 1
- shot_order: int32 [64], replicated, may hold values from 0 to 63, as said below
- line_of_slot: int32 [8], replicated, may hold values from 0 to 7, as said below
- coupling: bfloat16 [2, 512, 512], replicated, may hold values from -0.25 to 0.25
- wavelet: float32 [2, 512], replicated, may hold values from -4 to 4
- damping: float32 [512], replicated, may hold values from 32768 to 524288
Outputs:
- new_wavelet: float32 [2, 512], replicated
- residual_out: bfloat16 [2, 64, 8, 256, 512], P(None, 'shot', None, 'rcv')
Inputs may be any that keep to these rules, and one draw needn't show every extreme that they name: Group g holds the shots shot_order[g * 8] to shot_order[(g + 1) * 8 - 1]; each shot number appears once. `line_of_slot`: each line appears in exactly one slot.
All inputs are finite; a program needn't handle non-finite values. No bound on the sum of `mask` on one device may be relied on, other than what follows from the above.
Results may differ from a plain program's by a relative error of at most 0.00045.
Values may be sent and summed in bfloat16 or wider, within the bound.
No kernel may reach another device: no remote copies, remote signals or barrier semaphores. Data moves between devices by JAX's collectives and lax.ppermute only.
A program may use at most 64 MiB of HBM per device.

v0:
```python
import jax
import jax.numpy as jnp
from jax import lax
from jax.sharding import PartitionSpec as P


def sent_to_all(array, axis):
    size = lax.axis_size(axis)
    return lax.all_to_all(
        jnp.broadcast_to(array[None], (size, *array.shape)), axis, 0, 0, tiled=True
    )


def of_everyone(array, axis):
    return sent_to_all(array, axis).sum(axis=0)


def in_one(arrays, axis):
    ends = [0]
    for a in arrays:
        ends.append(ends[-1] + a.size)
    subtotal = of_everyone(jnp.concatenate([a.ravel() for a in arrays]), axis)
    return tuple((subtotal[b:e].reshape(a.shape) for a, b, e in zip(arrays, ends, ends[1:])))


def weigh(trace, coupling):
    real_part = jnp.dot(trace[0], coupling[0], preferred_element_type=jnp.float32) - jnp.dot(
        trace[1], coupling[1], preferred_element_type=jnp.float32
    )
    imag_part = jnp.dot(trace[0], coupling[1], preferred_element_type=jnp.float32) + jnp.dot(
        trace[1], coupling[0], preferred_element_type=jnp.float32
    )
    return jnp.stack([real_part, imag_part])


def per_device(modeled, observed, mask, shot_order, line_of_slot, coupling, wavelet, damping):
    group_size = modeled.shape[1]
    line_count = modeled.shape[2]
    slot_count = lax.axis_size("shot")
    stored = observed[:, 0]
    spread = lax.all_to_all(stored, "rcv", split_axis=2, concat_axis=1, tiled=True)
    grouped = jnp.take(spread, shot_order, axis=1)
    grouped = grouped.reshape(2, slot_count, group_size, grouped.shape[2], grouped.shape[3])
    arrived = lax.all_to_all(grouped, "shot", split_axis=1, concat_axis=1, tiled=True)
    inverse = (
        jnp.zeros((line_count,), jnp.int32)
        .at[line_of_slot]
        .set(jnp.arange(line_count, dtype=jnp.int32))
    )
    by_line = jnp.transpose(jnp.take(arrived, inverse, axis=1), (0, 2, 1, 3, 4))
    wd = weigh(by_line, coupling)
    wg = weigh(modeled, coupling)
    live = mask.astype(jnp.float32)[..., None]
    res_re = live * (wd[0] - (wavelet[0] * wg[0] - wavelet[1] * wg[1]))
    res_im = live * (wd[1] - (wavelet[0] * wg[1] + wavelet[1] * wg[0]))
    num_re = jnp.sum(wg[0] * res_re + wg[1] * res_im, axis=(0, 1, 2))
    num_im = jnp.sum(wg[0] * res_im - wg[1] * res_re, axis=(0, 1, 2))
    den = jnp.sum(live * (wg[0] * wg[0] + wg[1] * wg[1]), axis=(0, 1, 2))
    numerator = jnp.stack([num_re, num_im])
    numerator, den = in_one((numerator, den), "rcv")
    numerator, den = in_one((numerator, den), "shot")
    new_wavelet = wavelet + numerator / (den + damping)[None, :]
    out_re = live * (wd[0] - (new_wavelet[0] * wg[0] - new_wavelet[1] * wg[1]))
    out_im = live * (wd[1] - (new_wavelet[0] * wg[1] + new_wavelet[1] * wg[0]))
    return (new_wavelet, jnp.stack([out_re, out_im]).astype(jnp.bfloat16))


def solution(mesh):
    placed = (
        P(None, "shot", None, "rcv", None),
        P(None, "shot", "rcv", None, None),
        P("shot", None, "rcv"),
        P(),
        P(),
        P(),
        P(),
        P(),
    )
    return jax.shard_map(
        per_device,
        mesh=mesh,
        in_specs=placed,
        out_specs=(P(), P(None, "shot", None, "rcv", None)),
        check_vma=False,
    )
```

profile of v0, /device:TPU:8, one launch (start us, length us, event | category | flops | bytes accessed | tf_op | source)
XLA Modules:
  0.0 104.6 jit_solution(12052726027214672724)
XLA Ops:
  0.6 3.3 %copy.49 = bf16[2,1,2,256,512]{4,2,0,3,1:T(2,128)(2,1)} copy(bf16[2,1,2,256,512]{4,3,2,1,0:T(8,128)(2,1)} %param.9) | data formatting | bytes 2097152 | tf_op args[1]
  3.9 9.9 %all-to-all-start = ((bf16[2,2,256,512]{3,1,0,2:T(2,128)(2,1)}), bf16[2,2,256,512]{3,1,0,2:T(2,128)(2,1)S(1)}, u32[]{:S(2)}, u32[]{:S(2)}) async-start(bf16[2,2,256,512]{3,1,0,2:T(2,128)(2,1)} %bitcast.74), calls=%async_computation | async-start | bytes 2097152 | tf_op jit(solution)/shard_map/all_to_all | solution.py:41
  14.0 0.6 copy-done.11
  14.6 0.6 scatter_custom_fusion
  15.3 0.6 copy-done.8
  15.9 26.4 %all-to-all-done = bf16[2,2,256,512]{3,1,0,2:T(2,128)(2,1)S(1)} async-done(((bf16[2,2,256,512]{3,1,0,2:T(2,128)(2,1)}), bf16[2,2,256,512]{3,1,0,2:T(2,128)(2,1)S(1)}, u32[]{:S(2)}, u32[]{:S(2)}) %all-to-all-start) | async-done | bytes 1048608 | tf_op jit(solution)/shard_map/all_to_all | solution.py:41
  42.3 0.2 copy.48
  42.5 0.1 copy.29
  42.6 0.6 gather_fusion
  43.3 1.1 %copy_select_fusion.1 = bf16[2,8,8,8,512]{4,3,2,0,1:T(8,128)(2,1)} fusion(bf16[2,8,8,8,512]{4,3,0,2,1:T(8,128)(2,1)S(1)} %bitcast.77, pred[8,8]{1,0:T(8,128)(4,1)S(1)} %broadcast_in_dim.43), kind=kLoop, calls=%fused_computation.10 | loop fusion | flops 524288 | bytes 2097216 | tf_op jit(solution)/shard_map/jit(_take)/select_n | solution.py:42
  44.4 7.2 %all-to-all-start.1 = ((bf16[2,8,8,8,512]{4,3,2,0,1:T(8,128)(2,1)}), bf16[2,8,8,8,512]{4,3,2,0,1:T(8,128)(2,1)S(1)}, u32[]{:S(2)}, u32[]{:S(2)}) async-start(bf16[2,8,8,8,512]{4,3,2,0,1:T(8,128)(2,1)} %copy_select_fusion.1), calls=%async_computation.1 | async-start | bytes 2097152 | tf_op jit(solution)/shard_map/all_to_all | solution.py:44
  51.7 1.4 %fusion.5 = f32[8,8,8,512]{3,2,1,0:T(8,128)} fusion(bf16[2,8,8,8,512]{4,3,2,1,0:T(8,128)(2,1)S(1)} %copy-done.4, bf16[2,512,512]{2,1,0:T(8,128)(2,1)S(1)} %copy-done), kind=kOutput, calls=%fused_computation.26 | convolution fusion | flops 268435456 | bytes 2097152 | tf_op jit(solution)/shard_map/dot_general | solution.py:30
  53.1 0.4 fusion.13
  53.5 1.4 %convolution_subtract_fusion.1 = f32[8,8,8,512]{3,2,1,0:T(8,128)} fusion(f32[8,8,8,512]{3,2,1,0:T(8,128)S(1)} %fusion.13, bf16[2,8,8,8,512]{4,3,2,1,0:T(8,128)(2,1)S(1)} %copy-done.4, bf16[2,512,512]{2,1,0:T(8,128)(2,1)S(1)} %copy-done), kind=kOutput, calls=%fused_computation.6 | convolution fusion | flops 268697600 | bytes 3145728 | tf_op jit(solution)/shard_map/dot_general | solution.py:27
  54.9 9.8 %all-to-all-done.1 = bf16[2,8,8,8,512]{4,3,2,0,1:T(8,128)(2,1)S(1)} async-done(((bf16[2,8,8,8,512]{4,3,2,0,1:T(8,128)(2,1)}), bf16[2,8,8,8,512]{4,3,2,0,1:T(8,128)(2,1)S(1)}, u32[]{:S(2)}, u32[]{:S(2)}) %all-to-all-start.1) | async-done | bytes 1048608 | tf_op jit(solution)/shard_map/all_to_all | solution.py:44
  64.8 0.6 gather_fusion.1
  65.4 0.2 fusion
  65.6 0.4 fusion.3
  66.0 0.4 fusion.11
  66.5 0.4 convolution_add_fusion
  66.9 0.4 convolution_subtract_fusion
  67.4 0.7 copy-done.1
  68.1 0.6 copy-done.5
  68.8 0.4 copy-done.6
  69.1 2.1 %add_reduce_fusion = (f32[512]{0:T(512)S(1)}, f32[512]{0:T(512)S(1)}, f32[512]{0:T(512)S(1)}, f32[8,8,8,512]{3,2,1,0:T(8,128)}) fusion(f32[8,8,8,512]{3,2,1,0:T(8,128)S(1)} %convolution_add_fusion, f32[8,8,8,512]{3,2,1,0:T(8,128)S(1)} %copy-done.1, f32[8,8,8,512]{3,2,1,0:T(8,128)S(1)} %convolution_subtract_fusion, f32[512]{0:T(512)S(1)} %bitcast.83, ...), kind=kOutput, calls=%fused_computation.17 | convolution fusion | flops 274725376 | bytes 6334464 | tf_op jit(solution)/shard_map/dot_general | solution.py:30
  71.4 16.8 %all_to_all.35 = f32[32,1,1536]{2,1,0:T(1,128)S(1)} all-to-all(f32[32,1,1536]{2,1,0:T(1,128)S(1)} %broadcast_in_dim.48), channel_id=1, replica_groups=mesh['shot'=8,'rcv'=32] {'rcv'}, dimensions={0} | all-to-all | bytes 393216 | tf_op jit(solution)/shard_map/all_to_all | solution.py:9
  88.2 0.1 reduce_sum.48
  88.4 12.1 %all_to_all.36 = f32[8,1,1536]{2,1,0:T(1,128)S(1)} all-to-all(f32[8,1,1536]{2,1,0:T(1,128)S(1)} %broadcast_in_dim.49), channel_id=1, replica_groups=mesh['shot'=8,'rcv'=32] {'shot'}, dimensions={0} | all-to-all | bytes 98304 | tf_op jit(solution)/shard_map/all_to_all | solution.py:9
  100.6 0.7 copy-done.10
  101.3 0.6 copy-done.9
  101.9 1.6 %fusion.1 = (bf16[1,8,8,8,512]{4,3,2,1,0:T(8,128)(2,1)S(1)}, bf16[1,8,8,8,512]{4,3,2,1,0:T(8,128)(2,1)S(1)}) fusion(f32[8,8,8,512]{3,2,1,0:T(8,128)S(1)} %copy-done.3, f32[8,8,8,512]{3,2,1,0:T(8,128)} %get-tuple-element.11, f32[8,8,8,512]{3,2,1,0:T(8,128)S(1)} %copy-done.1, f32[512]{0:T(512)S(1)} %bitcast.81, f32[512]{0:T(512)S(1)} %bitcast.80, ...), kind=kLoop, calls=%fused_computation.20 | loop fusion | flops 3145728 | bytes 5249024 | tf_op jit(solution)/shard_map/stack | solution.py:65
  103.5 1.1 %pad_maximum_fusion = bf16[2,8,8,8,512]{4,3,2,1,0:T(8,128)(2,1)} fusion(bf16[1,8,8,8,512]{4,3,2,1,0:T(8,128)(2,1)S(1)} %get-tuple-element.6, bf16[1,8,8,8,512]{4,3,2,1,0:T(8,128)(2,1)S(1)} %get-tuple-element.5), kind=kLoop, calls=%fused_computation.7 | loop fusion | flops 524288 | bytes 2097152 | tf_op jit(solution)/shard_map/stack | solution.py:65
  (42 shorter events, 0.5 us)
Async XLA Ops:
  3.9 9.9 %copy-start.12 = (s32[64]{0:T(128)S(1)}, s32[64]{0:T(128)}, u32[]{:S(2)}) copy-start(s32[64]{0:T(128)} %param.11) | copy-start | bytes 772
  3.9 10.0 %copy-start.7 = (s32[8,8,8]{2,1,0:T(8,128)S(1)}, s32[8,8,8]{2,1,0:T(8,128)}, u32[]{:S(2)}) copy-start(s32[8,8,8]{2,1,0:T(8,128)} %param.10) | copy-start | bytes 6148
  3.9 38.4 %all-to-all-start = ((bf16[2,2,256,512]{3,1,0,2:T(2,128)(2,1)}), bf16[2,2,256,512]{3,1,0,2:T(2,128)(2,1)S(1)}, u32[]{:S(2)}, u32[]{:S(2)}) async-start(bf16[2,2,256,512]{3,1,0,2:T(2,128)(2,1)} %bitcast.74), calls=%async_computation | async-start | bytes 2097152 | tf_op jit(solution)/shard_map/all_to_all | solution.py:41
  13.9 0.7 copy-start.11
  15.2 0.7 copy-start.8
  44.4 7.2 %copy-start = (bf16[2,512,512]{2,1,0:T(8,128)(2,1)S(1)}, bf16[2,512,512]{2,1,0:T(8,128)(2,1)}, u32[]{:S(2)}) copy-start(bf16[2,512,512]{2,1,0:T(8,128)(2,1)} %param.13) | copy-start | bytes 3145732
  44.4 7.2 %copy-start.4 = (bf16[2,8,8,8,512]{4,3,2,1,0:T(8,128)(2,1)S(1)}, bf16[2,8,8,8,512]{4,3,2,1,0:T(8,128)(2,1)}, u32[]{:S(2)}) copy-start(bf16[2,8,8,8,512]{4,3,2,1,0:T(8,128)(2,1)} %param.8) | copy-start | bytes 3145732
  44.4 20.3 %all-to-all-start.1 = ((bf16[2,8,8,8,512]{4,3,2,0,1:T(8,128)(2,1)}), bf16[2,8,8,8,512]{4,3,2,0,1:T(8,128)(2,1)S(1)}, u32[]{:S(2)}, u32[]{:S(2)}) async-start(bf16[2,8,8,8,512]{4,3,2,0,1:T(8,128)(2,1)} %copy_select_fusion.1), calls=%async_computation.1 | async-start | bytes 2097152 | tf_op jit(solution)/shard_map/all_to_all | solution.py:44
  66.9 1.2 %copy-start.1 = (f32[8,8,8,512]{3,2,1,0:T(8,128)S(1)}, f32[8,8,8,512]{3,2,1,0:T(8,128)}, u32[]{:S(2)}) copy-start(f32[8,8,8,512]{3,2,1,0:T(8,128)} %convolution_subtract_fusion.1) | copy-start | bytes 3145732
  66.9 1.9 %copy-start.5 = (bf16[2,8,8,8,512]{4,3,2,1,0:T(8,128)(2,1)S(1)}, bf16[2,8,8,8,512]{4,3,2,1,0:T(8,128)(2,1)}, u32[]{:S(2)}) copy-start(bf16[2,8,8,8,512]{4,3,2,1,0:T(8,128)(2,1)} %param.8) | copy-start | bytes 3145732
  66.9 2.2 %copy-start.6 = (f32[8,8,8,512]{3,2,1,0:T(8,128)S(1)}, f32[8,8,8,512]{3,2,1,0:T(8,128)}, u32[]{:S(2)}) copy-start(f32[8,8,8,512]{3,2,1,0:T(8,128)} %fusion.5) | copy-start | bytes 3145732
  67.4 3.9 %copy-start.2 = (f32[8,8,8,512]{3,2,1,0:T(8,128)}, f32[8,8,8,512]{3,2,1,0:T(8,128)S(1)}, u32[]{:S(2)}) copy-start(f32[8,8,8,512]{3,2,1,0:T(8,128)S(1)} %convolution_subtract_fusion) | copy-start | bytes 3145732
  71.3 30.6 %copy-start.3 = (f32[8,8,8,512]{3,2,1,0:T(8,128)S(1)}, f32[8,8,8,512]{3,2,1,0:T(8,128)}, u32[]{:S(2)}) copy-start(f32[8,8,8,512]{3,2,1,0:T(8,128)} %copy-done.2) | copy-start | bytes 3145732
  100.6 0.7 copy-start.10
  101.3 0.6 copy-start.9
where the time goes:
time: 105 us
  waiting for transfers between devices  36.1 us (34%)
  blocking collectives  28.9 us (28%)
  starting transfers between devices  17.1 us (16%)
  local copies, waits for them, and re-layouts  10.1 us (10%)
  matrix products  7.15 us (7%)
  other arithmetic  4.23 us (4%)
    all_to_all x2, blocking collectives, sent_to_all(): lax.all_to_all(jnp.broadcast_to(array[None], (size, *array.shape)), axis,...  28.9 us
    all_to_all x1, waiting for transfers between devices, per_device(): lax.all_to_all(stored, 'rcv', split_axis=2, concat_axis=1, tiled=True)  26.4 us
    all_to_all x1, starting transfers between devices, per_device(): lax.all_to_all(stored, 'rcv', split_axis=2, concat_axis=1, tiled=True)  9.91 us
    all_to_all x1, waiting for transfers between devices, per_device(): lax.all_to_all(grouped, 'shot', split_axis=1, concat_axis=1, tiled=True)  9.76 us
    unnamed x28, local copies, waits for them, and re-layouts  7.58 us
    all_to_all x1, starting transfers between devices, per_device(): lax.all_to_all(grouped, 'shot', split_axis=1, concat_axis=1, tiled=True)  7.21 us
    another operation x2, other arithmetic, per_device(): return (new_wavelet, jnp.stack([out_re, out_im]).astype(jnp.bfloat16))  2.7 us
    dot_general x2, matrix products, weigh(): jnp.dot(trace[1], coupling[0], preferred_element_type=jnp.float32)  2.58 us
  transfers between devices with their start and end apart: 2, of which 2 were waited for; matrix products, arithmetic and copies ran while one was open for 4% of the time, Pallas kernels for 0%

commit v1 on v0

v1 whole, which is shorter than its diff:
```python
import jax
import jax.numpy as jnp
from jax import lax
from jax.experimental import pallas as pl
from jax.experimental.pallas import tpu as pltpu
from jax.sharding import Mesh, PartitionSpec as P

F32 = jnp.float32
BF16 = jnp.bfloat16
SHOT = ("xh", "y")
RCV = ("xl", "z", "c")
REST = ("xh", "y", "xl")

VM = pl.BlockSpec(memory_space=pltpu.VMEM)
SM = pl.BlockSpec(memory_space=pltpu.SMEM)
ANY = pl.BlockSpec(memory_space=pl.ANY)


def call(body, outs, in_specs, out_specs=None, scratch=(), limit=12 << 20, flops=0, nbytes=1 << 20):
    many = isinstance(outs, (tuple, list))
    return pl.pallas_call(
        body,
        out_shape=outs,
        in_specs=in_specs,
        out_specs=out_specs if out_specs is not None else ([VM] * len(outs) if many else VM),
        scratch_shapes=list(scratch),
        compiler_params=pltpu.CompilerParams(vmem_limit_bytes=limit),
        cost_estimate=pl.CostEstimate(flops=flops, bytes_accessed=nbytes, transcendentals=0),
    )


CHUNKS = 4


def k_spread(obs_ref, out_ref, buf, sem_in, sem_out):
    parts, pieces = obs_ref.shape[:2]
    step = pieces // CHUNKS
    ins, outs = [], []
    for q in range(CHUNKS):
        rows = pl.ds(q * step, step)
        for i in range(parts):
            ins.append(pltpu.make_async_copy(obs_ref.at[i, rows], buf.at[rows, i], sem_in.at[q, i]))
        outs.append(pltpu.make_async_copy(buf.at[rows], out_ref.at[rows], sem_out.at[q]))
    for c in ins:
        c.start()
    for q in range(CHUNKS):
        for i in range(parts):
            ins[q * parts + i].wait()
        outs[q].start()
    for c in outs:
        c.wait()


def k_couple(c_ref, out_ref):
    f = c_ref.shape[1]
    re, im = c_ref[0], c_ref[1]
    out_ref[0, :f] = re
    out_ref[0, f:] = -im
    out_ref[1, :f] = im
    out_ref[1, f:] = re


def k_mask(me_ref, slot_ref, mod_ref, mask_ref, live_ref, *out_refs):
    me = me_ref[0]
    shots, rb = mod_ref.shape[1], mod_ref.shape[3]
    f = mod_ref.shape[4]
    eye = lax.broadcasted_iota(jnp.int32, (rb, rb), 0) == lax.broadcasted_iota(jnp.int32, (rb, rb), 1)
    for b, out_ref in enumerate(out_refs):
        line = slot_ref[lax.bitwise_xor(me, b)]
        for s in range(shots):
            row = mask_ref[s, pl.ds(line, 1)].astype(F32)
            column = jnp.where(eye, row, 0.0).sum(axis=1, keepdims=True)
            rows = pl.ds(s * rb, rb)
            live_ref[b, rows] = jnp.broadcast_to(column, (rb, 128))
            live = jnp.broadcast_to(column, (rb, f)) > 0.5
            for c in range(2):
                x = mod_ref[c, s, line].astype(F32)
                out_ref[c, rows] = jnp.where(live, x, 0.0).astype(BF16)


def window(x, b_ref, d):
    return jnp.dot(x, b_ref[d], preferred_element_type=F32)


def k_window(*refs):
    xs, b_ref, out_ref = refs[:-2], refs[-2], refs[-1]
    x = jnp.concatenate([jnp.concatenate([x[c] for x in xs], axis=0) for c in range(2)], axis=1)
    out_ref[0] = window(x, b_ref, 0)
    out_ref[1] = window(x, b_ref, 1)


def k_window_own(me_ref, own_ref, live_ref, b_ref, out_ref, x_ref):
    me = me_ref[0]
    slots, _, rows, f = own_ref.shape
    for b in range(slots):
        k = lax.bitwise_xor(me, b)
        live = jnp.concatenate([live_ref[b]] * (f // live_ref.shape[2]), axis=1) > 0.5
        for c in range(2):
            x = own_ref[k, c].astype(F32)
            x_ref[b * rows : (b + 1) * rows, c * f : (c + 1) * f] = jnp.where(live, x, 0.0).astype(BF16)
    x = x_ref[...]
    out_ref[0] = window(x, b_ref, 0)
    out_ref[1] = window(x, b_ref, 1)


def k_group(order_ref, own_ref, out_ref):
    groups, _, rows, _ = out_ref.shape
    rb = own_ref.shape[2]
    size = rows // rb
    for g in range(groups):
        for s in range(size):
            n = order_ref[g * size + s]
            j = lax.shift_right_logical(n, 1)
            h = lax.bitwise_and(n, 1)
            for c in range(2):
                out_ref[g, c, s * rb : (s + 1) * rb] = own_ref[j, 2 * c + h]


def fold(x):
    return x.reshape(x.shape[0] // 8, 8, x.shape[1]).sum(axis=0).sum(axis=0, keepdims=True)


def k_cross(me_ref, order_ref, own_ref, b_ref, wg_ref, out_ref, x_ref):
    me = me_ref[0]
    rb, f = own_ref.shape[2:]
    size = order_ref.shape[0] // 8
    for b in range(8):
        g = lax.bitwise_xor(me, b)
        for s in range(size):
            n = order_ref[g * size + s]
            j = lax.shift_right_logical(n, 1)
            h = lax.bitwise_and(n, 1)
            row = (b * size + s) * rb
            for c in range(2):
                x_ref[row : row + rb, c * f : (c + 1) * f] = own_ref[j, 2 * c + h]
    x = x_ref[...]
    wd_re = window(x, b_ref, 0)
    wd_im = window(x, b_ref, 1)
    wg_re, wg_im = wg_ref[0], wg_ref[1]
    out_ref[0:1] = fold(wg_re * wd_re + wg_im * wd_im)
    out_ref[1:2] = fold(wg_re * wd_im - wg_im * wd_re)
    out_ref[2:3] = fold(wg_re * wg_re + wg_im * wg_im)


def k_final(me_ref, slot_ref, wd_ref, wg_ref, sums_ref, wav_ref, damp_ref, nw_ref, out_ref):
    me = me_ref[0]
    total = sums_ref[...].sum(axis=0)
    den = total[2:3]
    wav_re, wav_im = wav_ref[0:1], wav_ref[1:2]
    scale = den + damp_ref[...]
    nw_re = wav_re + (total[0:1] - wav_re * den) / scale
    nw_im = wav_im + (total[1:2] - wav_im * den) / scale
    nw_ref[0:1] = nw_re
    nw_ref[1:2] = nw_im
    _, shots, lines, rb, _ = out_ref.shape
    for b in range(lines):
        line = slot_ref[lax.bitwise_xor(me, b)]
        for s in range(shots):
            rows = pl.ds((b * shots + s) * rb, rb)
            wg_re, wg_im = wg_ref[0, rows], wg_ref[1, rows]
            out_ref[0, s, line] = (wd_ref[0, rows] - (nw_re * wg_re - nw_im * wg_im)).astype(BF16)
            out_ref[1, s, line] = (wd_ref[1, rows] - (nw_re * wg_im + nw_im * wg_re)).astype(BF16)


def swapped(x, axis, bit):
    size = lax.axis_size(axis)
    return lax.ppermute(x, axis, [(i, i ^ bit) for i in range(size)])


def sent_to_all(array, axis):
    size = lax.axis_size(axis)
    return lax.all_to_all(
        jnp.broadcast_to(array[None], (size, *array.shape)), axis, 0, 0, tiled=True
    )


def update(modeled, observed, mask, shot_order, line_of_slot, coupling, wavelet, damping):
    _, shots, lines, rb, f = modeled.shape
    slots = lax.axis_size(SHOT)
    held = observed.shape[2]
    pieces = lax.axis_size(RCV)
    rows = shots * rb
    traces = lines * rows
    flops = 8 * traces * f * f
    me = lax.axis_index(SHOT).astype(jnp.int32).reshape(1)

    own_spread = call(
        k_spread, jax.ShapeDtypeStruct((pieces, 2 * held, rb, f), BF16), [ANY], ANY,
        limit=60 << 20,
        scratch=[
            pltpu.VMEM((pieces, 2 * held, rb, f), BF16),
            pltpu.SemaphoreType.DMA((CHUNKS, 2 * held)),
            pltpu.SemaphoreType.DMA((CHUNKS,)),
        ],
    )(observed.reshape(2 * held, pieces, rb, f))
    own_natural = lax.all_to_all(own_spread, RCV, 0, 0, tiled=True)

    both = call(k_couple, jax.ShapeDtypeStruct((2, 2 * f, f), BF16), [VM])(coupling)
    piece = jax.ShapeDtypeStruct((2, rows, f), BF16)
    live, *masked = call(
        k_mask, (jax.ShapeDtypeStruct((slots, rows, 128), F32), *[piece] * slots),
        [SM, SM, VM, VM],
    )(me, line_of_slot, modeled, mask)
    wide = jax.ShapeDtypeStruct((2, traces, f), F32)
    arrived = [masked[0]]
    for b in range(1, slots):
        arrived.append(swapped(masked[b], SHOT, b))
    wg_here = call(k_window, wide, [VM] * (slots + 1), flops=flops)(*masked, both)
    wg_slot = call(k_window, wide, [VM] * (slots + 1), flops=flops)(*arrived, both)

    own_group = call(
        k_group, jax.ShapeDtypeStruct((slots, 2, rows, f), BF16), [SM, VM],
    )(shot_order, own_natural)
    own_here = lax.all_to_all(own_group, SHOT, 0, 0, tiled=True)
    sums = call(
        k_cross, jax.ShapeDtypeStruct((3, f), F32), [SM, SM, VM, VM, VM],
        scratch=[pltpu.VMEM((traces, 2 * f), BF16)], flops=flops,
    )(me, shot_order, own_natural, both, wg_slot)
    sums = sums.reshape(3 * f // 128, 128)
    for axis, bit in (("c", 1), ("z", 1), ("z", 2), ("z", 4)):
        sums = sums + swapped(sums, axis, bit)
    parts = sent_to_all(sums.reshape(1, 3 * f), REST).reshape(-1, 3, f)
    wd_here = call(
        k_window_own, wide, [SM, VM, VM, VM], flops=flops,
        scratch=[pltpu.VMEM((traces, 2 * f), BF16)],
    )(me, own_here, live, both)

    new_wavelet, residual = call(
        k_final,
        (jax.ShapeDtypeStruct((2, f), F32), jax.ShapeDtypeStruct(modeled.shape, BF16)),
        [SM, SM] + [VM] * 5,
    )(me, line_of_slot, wd_here, wg_here, parts, wavelet, damping.reshape(1, f))
    return new_wavelet, residual


def solution(mesh):
    fine = Mesh(mesh.devices.reshape(2, 4, 2, 8, 2), ("xh", "y", "xl", "z", "c"))
    placed = (
        P(None, SHOT, None, RCV, None),
        P(None, SHOT, RCV, None, None),
        P(SHOT, None, RCV),
        P(),
        P(),
        P(),
        P(),
        P(),
    )
    return jax.shard_map(
        update,
        mesh=fine,
        in_specs=placed,
        out_specs=(P(), P(None, SHOT, None, RCV, None)),
        check_vma=False,
    )
```

time: 105 us -> 103 us (0.981)
  blocking collectives: 28.9 us -> 0 us
  starting transfers between devices: 17.1 us -> 43.3 us
  Pallas kernels: 0 us -> 12.9 us
  matrix products: 7.15 us -> 0 us
  waiting for transfers between devices: 36.1 us -> 30.8 us
  other arithmetic: 4.23 us -> 1.84 us
  local copies, waits for them, and re-layouts: 10.1 us -> 12.4 us
    all_to_all x2 -> x0, blocking collectives: 28.9 us -> none  [sent_to_all(): lax.all_to_all(jnp.broadcast_to(array[None], (size, *array.shape)), axis,...]
    all_to_all x2 -> x3, waiting for transfers between devices: 36.1 us -> 11.7 us  [the longest x1 6.89 us: update(): own_here = lax.all_to_all(own_group, SHOT, 0, 0, tiled=True)]
    ppermute x0 -> x11, starting transfers between devices: none -> 21.6 us  [swapped(): return lax.ppermute(x, axis, [(i, i ^ bit) for i in range(size)])]
    ppermute x0 -> x11, waiting for transfers between devices: none -> 19.1 us  [swapped(): return lax.ppermute(x, axis, [(i, i ^ bit) for i in range(size)])]
    pallas_call x0 -> x9, Pallas kernels: none -> 12.9 us  [the longest x1 2.62 us: update(): call(k_window_own, wide, [SM, VM, VM, VM], flops=flops, scratch=[pltpu.VM...]
    dot_general x8 -> x0, matrix products: 7.15 us -> none  [the longest x2 2.58 us: weigh(): jnp.dot(trace[1], coupling[0], preferred_element_type=jnp.float32)]
    all_to_all x2 -> x3, starting transfers between devices: 17.1 us -> 21.7 us  [the longest x1 9.8 us: update(): own_natural = lax.all_to_all(own_spread, RCV, 0, 0, tiled=True)]
    unnamed x28 -> x52, local copies, waits for them, and re-layouts: 7.58 us -> 11 us
  transfers between devices with their start and end apart: 2 -> 14, of which waited for: 2 -> 9; matrix products, arithmetic and copies ran while one was open for 4% -> 1% of each run, Pallas kernels for 0% -> 4%
where the time goes in v1:
time: 103 us; the launch traced here: 102 us
  starting transfers between devices  43.3 us (42%)
  waiting for transfers between devices  30.8 us (30%)
  Pallas kernels  12.9 us (13%)
  local copies, waits for them, and re-layouts  12.4 us (12%)
  other arithmetic  1.84 us (2%)
    ppermute x11, starting transfers between devices, swapped(): return lax.ppermute(x, axis, [(i, i ^ bit) for i in range(size)])  21.6 us
    ppermute x11, waiting for transfers between devices, swapped(): return lax.ppermute(x, axis, [(i, i ^ bit) for i in range(size)])  19.1 us
    unnamed x52, local copies, waits for them, and re-layouts  11 us
    all_to_all x1, starting transfers between devices, update(): own_natural = lax.all_to_all(own_spread, RCV, 0, 0, tiled=True)  9.8 us
    all_to_all x1, waiting for transfers between devices, update(): own_here = lax.all_to_all(own_group, SHOT, 0, 0, tiled=True)  6.89 us
    all_to_all x1, starting transfers between devices, sent_to_all(): lax.all_to_all(jnp.broadcast_to(array[None], (size, *array.shape)), axis,...  6.18 us
    all_to_all x1, starting transfers between devices, update(): own_here = lax.all_to_all(own_group, SHOT, 0, 0, tiled=True)  5.76 us
    all_to_all x1, waiting for transfers between devices, sent_to_all(): lax.all_to_all(jnp.broadcast_to(array[None], (size, *array.shape)), axis,...  4.77 us
  transfers between devices with their start and end apart: 14, of which 9 were waited for; matrix products, arithmetic and copies ran while one was open for 1% of the time, Pallas kernels for 4%

profile of v1, /device:TPU:8, one launch (start us, length us, event | category | flops | bytes accessed | tf_op | source)
XLA Modules:
  0.0 102.2 jit_solution(8376334179335516138)
XLA Ops:
  0.7 2.2 %shard_map.95 = bf16[32,4,8,512]{3,2,1,0:T(8,128)(2,1)} custom-call(bf16[4,32,8,512]{3,2,1,0:T(8,128)(2,1)} %bitcast.6), custom_call_target="tpu_custom_call" | custom-call | bytes 1048576 | tf_op jit(solution)/shard_map/pallas_call | solution.py:187
  2.9 9.8 %all-to-all-start = ((bf16[32,4,8,512]{3,2,1,0:T(8,128)(2,1)}), bf16[32,4,8,512]{3,2,1,0:T(8,128)(2,1)S(1)}, u32[]{:S(2)}, u32[]{:S(2)}) async-start(bf16[32,4,8,512]{3,2,1,0:T(8,128)(2,1)} %shard_map.95), calls=%async_computation | async-start | bytes 2097152 | tf_op jit(solution)/shard_map/all_to_all | solution.py:196
  14.7 2.6 %collective-permute-start.1 = (bf16[2,64,512]{2,1,0:T(8,128)(2,1)S(1)}, bf16[2,64,512]{2,1,0:T(8,128)(2,1)S(1)}, u32[]{:S(2)}, u32[]{:S(2)}) collective-permute-start(bf16[2,64,512]{2,1,0:T(8,128)(2,1)S(1)} %get-tuple-element.14.refs_2_), channel_id=1, source_target_pairs={{0,64},{32,96},{64,0},{96,32},{128,192},{160,224},{192,128},{224,1... | collective-permute-start | bytes 393224 | tf_op jit(solution)/shard_map/ppermute | solution.py:167
  19.0 2.7 %collective-permute-start.3 = (bf16[2,64,512]{2,1,0:T(8,128)(2,1)S(1)}, bf16[2,64,512]{2,1,0:T(8,128)(2,1)S(1)}, u32[]{:S(2)}, u32[]{:S(2)}) collective-permute-start(bf16[2,64,512]{2,1,0:T(8,128)(2,1)S(1)} %get-tuple-element.16.refs_4_), channel_id=1, source_target_pairs={{0,128},{32,160},{64,192},{96,224},{128,0},{160,32},{192,64},{224,... | collective-permute-start | bytes 393224 | tf_op jit(solution)/shard_map/ppermute | solution.py:167
  22.4 1.9 %collective-permute-start.4 = (bf16[2,64,512]{2,1,0:T(8,128)(2,1)S(1)}, bf16[2,64,512]{2,1,0:T(8,128)(2,1)S(1)}, u32[]{:S(2)}, u32[]{:S(2)}) collective-permute-start(bf16[2,64,512]{2,1,0:T(8,128)(2,1)S(1)} %get-tuple-element.17.refs_5_), channel_id=1, source_target_pairs={{0,160},{32,128},{64,224},{96,192},{128,32},{160,0},{192,96},{224,... | collective-permute-start | bytes 393224 | tf_op jit(solution)/shard_map/ppermute | solution.py:167
  24.9 3.5 %collective-permute-start.5 = (bf16[2,64,512]{2,1,0:T(8,128)(2,1)S(1)}, bf16[2,64,512]{2,1,0:T(8,128)(2,1)S(1)}, u32[]{:S(2)}, u32[]{:S(2)}) collective-permute-start(bf16[2,64,512]{2,1,0:T(8,128)(2,1)S(1)} %get-tuple-element.18.refs_6_), channel_id=1, source_target_pairs={{0,192},{32,224},{64,128},{96,160},{128,64},{160,96},{192,0},{224,... | collective-permute-start | bytes 393224 | tf_op jit(solution)/shard_map/ppermute | solution.py:167
  29.1 1.0 %collective-permute-start.6 = (bf16[2,64,512]{2,1,0:T(8,128)(2,1)S(1)}, bf16[2,64,512]{2,1,0:T(8,128)(2,1)S(1)}, u32[]{:S(2)}, u32[]{:S(2)}) collective-permute-start(bf16[2,64,512]{2,1,0:T(8,128)(2,1)S(1)} %get-tuple-element.19.refs_7_), channel_id=1, source_target_pairs={{0,224},{32,192},{64,160},{96,128},{128,96},{160,64},{192,32},{224... | collective-permute-start | bytes 393224 | tf_op jit(solution)/shard_map/ppermute | solution.py:167
  30.8 1.2 %copy-done.5 = bf16[2,512,512]{2,1,0:T(8,128)(2,1)S(1)} copy-done((bf16[2,512,512]{2,1,0:T(8,128)(2,1)S(1)}, bf16[2,512,512]{2,1,0:T(8,128)(2,1)}, u32[]{:S(2)}) %copy-start.5) | copy-done | bytes 1048600
  32.2 2.8 %collective-permute-done.4.refs_5_ = bf16[2,64,512]{2,1,0:T(8,128)(2,1)S(1)} collective-permute-done((bf16[2,64,512]{2,1,0:T(8,128)(2,1)S(1)}, bf16[2,64,512]{2,1,0:T(8,128)(2,1)S(1)}, u32[]{:S(2)}, u32[]{:S(2)}) %collective-permute-start.4) | collective-permute-done | bytes 131104 | tf_op jit(solution)/shard_map/ppermute | solution.py:167
  35.0 6.1 %collective-permute-done.5.refs_6_ = bf16[2,64,512]{2,1,0:T(8,128)(2,1)S(1)} collective-permute-done((bf16[2,64,512]{2,1,0:T(8,128)(2,1)S(1)}, bf16[2,64,512]{2,1,0:T(8,128)(2,1)S(1)}, u32[]{:S(2)}, u32[]{:S(2)}) %collective-permute-start.5) | collective-permute-done | bytes 131104 | tf_op jit(solution)/shard_map/ppermute | solution.py:167
  41.1 2.0 %collective-permute-done.6.refs_7_ = bf16[2,64,512]{2,1,0:T(8,128)(2,1)S(1)} collective-permute-done((bf16[2,64,512]{2,1,0:T(8,128)(2,1)S(1)}, bf16[2,64,512]{2,1,0:T(8,128)(2,1)S(1)}, u32[]{:S(2)}, u32[]{:S(2)}) %collective-permute-start.6) | collective-permute-done | bytes 131104 | tf_op jit(solution)/shard_map/ppermute | solution.py:167
  43.0 1.2 %shard_map.101.wg_ref = f32[2,512,512]{2,1,0:T(8,128)S(1)} custom-call(bf16[2,64,512]{2,1,0:T(8,128)(2,1)S(1)} %get-tuple-element.12.refs_0_, bf16[2,64,512]{2,1,0:T(8,128)(2,1)S(1)} %collective-permute-done.refs_1_, bf16[2,64,512]{2,1,0:T(8,128)(2,1)S(1)} %collective-permute-done.1.refs_2_, bf16[2,64,512]{2,1,0:T(8,128)(2,1)S(1)} %collective-permute-done.2.refs_3_, ...), custom_call_target="tpu_custom_call" | custom-call | flops 1073741824 | bytes 1048576 | tf_op jit(solution)/shard_map/pallas_call | solution.py:209
  44.3 1.3 %copy-done.2 = f32[2,512,512]{2,1,0:T(8,128)} copy-done((f32[2,512,512]{2,1,0:T(8,128)}, f32[2,512,512]{2,1,0:T(8,128)S(1)}, u32[]{:S(2)}) %copy-start.2) | copy-done | bytes 2097176
  45.6 1.6 %copy-done.3 = f32[2,512,512]{2,1,0:T(8,128)S(1)} copy-done((f32[2,512,512]{2,1,0:T(8,128)S(1)}, f32[2,512,512]{2,1,0:T(8,128)}, u32[]{:S(2)}) %copy-start.3) | copy-done | bytes 2097176
  47.2 2.1 %shard_map.102 = f32[3,512]{1,0:T(4,128)S(1)} custom-call(s32[1]{0:T(128)} %bitcast.me_ref, s32[64]{0:T(128)S(1)} %copy-done.25, bf16[32,4,8,512]{3,2,1,0:T(8,128)(2,1)S(1)} %all-to-all-done.own_ref, bf16[2,1024,512]{2,1,0:T(8,128)(2,1)S(1)} %shard_map.98.b_ref.refs_8_, f32[2,512,512]{2,1,0:T(8,128)S(1)} %copy-done.3), custom_call_target="tpu_custom_call" | custom-call | flops 1073741824 | bytes 1048576 | tf_op jit(solution)/shard_map/pallas_call | solution.py:215
  50.0 1.4 %collective-permute-done.7 = f32[12,128]{1,0:T(8,128)S(1)} collective-permute-done((f32[12,128]{1,0:T(8,128)}, f32[12,128]{1,0:T(8,128)S(1)}, u32[]{:S(2)}, u32[]{:S(2)}) %collective-permute-start.7) | collective-permute-done | bytes 6176 | tf_op jit(solution)/shard_map/ppermute | solution.py:167
  52.0 1.4 %collective-permute-start.8 = (f32[12,128]{1,0:T(8,128)S(1)}, f32[12,128]{1,0:T(8,128)S(1)}, u32[]{:S(2)}, u32[]{:S(2)}) collective-permute-start(f32[12,128]{1,0:T(8,128)S(1)} %add.16), channel_id=1, source_target_pairs={{0,2},{2,0},{4,6},{6,4},{8,10},{10,8},{12,14},{14,12},{1,3},{3,1},... | collective-permute-start | bytes 18440 | tf_op jit(solution)/shard_map/ppermute | solution.py:167
  53.4 2.3 %collective-permute-done.8 = f32[12,128]{1,0:T(8,128)S(1)} collective-permute-done((f32[12,128]{1,0:T(8,128)S(1)}, f32[12,128]{1,0:T(8,128)S(1)}, u32[]{:S(2)}, u32[]{:S(2)}) %collective-permute-start.8) | collective-permute-done | bytes 6176 | tf_op jit(solution)/shard_map/ppermute | solution.py:167
  55.7 2.6 %collective-permute-start.9 = (f32[12,128]{1,0:T(8,128)S(1)}, f32[12,128]{1,0:T(8,128)S(1)}, u32[]{:S(2)}, u32[]{:S(2)}) collective-permute-start(f32[12,128]{1,0:T(8,128)S(1)} %add.17), channel_id=1, source_target_pairs={{0,4},{2,6},{4,0},{6,2},{8,12},{10,14},{12,8},{14,10},{1,5},{3,7},... | collective-permute-start | bytes 18440 | tf_op jit(solution)/shard_map/ppermute | solution.py:167
  58.3 2.0 %collective-permute-done.9 = f32[12,128]{1,0:T(8,128)S(1)} collective-permute-done((f32[12,128]{1,0:T(8,128)S(1)}, f32[12,128]{1,0:T(8,128)S(1)}, u32[]{:S(2)}, u32[]{:S(2)}) %collective-permute-start.9) | collective-permute-done | bytes 6176 | tf_op jit(solution)/shard_map/ppermute | solution.py:167
  60.2 4.9 %collective-permute-start.10 = (f32[12,128]{1,0:T(8,128)S(1)}, f32[12,128]{1,0:T(8,128)S(1)}, u32[]{:S(2)}, u32[]{:S(2)}) collective-permute-start(f32[12,128]{1,0:T(8,128)S(1)} %add.18), channel_id=1, source_target_pairs={{0,8},{2,10},{4,12},{6,14},{8,0},{10,2},{12,4},{14,6},{1,9},{3,11}... | collective-permute-start | bytes 18440 | tf_op jit(solution)/shard_map/ppermute | solution.py:167
  65.1 2.7 %collective-permute-done.10 = f32[12,128]{1,0:T(8,128)S(1)} collective-permute-done((f32[12,128]{1,0:T(8,128)S(1)}, f32[12,128]{1,0:T(8,128)S(1)}, u32[]{:S(2)}, u32[]{:S(2)}) %collective-permute-start.10) | collective-permute-done | bytes 6176 | tf_op jit(solution)/shard_map/ppermute | solution.py:167
  68.5 6.2 %all-to-all-start.2 = ((f32[16,1,1536]{2,1,0:T(1,128)}), f32[16,1,1536]{2,1,0:T(1,128)}, u32[]{:S(2)}, u32[]{:S(2)}) async-start(f32[16,1,1536]{2,1,0:T(1,128)} %broadcast_in_dim.8), calls=%async_computation.2 | async-start | bytes 196608 | tf_op jit(solution)/shard_map/all_to_all | solution.py:172
  75.4 1.0 copy-done.4
  76.4 4.8 %all-to-all-done.2 = f32[16,1,1536]{2,1,0:T(1,128)} async-done(((f32[16,1,1536]{2,1,0:T(1,128)}), f32[16,1,1536]{2,1,0:T(1,128)}, u32[]{:S(2)}, u32[]{:S(2)}) %all-to-all-start.2) | async-done | bytes 98336 | tf_op jit(solution)/shard_map/all_to_all | solution.py:172
  81.1 5.8 %all-to-all-start.1 = ((bf16[8,2,64,512]{3,2,1,0:T(8,128)(2,1)}), bf16[8,2,64,512]{3,2,1,0:T(8,128)(2,1)}, u32[]{:S(2)}, u32[]{:S(2)}) async-start(bf16[8,2,64,512]{3,2,1,0:T(8,128)(2,1)} %copy-done.4), calls=%async_computation.1 | async-start | bytes 2097152 | tf_op jit(solution)/shard_map/all_to_all | solution.py:214
  87.0 1.2 %shard_map.100.wg_ref = f32[2,512,512]{2,1,0:T(8,128)S(1)} custom-call(bf16[2,64,512]{2,1,0:T(8,128)(2,1)S(1)} %get-tuple-element.12.refs_0_, bf16[2,64,512]{2,1,0:T(8,128)(2,1)S(1)} %copy-done.8, bf16[2,64,512]{2,1,0:T(8,128)(2,1)S(1)} %copy-done.10, bf16[2,64,512]{2,1,0:T(8,128)(2,1)S(1)} %copy-done.12, bf16[2,64,512]{2,1,0:T(8,128)(2,1)S(1)} %copy-done.14, ...), custom_call_target="tpu_custom_call" | custom-call | flops 1073741824 | bytes 1048576 | tf_op jit(solution)/shard_map/pallas_call | solution.py:208
  88.2 1.3 %copy-done = f32[2,512,512]{2,1,0:T(8,128)} copy-done((f32[2,512,512]{2,1,0:T(8,128)}, f32[2,512,512]{2,1,0:T(8,128)S(1)}, u32[]{:S(2)}) %copy-start) | copy-done | bytes 2097176
  89.6 1.1 %reduce = f32[16,1536]{1,0:T(8,128)S(1)} reduce(f32[16,1,1536]{2,1,0:T(1,128)} %all-to-all-done.2, f32[]{:T(128)} %constant.17), dimensions={1}, to_apply=%all_to_all.11.reduce_sub_computation | reduce | bytes 196612 | tf_op jit(solution)/shard_map/all_to_all | solution.py:172
  90.8 6.9 %all-to-all-done.1.own_ref = bf16[8,2,64,512]{3,2,1,0:T(8,128)(2,1)} async-done(((bf16[8,2,64,512]{3,2,1,0:T(8,128)(2,1)}), bf16[8,2,64,512]{3,2,1,0:T(8,128)(2,1)}, u32[]{:S(2)}, u32[]{:S(2)}) %all-to-all-start.1) | async-done | bytes 1048608 | tf_op jit(solution)/shard_map/all_to_all | solution.py:214
  97.7 2.6 %shard_map.99.wd_ref = f32[2,512,512]{2,1,0:T(8,128)S(1)} custom-call(s32[1]{0:T(128)} %bitcast.me_ref, bf16[8,2,64,512]{3,2,1,0:T(8,128)(2,1)} %all-to-all-done.1.own_ref, f32[8,64,128]{2,1,0:T(8,128)S(1)} %get-tuple-element.11.live_ref, bf16[2,1024,512]{2,1,0:T(8,128)(2,1)S(1)} %shard_map.98.b_ref.refs_8_), custom_call_target="tpu_custom_call" | custom-call | flops 1073741824 | bytes 1048576 | tf_op jit(solution)/shard_map/pallas_call | solution.py:223
  100.3 1.9 %shard_map.103 = (f32[2,512]{1,0:T(2,128)}, bf16[2,8,8,8,512]{4,3,2,1,0:T(8,128)(2,1)}) custom-call(s32[1]{0:T(128)} %bitcast.me_ref, s32[8]{0:T(128)S(1)} %copy-done.24, f32[2,512,512]{2,1,0:T(8,128)S(1)} %shard_map.99.wd_ref, f32[2,512,512]{2,1,0:T(8,128)S(1)} %copy-done.1, f32[16,3,512]{2,1,0:T(4,128)S(1)} %reshape.25.sums_ref, f32[2,512]{1,0:T(2,128)S(1)} %copy-done.22, ...), custom_call_target="tpu_custom_call" | custom-call | bytes 1048576 | tf_op jit(solution)/shard_map/pallas_call | solution.py:228
  (65 shorter events, 9.3 us)
Async XLA Ops:
  0.6 12.0 %copy-start.6 = (bf16[2,8,8,8,512]{4,3,2,1,0:T(8,128)(2,1)S(1)}, bf16[2,8,8,8,512]{4,3,2,1,0:T(8,128)(2,1)}, u32[]{:S(2)}) copy-start(bf16[2,8,8,8,512]{4,3,2,1,0:T(8,128)(2,1)} %mod_ref.1) | copy-start | bytes 3145732
  0.6 12.0 %copy-start.21 = (s32[8,8,8]{2,1,0:T(8,128)S(1)}, s32[8,8,8]{2,1,0:T(8,128)}, u32[]{:S(2)}) copy-start(s32[8,8,8]{2,1,0:T(8,128)} %mask_ref.1) | copy-start | bytes 6148
  0.7 12.0 %copy-start.24 = (s32[8]{0:T(128)S(1)}, s32[8]{0:T(128)}, u32[]{:S(2)}) copy-start(s32[8]{0:T(128)} %slot_ref.3) | copy-start | bytes 100
  2.9 42.8 %all-to-all-start = ((bf16[32,4,8,512]{3,2,1,0:T(8,128)(2,1)}), bf16[32,4,8,512]{3,2,1,0:T(8,128)(2,1)S(1)}, u32[]{:S(2)}, u32[]{:S(2)}) async-start(bf16[32,4,8,512]{3,2,1,0:T(8,128)(2,1)} %shard_map.95), calls=%async_computation | async-start | bytes 2097152 | tf_op jit(solution)/shard_map/all_to_all | solution.py:196
  13.5 11.4 %collective-permute-start = (bf16[2,64,512]{2,1,0:T(8,128)(2,1)S(1)}, bf16[2,64,512]{2,1,0:T(8,128)(2,1)S(1)}, u32[]{:S(2)}, u32[]{:S(2)}) collective-permute-start(bf16[2,64,512]{2,1,0:T(8,128)(2,1)S(1)} %get-tuple-element.13.refs_1_), channel_id=1, source_target_pairs={{0,32},{32,0},{64,96},{96,64},{128,160},{160,128},{192,224},{224,1... | collective-permute-start | bytes 393224 | tf_op jit(solution)/shard_map/ppermute | solution.py:167
  14.7 14.4 %collective-permute-start.1 = (bf16[2,64,512]{2,1,0:T(8,128)(2,1)S(1)}, bf16[2,64,512]{2,1,0:T(8,128)(2,1)S(1)}, u32[]{:S(2)}, u32[]{:S(2)}) collective-permute-start(bf16[2,64,512]{2,1,0:T(8,128)(2,1)S(1)} %get-tuple-element.14.refs_2_), channel_id=1, source_target_pairs={{0,64},{32,96},{64,0},{96,32},{128,192},{160,224},{192,128},{224,1... | collective-permute-start | bytes 393224 | tf_op jit(solution)/shard_map/ppermute | solution.py:167
  17.9 14.3 %collective-permute-start.2 = (bf16[2,64,512]{2,1,0:T(8,128)(2,1)S(1)}, bf16[2,64,512]{2,1,0:T(8,128)(2,1)S(1)}, u32[]{:S(2)}, u32[]{:S(2)}) collective-permute-start(bf16[2,64,512]{2,1,0:T(8,128)(2,1)S(1)} %get-tuple-element.15.refs_3_), channel_id=1, source_target_pairs={{0,96},{32,64},{64,32},{96,0},{128,224},{160,192},{192,160},{224,1... | collective-permute-start | bytes 393224 | tf_op jit(solution)/shard_map/ppermute | solution.py:167
  19.0 13.2 %collective-permute-start.3 = (bf16[2,64,512]{2,1,0:T(8,128)(2,1)S(1)}, bf16[2,64,512]{2,1,0:T(8,128)(2,1)S(1)}, u32[]{:S(2)}, u32[]{:S(2)}) collective-permute-start(bf16[2,64,512]{2,1,0:T(8,128)(2,1)S(1)} %get-tuple-element.16.refs_4_), channel_id=1, source_target_pairs={{0,128},{32,160},{64,192},{96,224},{128,0},{160,32},{192,64},{224,... | collective-permute-start | bytes 393224 | tf_op jit(solution)/shard_map/ppermute | solution.py:167
  22.4 12.6 %collective-permute-start.4 = (bf16[2,64,512]{2,1,0:T(8,128)(2,1)S(1)}, bf16[2,64,512]{2,1,0:T(8,128)(2,1)S(1)}, u32[]{:S(2)}, u32[]{:S(2)}) collective-permute-start(bf16[2,64,512]{2,1,0:T(8,128)(2,1)S(1)} %get-tuple-element.17.refs_5_), channel_id=1, source_target_pairs={{0,160},{32,128},{64,224},{96,192},{128,32},{160,0},{192,96},{224,... | collective-permute-start | bytes 393224 | tf_op jit(solution)/shard_map/ppermute | solution.py:167
  24.9 16.1 %collective-permute-start.5 = (bf16[2,64,512]{2,1,0:T(8,128)(2,1)S(1)}, bf16[2,64,512]{2,1,0:T(8,128)(2,1)S(1)}, u32[]{:S(2)}, u32[]{:S(2)}) collective-permute-start(bf16[2,64,512]{2,1,0:T(8,128)(2,1)S(1)} %get-tuple-element.18.refs_6_), channel_id=1, source_target_pairs={{0,192},{32,224},{64,128},{96,160},{128,64},{160,96},{192,0},{224,... | collective-permute-start | bytes 393224 | tf_op jit(solution)/shard_map/ppermute | solution.py:167
  29.1 13.9 %collective-permute-start.6 = (bf16[2,64,512]{2,1,0:T(8,128)(2,1)S(1)}, bf16[2,64,512]{2,1,0:T(8,128)(2,1)S(1)}, u32[]{:S(2)}, u32[]{:S(2)}) collective-permute-start(bf16[2,64,512]{2,1,0:T(8,128)(2,1)S(1)} %get-tuple-element.19.refs_7_), channel_id=1, source_target_pairs={{0,224},{32,192},{64,160},{96,128},{128,96},{160,64},{192,32},{224... | collective-permute-start | bytes 393224 | tf_op jit(solution)/shard_map/ppermute | solution.py:167
  30.8 1.2 %copy-start.5 = (bf16[2,512,512]{2,1,0:T(8,128)(2,1)S(1)}, bf16[2,512,512]{2,1,0:T(8,128)(2,1)}, u32[]{:S(2)}) copy-start(bf16[2,512,512]{2,1,0:T(8,128)(2,1)} %c_ref.1) | copy-start | bytes 3145732
  43.0 2.6 %copy-start.25 = (s32[64]{0:T(128)S(1)}, s32[64]{0:T(128)}, u32[]{:S(2)}) copy-start(s32[64]{0:T(128)} %order_ref.3) | copy-start | bytes 772
  44.3 1.4 %copy-start.2 = (f32[2,512,512]{2,1,0:T(8,128)}, f32[2,512,512]{2,1,0:T(8,128)S(1)}, u32[]{:S(2)}) copy-start(f32[2,512,512]{2,1,0:T(8,128)S(1)} %shard_map.101.wg_ref) | copy-start | bytes 6291460
  45.6 1.6 %copy-start.3 = (f32[2,512,512]{2,1,0:T(8,128)S(1)}, f32[2,512,512]{2,1,0:T(8,128)}, u32[]{:S(2)}) copy-start(f32[2,512,512]{2,1,0:T(8,128)} %copy-done.2) | copy-start | bytes 6291460
  50.0 1.4 %collective-permute-start.7 = (f32[12,128]{1,0:T(8,128)}, f32[12,128]{1,0:T(8,128)S(1)}, u32[]{:S(2)}, u32[]{:S(2)}) collective-permute-start(f32[12,128]{1,0:T(8,128)} %reshape.24), channel_id=1, source_target_pairs={{0,1},{1,0},{2,3},{3,2},{4,5},{5,4},{6,7},{7,6},{8,9},{9,8},{10,11... | collective-permute-start | bytes 18440 | tf_op jit(solution)/shard_map/ppermute | solution.py:167
  52.0 3.7 %collective-permute-start.8 = (f32[12,128]{1,0:T(8,128)S(1)}, f32[12,128]{1,0:T(8,128)S(1)}, u32[]{:S(2)}, u32[]{:S(2)}) collective-permute-start(f32[12,128]{1,0:T(8,128)S(1)} %add.16), channel_id=1, source_target_pairs={{0,2},{2,0},{4,6},{6,4},{8,10},{10,8},{12,14},{14,12},{1,3},{3,1},... | collective-permute-start | bytes 18440 | tf_op jit(solution)/shard_map/ppermute | solution.py:167
  55.7 4.5 %collective-permute-start.9 = (f32[12,128]{1,0:T(8,128)S(1)}, f32[12,128]{1,0:T(8,128)S(1)}, u32[]{:S(2)}, u32[]{:S(2)}) collective-permute-start(f32[12,128]{1,0:T(8,128)S(1)} %add.17), channel_id=1, source_target_pairs={{0,4},{2,6},{4,0},{6,2},{8,12},{10,14},{12,8},{14,10},{1,5},{3,7},... | collective-permute-start | bytes 18440 | tf_op jit(solution)/shard_map/ppermute | solution.py:167
  60.2 7.6 %collective-permute-start.10 = (f32[12,128]{1,0:T(8,128)S(1)}, f32[12,128]{1,0:T(8,128)S(1)}, u32[]{:S(2)}, u32[]{:S(2)}) collective-permute-start(f32[12,128]{1,0:T(8,128)S(1)} %add.18), channel_id=1, source_target_pairs={{0,8},{2,10},{4,12},{6,14},{8,0},{10,2},{12,4},{14,6},{1,9},{3,11}... | collective-permute-start | bytes 18440 | tf_op jit(solution)/shard_map/ppermute | solution.py:167
  68.5 12.6 %all-to-all-start.2 = ((f32[16,1,1536]{2,1,0:T(1,128)}), f32[16,1,1536]{2,1,0:T(1,128)}, u32[]{:S(2)}, u32[]{:S(2)}) async-start(f32[16,1,1536]{2,1,0:T(1,128)} %broadcast_in_dim.8), calls=%async_computation.2 | async-start | bytes 196608 | tf_op jit(solution)/shard_map/all_to_all | solution.py:172
  76.3 10.6 %copy-start.8 = (bf16[2,64,512]{2,1,0:T(8,128)(2,1)S(1)}, bf16[2,64,512]{2,1,0:T(8,128)(2,1)}, u32[]{:S(2)}) copy-start(bf16[2,64,512]{2,1,0:T(8,128)(2,1)} %copy-done.7) | copy-start | bytes 393220
  76.3 10.6 %copy-start.10 = (bf16[2,64,512]{2,1,0:T(8,128)(2,1)S(1)}, bf16[2,64,512]{2,1,0:T(8,128)(2,1)}, u32[]{:S(2)}) copy-start(bf16[2,64,512]{2,1,0:T(8,128)(2,1)} %copy-done.9) | copy-start | bytes 393220
  76.3 10.6 %copy-start.12 = (bf16[2,64,512]{2,1,0:T(8,128)(2,1)S(1)}, bf16[2,64,512]{2,1,0:T(8,128)(2,1)}, u32[]{:S(2)}) copy-start(bf16[2,64,512]{2,1,0:T(8,128)(2,1)} %copy-done.11) | copy-start | bytes 393220
  76.3 10.6 %copy-start.14 = (bf16[2,64,512]{2,1,0:T(8,128)(2,1)S(1)}, bf16[2,64,512]{2,1,0:T(8,128)(2,1)}, u32[]{:S(2)}) copy-start(bf16[2,64,512]{2,1,0:T(8,128)(2,1)} %copy-done.13) | copy-start | bytes 393220
  76.3 10.6 %copy-start.16 = (bf16[2,64,512]{2,1,0:T(8,128)(2,1)S(1)}, bf16[2,64,512]{2,1,0:T(8,128)(2,1)}, u32[]{:S(2)}) copy-start(bf16[2,64,512]{2,1,0:T(8,128)(2,1)} %copy-done.15) | copy-start | bytes 393220
  76.3 10.6 %copy-start.18 = (bf16[2,64,512]{2,1,0:T(8,128)(2,1)S(1)}, bf16[2,64,512]{2,1,0:T(8,128)(2,1)}, u32[]{:S(2)}) copy-start(bf16[2,64,512]{2,1,0:T(8,128)(2,1)} %copy-done.17) | copy-start | bytes 393220
  76.4 10.6 %copy-start.20 = (bf16[2,64,512]{2,1,0:T(8,128)(2,1)S(1)}, bf16[2,64,512]{2,1,0:T(8,128)(2,1)}, u32[]{:S(2)}) copy-start(bf16[2,64,512]{2,1,0:T(8,128)(2,1)} %copy-done.19) | copy-start | bytes 393220
  81.1 16.5 %all-to-all-start.1 = ((bf16[8,2,64,512]{3,2,1,0:T(8,128)(2,1)}), bf16[8,2,64,512]{3,2,1,0:T(8,128)(2,1)}, u32[]{:S(2)}, u32[]{:S(2)}) async-start(bf16[8,2,64,512]{3,2,1,0:T(8,128)(2,1)} %copy-done.4), calls=%async_computation.1 | async-start | bytes 2097152 | tf_op jit(solution)/shard_map/all_to_all | solution.py:214
  88.2 1.4 %copy-start = (f32[2,512,512]{2,1,0:T(8,128)}, f32[2,512,512]{2,1,0:T(8,128)S(1)}, u32[]{:S(2)}) copy-start(f32[2,512,512]{2,1,0:T(8,128)S(1)} %shard_map.100.wg_ref) | copy-start | bytes 6291460
  97.7 2.6 %copy-start.1 = (f32[2,512,512]{2,1,0:T(8,128)S(1)}, f32[2,512,512]{2,1,0:T(8,128)}, u32[]{:S(2)}) copy-start(f32[2,512,512]{2,1,0:T(8,128)} %copy-done) | copy-start | bytes 6291460
  97.7 2.6 %copy-start.22 = (f32[2,512]{1,0:T(2,128)S(1)}, f32[2,512]{1,0:T(2,128)}, u32[]{:S(2)}) copy-start(f32[2,512]{1,0:T(2,128)} %wav_ref.1) | copy-start | bytes 12292
  97.7 2.6 %copy-start.23 = (f32[512]{0:T(512)S(1)}, f32[512]{0:T(512)}, u32[]{:S(2)}) copy-start(f32[512]{0:T(512)} %param.15) | copy-start | bytes 6148
  (8 other events, 5.5 us)

commit v2 on v1

v2 whole, which is shorter than its diff:
```python
import jax
import jax.numpy as jnp
from jax import lax
from jax.experimental import pallas as pl
from jax.experimental.pallas import tpu as pltpu
from jax.sharding import Mesh, PartitionSpec as P

F32 = jnp.float32
BF16 = jnp.bfloat16
SHOT = ("xh", "yh", "yl")
RCV = ("xl", "zh", "zm", "zl", "c")
REST = ("xh", "yh", "xl", "zh")
SWAPS = (4, 5, 6, 7, 1, 2, 3)

VM = pl.BlockSpec(memory_space=pltpu.VMEM)
SM = pl.BlockSpec(memory_space=pltpu.SMEM)
ANY = pl.BlockSpec(memory_space=pl.ANY)
HBM = pl.BlockSpec(memory_space=pltpu.HBM)


def call(body, outs, in_specs, out_specs=None, scratch=(), limit=12 << 20, flops=0, nbytes=1 << 20):
    many = isinstance(outs, (tuple, list))
    return pl.pallas_call(
        body,
        out_shape=outs,
        in_specs=in_specs,
        out_specs=out_specs if out_specs is not None else ([VM] * len(outs) if many else VM),
        scratch_shapes=list(scratch),
        compiler_params=pltpu.CompilerParams(vmem_limit_bytes=limit),
        cost_estimate=pl.CostEstimate(flops=flops, bytes_accessed=nbytes, transcendentals=0),
    )


CHUNKS = 4
BIG = 62 << 20
MID = 40 << 20


def k_spread(obs_ref, out_ref, buf, sem_in, sem_out):
    parts, pieces = obs_ref.shape[:2]
    step = pieces // CHUNKS
    ins, outs = [], []
    for q in range(CHUNKS):
        rows = pl.ds(q * step, step)
        for i in range(parts):
            ins.append(pltpu.make_async_copy(obs_ref.at[i, rows], buf.at[rows, i], sem_in.at[q, i]))
        outs.append(pltpu.make_async_copy(buf.at[rows], out_ref.at[rows], sem_out.at[q]))
    for c in ins:
        c.start()
    for q in range(CHUNKS):
        for i in range(parts):
            ins[q * parts + i].wait()
        outs[q].start()
    for c in outs:
        c.wait()


def couple(c_ref, b_ref):
    f = c_ref.shape[1]
    re, im = c_ref[0], c_ref[1]
    b_ref[0, :f] = re
    b_ref[0, f:] = -im
    b_ref[1, :f] = im
    b_ref[1, f:] = re


def k_mask(me_ref, slot_ref, mod_ref, mask_ref, live_ref, *out_refs):
    me = me_ref[0]
    shots, rb = mod_ref.shape[1], mod_ref.shape[3]
    f = mod_ref.shape[4]
    eye = lax.broadcasted_iota(jnp.int32, (rb, rb), 0) == lax.broadcasted_iota(jnp.int32, (rb, rb), 1)
    for b, out_ref in enumerate(out_refs):
        line = slot_ref[lax.bitwise_xor(me, b)]
        for s in range(shots):
            row = mask_ref[s, pl.ds(line, 1)].astype(F32)
            column = jnp.where(eye, row, 0.0).sum(axis=1, keepdims=True)
            rows = pl.ds(s * rb, rb)
            live_ref[b, rows] = jnp.broadcast_to(column, (rb, 128))
            live = jnp.broadcast_to(column, (rb, f)) > 0.5
            for c in range(2):
                x = mod_ref[c, s, line].astype(F32)
                out_ref[c, rows] = jnp.where(live, x, 0.0).astype(BF16)


def window_out(x_ref, b_ref, out_ref, buf, sem):
    copies = []
    for d in range(2):
        w = jnp.dot(x_ref[...], b_ref[d], preferred_element_type=F32)
        buf[d] = w.reshape(buf.shape[1:])
        copies.append(pltpu.make_async_copy(buf.at[d], out_ref.at[d], sem.at[d]))
        if d:
            copies[d - 1].start()
    copies[-1].start()
    for c in copies:
        c.wait()


def k_window_here(*refs):
    xs, c_ref, out_ref, x_ref, b_ref, buf, sem = refs[:-6], *refs[-6:]
    couple(c_ref, b_ref)
    rows, f = xs[0].shape[1:]
    for b, x in enumerate(xs):
        for c in range(2):
            x_ref[b * rows : (b + 1) * rows, c * f : (c + 1) * f] = x[c]
    window_out(x_ref, b_ref, out_ref, buf, sem)


def k_window_own(me_ref, own_ref, live_ref, c_ref, out_ref, own, live, coup, x_ref, b_ref, buf, isem, sem):
    me = me_ref[0]
    ins = [
        pltpu.make_async_copy(src, dst, isem.at[i])
        for i, (src, dst) in enumerate(((c_ref, coup), (live_ref, live), (own_ref, own)))
    ]
    for c in ins:
        c.start()
    slots, _, rows, f = own_ref.shape
    ins[0].wait()
    couple(coup, b_ref)
    ins[1].wait()
    ins[2].wait()
    for b in range(slots):
        k = lax.bitwise_xor(me, b)
        alive = jnp.concatenate([live[b]] * (f // live.shape[2]), axis=1) > 0.5
        for c in range(2):
            x = own[k, c].astype(F32)
            x_ref[b * rows : (b + 1) * rows, c * f : (c + 1) * f] = jnp.where(alive, x, 0.0).astype(BF16)
    window_out(x_ref, b_ref, out_ref, buf, sem)


def k_group(order_ref, own_ref, out_ref, buf, isem, sem):
    groups, _, size = out_ref.shape[:3]
    for g in range(groups):
        for s in range(size):
            n = order_ref[g * size + s]
            j = lax.shift_right_logical(n, 1)
            h = lax.bitwise_and(n, 1)
            for c in range(2):
                pltpu.make_async_copy(own_ref.at[j, 2 * c + h], buf.at[g, c, s], isem.at[g]).start()
    copies = [pltpu.make_async_copy(buf.at[g], out_ref.at[g], sem.at[g]) for g in range(groups)]
    for g in range(groups):
        pltpu.make_async_copy(out_ref.at[g], buf.at[g], isem.at[g]).wait()
        copies[g].start()
    for c in copies:
        c.wait()


def fold(x):
    return x.reshape(x.shape[0] // 8, 8, x.shape[1]).sum(axis=0).sum(axis=0, keepdims=True)


def k_cross(me_ref, own_ref, c_ref, *refs):
    mods, (out_ref, x_ref, m_ref, coup, b_ref, csem, osem, msem) = refs[:-8], refs[-8:]
    me = me_ref[0]
    groups = len(mods)
    rows, f = mods[0].shape[1:]

    def rows_of(dst, b, c):
        return dst.at[pl.ds(b * rows, rows), pl.ds(c * f, f)]

    first = pltpu.make_async_copy(c_ref, coup, csem)
    first.start()
    pairs = [(b, c) for b in range(groups) for c in range(2)]
    owns = [
        pltpu.make_async_copy(own_ref.at[lax.bitwise_xor(me, b), c], rows_of(x_ref, b, c), osem.at[b, c])
        for b, c in pairs
    ]
    for c in owns:
        c.start()
    copies = [pltpu.make_async_copy(mods[b].at[c], rows_of(m_ref, b, c), msem.at[b, c]) for b, c in pairs]
    for c in copies:
        c.start()
    first.wait()
    couple(coup, b_ref)
    for c in owns:
        c.wait()
    wd_re = jnp.dot(x_ref[...], b_ref[0], preferred_element_type=F32)
    wd_im = jnp.dot(x_ref[...], b_ref[1], preferred_element_type=F32)
    for c in copies:
        c.wait()
    wg_re = jnp.dot(m_ref[...], b_ref[0], preferred_element_type=F32)
    wg_im = jnp.dot(m_ref[...], b_ref[1], preferred_element_type=F32)
    out_ref[0:1] = fold(wg_re * wd_re + wg_im * wd_im)
    out_ref[1:2] = fold(wg_re * wd_im - wg_im * wd_re)
    out_ref[2:3] = fold(wg_re * wg_re + wg_im * wg_im)


def k_final(me_ref, slot_ref, wd_ref, wg_ref, sums_ref, wav_ref, damp_ref, nw_ref, out_ref, wd, wg, buf, sem, osem):
    me = me_ref[0]
    _, lines, _, f = wd_ref.shape
    shots, rb = out_ref.shape[1], out_ref.shape[3]
    ins = [
        [
            pltpu.make_async_copy(src.at[:, b], dst.at[:, b], sem.at[i, b])
            for i, (src, dst) in enumerate(((wd_ref, wd), (wg_ref, wg)))
        ]
        for b in range(lines)
    ]
    for pair in ins:
        for c in pair:
            c.start()
    outs = [
        pltpu.make_async_copy(
            buf.at[b], out_ref.at[:, :, slot_ref[lax.bitwise_xor(me, b)]], osem.at[b]
        )
        for b in range(lines)
    ]
    total = sums_ref[...].sum(axis=0)
    cross_re, cross_im, den = total[:, :f], total[:, f : 2 * f], total[:, 2 * f :]
    wav_re, wav_im = wav_ref[0:1], wav_ref[1:2]
    scale = den + damp_ref[...]
    nw_re = wav_re + (cross_re - wav_re * den) / scale
    nw_im = wav_im + (cross_im - wav_im * den) / scale
    nw_ref[0:1] = nw_re
    nw_ref[1:2] = nw_im
    for b in range(lines):
        for c in ins[b]:
            c.wait()
        wg_re, wg_im = wg[0, b], wg[1, b]
        out_re = wd[0, b] - (nw_re * wg_re - nw_im * wg_im)
        out_im = wd[1, b] - (nw_re * wg_im + nw_im * wg_re)
        buf[b, 0] = out_re.reshape(shots, rb, f).astype(BF16)
        buf[b, 1] = out_im.reshape(shots, rb, f).astype(BF16)
        if b:
            outs[b - 1].start()
    outs[-1].start()
    for c in outs:
        c.wait()


def swapped(x, axis, bit):
    size = lax.axis_size(axis)
    return lax.ppermute(x, axis, [(i, i ^ bit) for i in range(size)])


def sent_to_all(array, axis):
    size = lax.axis_size(axis)
    return lax.all_to_all(
        jnp.broadcast_to(array[None], (size, *array.shape)), axis, 0, 0, tiled=True
    )


def update(modeled, observed, mask, shot_order, line_of_slot, coupling, wavelet, damping):
    _, shots, lines, rb, f = modeled.shape
    slots = lax.axis_size(SHOT)
    held = observed.shape[2]
    pieces = lax.axis_size(RCV)
    rows = shots * rb
    traces = lines * rows
    flops = 8 * traces * f * f
    me = lax.axis_index(SHOT).astype(jnp.int32).reshape(1)

    own_spread = call(
        k_spread, jax.ShapeDtypeStruct((pieces, 2 * held, rb, f), BF16), [ANY], HBM,
        limit=BIG,
        scratch=[
            pltpu.VMEM((pieces, 2 * held, rb, f), BF16),
            pltpu.SemaphoreType.DMA((CHUNKS, 2 * held)),
            pltpu.SemaphoreType.DMA((CHUNKS,)),
        ],
    )(observed.reshape(2 * held, pieces, rb, f))
    own_natural = lax.all_to_all(own_spread, RCV, 0, 0, tiled=True)

    piece = jax.ShapeDtypeStruct((2, rows, f), BF16)
    live, *masked = call(
        k_mask, (jax.ShapeDtypeStruct((slots, rows, 128), F32), *[piece] * slots),
        [SM, SM, VM, VM],
    )(me, line_of_slot, modeled, mask)
    wide = jax.ShapeDtypeStruct((2, slots, rows, f), F32)
    x_block = pltpu.VMEM((traces, 2 * f), BF16)
    b_block = pltpu.VMEM((2, 2 * f, f), BF16)
    window_scratch = [x_block, b_block, pltpu.VMEM((2, slots, rows, f), F32), pltpu.SemaphoreType.DMA((2,))]
    arrived = {0: masked[0]}
    for b in SWAPS:
        arrived[b] = swapped(masked[b], SHOT, b)
    wg_here = call(
        k_window_here, wide, [VM] * (slots + 1), HBM, flops=flops,
        scratch=window_scratch,
    )(*masked, coupling)

    own_group = call(
        k_group, jax.ShapeDtypeStruct((slots, 2, shots, rb, f), BF16), [SM, ANY], HBM,
        scratch=[
            pltpu.VMEM((slots, 2, shots, rb, f), BF16),
            pltpu.SemaphoreType.DMA((slots,)),
            pltpu.SemaphoreType.DMA((slots,)),
        ],
        limit=BIG,
    )(shot_order, own_natural).reshape(slots, 2, rows, f)
    own_here = lax.all_to_all(own_group, SHOT, 0, 0, tiled=True)
    coup = pltpu.VMEM(coupling.shape, BF16)
    sums = call(
        k_cross, jax.ShapeDtypeStruct((3, f), F32), [SM, ANY, ANY] + [ANY] * slots,
        scratch=[
            x_block, x_block, coup, b_block, pltpu.SemaphoreType.DMA,
            pltpu.SemaphoreType.DMA((slots, 2)), pltpu.SemaphoreType.DMA((slots, 2)),
        ],
        limit=MID, flops=2 * flops,
    )(me, own_group, coupling, *[arrived[b] for b in range(slots)])
    sums = sums.reshape(3 * f // 128, 128)
    for axis in ("c", "zl", "zm", "yl"):
        sums = sums + swapped(sums, axis, 1)
    parts = sent_to_all(sums.reshape(1, 3 * f), REST)
    wd_here = call(
        k_window_own, wide, [SM, ANY, ANY, ANY], HBM, flops=flops, limit=MID,
        scratch=[
            pltpu.VMEM(own_here.shape, BF16), pltpu.VMEM(live.shape, F32), coup, x_block, b_block,
            window_scratch[2], pltpu.SemaphoreType.DMA((3,)), pltpu.SemaphoreType.DMA((2,)),
        ],
    )(me, own_here, live, coupling)

    new_wavelet, residual = call(
        k_final,
        (jax.ShapeDtypeStruct((2, f), F32), jax.ShapeDtypeStruct(modeled.shape, BF16)),
        [SM, SM, ANY, ANY, VM, VM, VM], [VM, HBM],
        scratch=[
            pltpu.VMEM((2, slots, rows, f), F32),
            pltpu.VMEM((2, slots, rows, f), F32),
            pltpu.VMEM((slots, 2, shots, rb, f), BF16),
            pltpu.SemaphoreType.DMA((2, slots)),
            pltpu.SemaphoreType.DMA((slots,)),
        ],
        limit=MID,
    )(me, line_of_slot, wd_here, wg_here, parts, wavelet, damping.reshape(1, f))
    return new_wavelet, residual


def solution(mesh):
    fine = Mesh(mesh.devices.reshape((2,) * 8), SHOT + RCV)
    placed = (
        P(None, SHOT, None, RCV, None),
        P(None, SHOT, RCV, None, None),
        P(SHOT, None, RCV),
        P(),
        P(),
        P(),
        P(),
        P(),
    )
    return jax.shard_map(
        update,
        mesh=fine,
        in_specs=placed,
        out_specs=(P(), P(None, SHOT, None, RCV, None)),
        check_vma=False,
    )
```

time: 103 us -> 127 us (1.23)
  blocking collectives: 0 us -> 38.4 us
  waiting for transfers between devices: 30.8 us -> 17.8 us
  starting transfers between devices: 43.3 us -> 34.4 us
  local copies, waits for them, and re-layouts: 12.4 us -> 18.5 us
  Pallas kernels: 12.9 us -> 15.4 us
  other arithmetic: 1.84 us -> 0.01 us
    all_to_all x0 -> x1, blocking collectives: none -> 38.4 us  [update(): own_natural = lax.all_to_all(own_spread, RCV, 0, 0, tiled=True)]
    all_to_all x1 -> x0, starting transfers between devices: 9.8 us -> none  [update(): own_natural = lax.all_to_all(own_spread, RCV, 0, 0, tiled=True)]
    all_to_all x1, waiting for transfers between devices: 6.89 us -> 0.01 us  [update(): own_here = lax.all_to_all(own_group, SHOT, 0, 0, tiled=True)]
    unnamed x52 -> x54, local copies, waits for them, and re-layouts: 11 us -> 17.8 us
    all_to_all x1, waiting for transfers between devices: 4.77 us -> 0.01 us  [sent_to_all(): lax.all_to_all(jnp.broadcast_to(array[None], (size, *array.shape)), axis,...]
    ppermute x11, starting transfers between devices: 21.6 us -> 19.7 us  [swapped(): return lax.ppermute(x, axis, [(i, i ^ bit) for i in range(size)])]
    pallas_call x6 -> x4, Pallas kernels: 8.04 us -> 9.68 us  [the longest x1 3.62 us: update(): call(k_cross, jax.ShapeDtypeStruct((3, f), F32), [SM, ANY, ANY] + [ANY] *...]
    all_to_all x1, starting transfers between devices: 5.76 us -> 7.23 us  [update(): own_here = lax.all_to_all(own_group, SHOT, 0, 0, tiled=True)]
  transfers between devices with their start and end apart: 14 -> 13, of which waited for: 9 -> 7; matrix products, arithmetic and copies ran while one was open for 1% -> 0% of each run, Pallas kernels for 4% -> 6%
where the time goes in v2:
time: 127 us; the launch traced here: 126 us
  blocking collectives  38.4 us (30%)
  starting transfers between devices  34.4 us (27%)
  local copies, waits for them, and re-layouts  18.5 us (15%)
  waiting for transfers between devices  17.8 us (14%)
  Pallas kernels  15.4 us (12%)
    all_to_all x1, blocking collectives, update(): own_natural = lax.all_to_all(own_spread, RCV, 0, 0, tiled=True)  38.4 us
    ppermute x11, starting transfers between devices, swapped(): return lax.ppermute(x, axis, [(i, i ^ bit) for i in range(size)])  19.7 us
    unnamed x54, local copies, waits for them, and re-layouts  17.8 us
    ppermute x11, waiting for transfers between devices, swapped(): return lax.ppermute(x, axis, [(i, i ^ bit) for i in range(size)])  17.8 us
    all_to_all x1, starting transfers between devices, sent_to_all(): lax.all_to_all(jnp.broadcast_to(array[None], (size, *array.shape)), axis,...  7.49 us
    all_to_all x1, starting transfers between devices, update(): own_here = lax.all_to_all(own_group, SHOT, 0, 0, tiled=True)  7.23 us
    pallas_call x1, Pallas kernels, update(): call(k_cross, jax.ShapeDtypeStruct((3, f), F32), [SM, ANY, ANY] + [ANY] *...  3.62 us
    pallas_call x1, Pallas kernels, update(): call(k_group, jax.ShapeDtypeStruct((slots, 2, shots, rb, f), BF16), [SM,...  2.96 us
  transfers between devices with their start and end apart: 13, of which 7 were waited for; matrix products, arithmetic and copies ran while one was open for 0% of the time, Pallas kernels for 6%

profile of v2, /device:TPU:8, one launch (start us, length us, event | category | flops | bytes accessed | tf_op | source)
XLA Modules:
  0.0 125.5 jit_solution(14182610447330127733)
XLA Ops:
  0.6 2.1 %shard_map.95 = bf16[32,4,8,512]{3,2,1,0:T(8,128)(2,1)} custom-call(bf16[4,32,8,512]{3,2,1,0:T(8,128)(2,1)} %bitcast.9), custom_call_target="tpu_custom_call" | custom-call | bytes 1048576 | tf_op jit(solution)/shard_map/pallas_call | solution.py:252
  2.8 38.4 %all_to_all.15.own_ref = bf16[32,4,8,512]{3,2,1,0:T(8,128)(2,1)} all-to-all(bf16[32,4,8,512]{3,2,1,0:T(8,128)(2,1)} %shard_map.95), channel_id=1, replica_groups=mesh['xh'=2,'yh'=2,'yl'=2,'xl'=2,'zh'=2,'zm'=2,'zl'=2,'c'=2] {'xl','zh',..., dimensions={0} | all-to-all | bytes 2097152 | tf_op jit(solution)/shard_map/all_to_all | solution.py:261
  41.1 3.0 %shard_map.96 = bf16[8,2,8,8,512]{4,3,2,1,0:T(8,128)(2,1)} custom-call(s32[64]{0:T(128)} %order_ref.1, bf16[32,4,8,512]{3,2,1,0:T(8,128)(2,1)} %all_to_all.15.own_ref), custom_call_target="tpu_custom_call" | custom-call | bytes 1048576 | tf_op jit(solution)/shard_map/pallas_call | solution.py:280
  44.1 7.2 %all-to-all-start.1 = ((bf16[8,2,64,512]{3,2,1,0:T(8,128)(2,1)}), bf16[8,2,64,512]{3,2,1,0:T(8,128)(2,1)S(1)}, u32[]{:S(2)}, u32[]{:S(2)}) async-start(bf16[8,2,64,512]{3,2,1,0:T(8,128)(2,1)} %bitcast.6), calls=%async_computation.1 | async-start | bytes 2097152 | tf_op jit(solution)/shard_map/all_to_all | solution.py:289
  51.4 1.2 copy-done.6
  54.1 2.9 %collective-permute-start.1 = (bf16[2,64,512]{2,1,0:T(8,128)(2,1)S(1)}, bf16[2,64,512]{2,1,0:T(8,128)(2,1)S(1)}, u32[]{:S(2)}, u32[]{:S(2)}) collective-permute-start(bf16[2,64,512]{2,1,0:T(8,128)(2,1)S(1)} %get-tuple-element.14.refs_2_), channel_id=1, source_target_pairs={{0,64},{32,96},{64,0},{96,32},{128,192},{160,224},{192,128},{224,1... | collective-permute-start | bytes 393224 | tf_op jit(solution)/shard_map/ppermute | solution.py:232
  58.9 3.0 %collective-permute-start.3 = (bf16[2,64,512]{2,1,0:T(8,128)(2,1)S(1)}, bf16[2,64,512]{2,1,0:T(8,128)(2,1)S(1)}, u32[]{:S(2)}, u32[]{:S(2)}) collective-permute-start(bf16[2,64,512]{2,1,0:T(8,128)(2,1)S(1)} %get-tuple-element.16.refs_4_), channel_id=1, source_target_pairs={{0,128},{32,160},{64,192},{96,224},{128,0},{160,32},{192,64},{224,... | collective-permute-start | bytes 393224 | tf_op jit(solution)/shard_map/ppermute | solution.py:232
  62.5 1.2 collective-permute-start.4
  64.4 2.9 %collective-permute-done.refs_1_ = bf16[2,64,512]{2,1,0:T(8,128)(2,1)S(1)} collective-permute-done((bf16[2,64,512]{2,1,0:T(8,128)(2,1)S(1)}, bf16[2,64,512]{2,1,0:T(8,128)(2,1)S(1)}, u32[]{:S(2)}, u32[]{:S(2)}) %collective-permute-start) | collective-permute-done | bytes 131104 | tf_op jit(solution)/shard_map/ppermute | solution.py:232
  67.3 6.5 %collective-permute-start.5 = (bf16[2,64,512]{2,1,0:T(8,128)(2,1)S(1)}, bf16[2,64,512]{2,1,0:T(8,128)(2,1)S(1)}, u32[]{:S(2)}, u32[]{:S(2)}) collective-permute-start(bf16[2,64,512]{2,1,0:T(8,128)(2,1)S(1)} %get-tuple-element.18.refs_6_), channel_id=1, source_target_pairs={{0,192},{32,224},{64,128},{96,160},{128,64},{160,96},{192,0},{224,... | collective-permute-start | bytes 393224 | tf_op jit(solution)/shard_map/ppermute | solution.py:232
  75.1 2.4 %collective-permute-done.5.refs_6_ = bf16[2,64,512]{2,1,0:T(8,128)(2,1)S(1)} collective-permute-done((bf16[2,64,512]{2,1,0:T(8,128)(2,1)S(1)}, bf16[2,64,512]{2,1,0:T(8,128)(2,1)S(1)}, u32[]{:S(2)}, u32[]{:S(2)}) %collective-permute-start.5) | collective-permute-done | bytes 131104 | tf_op jit(solution)/shard_map/ppermute | solution.py:232
  77.5 4.3 %collective-permute-done.6.refs_7_ = bf16[2,64,512]{2,1,0:T(8,128)(2,1)S(1)} collective-permute-done((bf16[2,64,512]{2,1,0:T(8,128)(2,1)S(1)}, bf16[2,64,512]{2,1,0:T(8,128)(2,1)S(1)}, u32[]{:S(2)}, u32[]{:S(2)}) %collective-permute-start.6) | collective-permute-done | bytes 131104 | tf_op jit(solution)/shard_map/ppermute | solution.py:232
  81.8 3.6 %shard_map.100 = f32[3,512]{1,0:T(4,128)S(1)} custom-call(s32[1]{0:T(128)} %bitcast.me_ref, bf16[8,2,64,512]{3,2,1,0:T(8,128)(2,1)S(1)} %bitcast.7, bf16[2,512,512]{2,1,0:T(8,128)(2,1)S(1)} %copy-done.3, bf16[2,64,512]{2,1,0:T(8,128)(2,1)S(1)} %get-tuple-element.12.refs_0_, bf16[2,64,512]{2,1,0:T(8,128)(2,1)S(1)} %collective-permute-done.refs_1_, ...), custom_call_target="tpu_custom_call" | custom-call | flops 2147483648 | bytes 1048576 | tf_op jit(solution)/shard_map/pallas_call | solution.py:291
  86.1 1.2 collective-permute-done.7
  87.3 2.6 %collective-permute-start.8 = (f32[12,128]{1,0:T(8,128)S(1)}, f32[12,128]{1,0:T(8,128)S(1)}, u32[]{:S(2)}, u32[]{:S(2)}) collective-permute-start(f32[12,128]{1,0:T(8,128)S(1)} %add.20), channel_id=1, source_target_pairs={{0,2},{2,0},{1,3},{3,1},{4,6},{6,4},{5,7},{7,5},{8,10},{10,8},{9,1... | collective-permute-start | bytes 18440 | tf_op jit(solution)/shard_map/ppermute | solution.py:232
  89.9 1.6 %collective-permute-done.8 = f32[12,128]{1,0:T(8,128)S(1)} collective-permute-done((f32[12,128]{1,0:T(8,128)S(1)}, f32[12,128]{1,0:T(8,128)S(1)}, u32[]{:S(2)}, u32[]{:S(2)}) %collective-permute-start.8) | collective-permute-done | bytes 6176 | tf_op jit(solution)/shard_map/ppermute | solution.py:232
  91.6 1.4 %collective-permute-start.9 = (f32[12,128]{1,0:T(8,128)S(1)}, f32[12,128]{1,0:T(8,128)S(1)}, u32[]{:S(2)}, u32[]{:S(2)}) collective-permute-start(f32[12,128]{1,0:T(8,128)S(1)} %add.21), channel_id=1, source_target_pairs={{0,4},{4,0},{1,5},{5,1},{2,6},{6,2},{3,7},{7,3},{8,12},{12,8},{9,1... | collective-permute-start | bytes 18440 | tf_op jit(solution)/shard_map/ppermute | solution.py:232
  93.0 3.1 %collective-permute-done.9 = f32[12,128]{1,0:T(8,128)S(1)} collective-permute-done((f32[12,128]{1,0:T(8,128)S(1)}, f32[12,128]{1,0:T(8,128)S(1)}, u32[]{:S(2)}, u32[]{:S(2)}) %collective-permute-start.9) | collective-permute-done | bytes 6176 | tf_op jit(solution)/shard_map/ppermute | solution.py:232
  96.1 1.4 %collective-permute-start.10 = (f32[12,128]{1,0:T(8,128)S(1)}, f32[12,128]{1,0:T(8,128)S(1)}, u32[]{:S(2)}, u32[]{:S(2)}) collective-permute-start(f32[12,128]{1,0:T(8,128)S(1)} %add.22), channel_id=1, source_target_pairs={{0,32},{32,0},{1,33},{33,1},{2,34},{34,2},{3,35},{35,3},{4,36},{36... | collective-permute-start | bytes 18440 | tf_op jit(solution)/shard_map/ppermute | solution.py:232
  97.5 2.3 %collective-permute-done.10 = f32[12,128]{1,0:T(8,128)S(1)} collective-permute-done((f32[12,128]{1,0:T(8,128)S(1)}, f32[12,128]{1,0:T(8,128)S(1)}, u32[]{:S(2)}, u32[]{:S(2)}) %collective-permute-start.10) | collective-permute-done | bytes 6176 | tf_op jit(solution)/shard_map/ppermute | solution.py:232
  100.5 7.5 %all-to-all-start.2 = ((f32[16,1,1536]{2,1,0:T(1,128)}), f32[16,1,1536]{2,1,0:T(1,128)S(1)}, u32[]{:S(2)}, u32[]{:S(2)}) async-start(f32[16,1,1536]{2,1,0:T(1,128)} %broadcast_in_dim.8), calls=%async_computation.2 | async-start | bytes 196608 | tf_op jit(solution)/shard_map/all_to_all | solution.py:237
  108.0 1.2 copy-done.4
  109.2 0.9 copy-done.8
  110.1 0.9 copy-done.10
  111.0 0.9 copy-done.12
  111.9 0.9 copy-done.14
  115.5 0.9 copy-done.22
  116.5 1.4 %shard_map.99.wg_ref = f32[2,8,64,512]{3,2,1,0:T(8,128)S(1)} custom-call(bf16[2,64,512]{2,1,0:T(8,128)(2,1)S(1)} %copy-done.8, bf16[2,64,512]{2,1,0:T(8,128)(2,1)S(1)} %copy-done.10, bf16[2,64,512]{2,1,0:T(8,128)(2,1)S(1)} %copy-done.12, bf16[2,64,512]{2,1,0:T(8,128)(2,1)S(1)} %copy-done.14, bf16[2,64,512]{2,1,0:T(8,128)(2,1)S(1)} %copy-done.16, ...), custom_call_target="tpu_custom_call" | custom-call | flops 1073741824 | bytes 1048576 | tf_op jit(solution)/shard_map/pallas_call | solution.py:275
  117.9 1.7 %shard_map.98.wd_ref = f32[2,8,64,512]{3,2,1,0:T(8,128)S(1)} custom-call(s32[1]{0:T(128)} %bitcast.me_ref, bf16[8,2,64,512]{3,2,1,0:T(8,128)(2,1)S(1)} %all-to-all-done.1.own_ref, f32[8,64,128]{2,1,0:T(8,128)S(1)} %get-tuple-element.11.live_ref, bf16[2,512,512]{2,1,0:T(8,128)(2,1)S(1)} %copy-done.5), custom_call_target="tpu_custom_call" | custom-call | flops 1073741824 | bytes 1048576 | tf_op jit(solution)/shard_map/pallas_call | solution.py:303
  119.6 1.4 %copy-done = f32[2,8,64,512]{3,2,1,0:T(8,128)} copy-done((f32[2,8,64,512]{3,2,1,0:T(8,128)}, f32[2,8,64,512]{3,2,1,0:T(8,128)S(1)}, u32[]{:S(2)}) %copy-start) | copy-done | bytes 2097176
  121.0 1.6 %copy-done.1 = f32[2,8,64,512]{3,2,1,0:T(8,128)S(1)} copy-done((f32[2,8,64,512]{3,2,1,0:T(8,128)S(1)}, f32[2,8,64,512]{3,2,1,0:T(8,128)}, u32[]{:S(2)}) %copy-start.1) | copy-done | bytes 2097176
  122.6 2.8 %shard_map.101 = (f32[2,512]{1,0:T(2,128)}, bf16[2,8,8,8,512]{4,3,2,1,0:T(8,128)(2,1)}) custom-call(s32[1]{0:T(128)} %bitcast.me_ref, s32[8]{0:T(128)S(1)} %copy-done.26, f32[2,8,64,512]{3,2,1,0:T(8,128)S(1)} %copy-done.1, f32[2,8,64,512]{3,2,1,0:T(8,128)S(1)} %shard_map.99.wg_ref, f32[16,1,1536]{2,1,0:T(1,128)S(1)} %all-to-all-done.2.sums_ref, ...), custom_call_target="tpu_custom_call" | custom-call | bytes 1048576 | tf_op jit(solution)/shard_map/pallas_call | solution.py:311
  (62 shorter events, 10.2 us)
Async XLA Ops:
  41.1 10.2 %copy-start.23 = (s32[8,8,8]{2,1,0:T(8,128)S(1)}, s32[8,8,8]{2,1,0:T(8,128)}, u32[]{:S(2)}) copy-start(s32[8,8,8]{2,1,0:T(8,128)} %mask_ref.1) | copy-start | bytes 6148
  41.1 10.2 %copy-start.26 = (s32[8]{0:T(128)S(1)}, s32[8]{0:T(128)}, u32[]{:S(2)}) copy-start(s32[8]{0:T(128)} %slot_ref.3) | copy-start | bytes 100
  44.1 37.7 %copy-start.2 = (bf16[8,2,8,8,512]{4,3,2,1,0:T(8,128)(2,1)S(1)}, bf16[8,2,8,8,512]{4,3,2,1,0:T(8,128)(2,1)}, u32[]{:S(2)}) copy-start(bf16[8,2,8,8,512]{4,3,2,1,0:T(8,128)(2,1)} %shard_map.96) | copy-start | bytes 3145732
  44.1 37.7 %copy-start.3 = (bf16[2,512,512]{2,1,0:T(8,128)(2,1)S(1)}, bf16[2,512,512]{2,1,0:T(8,128)(2,1)}, u32[]{:S(2)}) copy-start(bf16[2,512,512]{2,1,0:T(8,128)(2,1)} %c_ref.3) | copy-start | bytes 3145732
  44.1 55.7 %all-to-all-start.1 = ((bf16[8,2,64,512]{3,2,1,0:T(8,128)(2,1)}), bf16[8,2,64,512]{3,2,1,0:T(8,128)(2,1)S(1)}, u32[]{:S(2)}, u32[]{:S(2)}) async-start(bf16[8,2,64,512]{3,2,1,0:T(8,128)(2,1)} %bitcast.6), calls=%async_computation.1 | async-start | bytes 2097152 | tf_op jit(solution)/shard_map/all_to_all | solution.py:289
  51.4 1.2 copy-start.6
  53.4 13.9 %collective-permute-start = (bf16[2,64,512]{2,1,0:T(8,128)(2,1)S(1)}, bf16[2,64,512]{2,1,0:T(8,128)(2,1)S(1)}, u32[]{:S(2)}, u32[]{:S(2)}) collective-permute-start(bf16[2,64,512]{2,1,0:T(8,128)(2,1)S(1)} %get-tuple-element.13.refs_1_), channel_id=1, source_target_pairs={{0,32},{32,0},{64,96},{96,64},{128,160},{160,128},{192,224},{224,1... | collective-permute-start | bytes 393224 | tf_op jit(solution)/shard_map/ppermute | solution.py:232
  54.1 20.3 %collective-permute-start.1 = (bf16[2,64,512]{2,1,0:T(8,128)(2,1)S(1)}, bf16[2,64,512]{2,1,0:T(8,128)(2,1)S(1)}, u32[]{:S(2)}, u32[]{:S(2)}) collective-permute-start(bf16[2,64,512]{2,1,0:T(8,128)(2,1)S(1)} %get-tuple-element.14.refs_2_), channel_id=1, source_target_pairs={{0,64},{32,96},{64,0},{96,32},{128,192},{160,224},{192,128},{224,1... | collective-permute-start | bytes 393224 | tf_op jit(solution)/shard_map/ppermute | solution.py:232
  57.7 17.4 %collective-permute-start.2 = (bf16[2,64,512]{2,1,0:T(8,128)(2,1)S(1)}, bf16[2,64,512]{2,1,0:T(8,128)(2,1)S(1)}, u32[]{:S(2)}, u32[]{:S(2)}) collective-permute-start(bf16[2,64,512]{2,1,0:T(8,128)(2,1)S(1)} %get-tuple-element.15.refs_3_), channel_id=1, source_target_pairs={{0,96},{32,64},{64,32},{96,0},{128,224},{160,192},{192,160},{224,1... | collective-permute-start | bytes 393224 | tf_op jit(solution)/shard_map/ppermute | solution.py:232
  58.9 16.2 %collective-permute-start.3 = (bf16[2,64,512]{2,1,0:T(8,128)(2,1)S(1)}, bf16[2,64,512]{2,1,0:T(8,128)(2,1)S(1)}, u32[]{:S(2)}, u32[]{:S(2)}) collective-permute-start(bf16[2,64,512]{2,1,0:T(8,128)(2,1)S(1)} %get-tuple-element.16.refs_4_), channel_id=1, source_target_pairs={{0,128},{32,160},{64,192},{96,224},{128,0},{160,32},{192,64},{224,... | collective-permute-start | bytes 393224 | tf_op jit(solution)/shard_map/ppermute | solution.py:232
  62.5 12.6 %collective-permute-start.4 = (bf16[2,64,512]{2,1,0:T(8,128)(2,1)S(1)}, bf16[2,64,512]{2,1,0:T(8,128)(2,1)S(1)}, u32[]{:S(2)}, u32[]{:S(2)}) collective-permute-start(bf16[2,64,512]{2,1,0:T(8,128)(2,1)S(1)} %get-tuple-element.17.refs_5_), channel_id=1, source_target_pairs={{0,160},{32,128},{64,224},{96,192},{128,32},{160,0},{192,96},{224,... | collective-permute-start | bytes 393224 | tf_op jit(solution)/shard_map/ppermute | solution.py:232
  67.3 10.2 %collective-permute-start.5 = (bf16[2,64,512]{2,1,0:T(8,128)(2,1)S(1)}, bf16[2,64,512]{2,1,0:T(8,128)(2,1)S(1)}, u32[]{:S(2)}, u32[]{:S(2)}) collective-permute-start(bf16[2,64,512]{2,1,0:T(8,128)(2,1)S(1)} %get-tuple-element.18.refs_6_), channel_id=1, source_target_pairs={{0,192},{32,224},{64,128},{96,160},{128,64},{160,96},{192,0},{224,... | collective-permute-start | bytes 393224 | tf_op jit(solution)/shard_map/ppermute | solution.py:232
  74.5 7.4 %collective-permute-start.6 = (bf16[2,64,512]{2,1,0:T(8,128)(2,1)S(1)}, bf16[2,64,512]{2,1,0:T(8,128)(2,1)S(1)}, u32[]{:S(2)}, u32[]{:S(2)}) collective-permute-start(bf16[2,64,512]{2,1,0:T(8,128)(2,1)S(1)} %get-tuple-element.19.refs_7_), channel_id=1, source_target_pairs={{0,224},{32,192},{64,160},{96,128},{128,96},{160,64},{192,32},{224... | collective-permute-start | bytes 393224 | tf_op jit(solution)/shard_map/ppermute | solution.py:232
  86.1 1.2 collective-permute-start.7
  87.3 4.3 %collective-permute-start.8 = (f32[12,128]{1,0:T(8,128)S(1)}, f32[12,128]{1,0:T(8,128)S(1)}, u32[]{:S(2)}, u32[]{:S(2)}) collective-permute-start(f32[12,128]{1,0:T(8,128)S(1)} %add.20), channel_id=1, source_target_pairs={{0,2},{2,0},{1,3},{3,1},{4,6},{6,4},{5,7},{7,5},{8,10},{10,8},{9,1... | collective-permute-start | bytes 18440 | tf_op jit(solution)/shard_map/ppermute | solution.py:232
  91.6 4.5 %collective-permute-start.9 = (f32[12,128]{1,0:T(8,128)S(1)}, f32[12,128]{1,0:T(8,128)S(1)}, u32[]{:S(2)}, u32[]{:S(2)}) collective-permute-start(f32[12,128]{1,0:T(8,128)S(1)} %add.21), channel_id=1, source_target_pairs={{0,4},{4,0},{1,5},{5,1},{2,6},{6,2},{3,7},{7,3},{8,12},{12,8},{9,1... | collective-permute-start | bytes 18440 | tf_op jit(solution)/shard_map/ppermute | solution.py:232
  96.1 3.7 %collective-permute-start.10 = (f32[12,128]{1,0:T(8,128)S(1)}, f32[12,128]{1,0:T(8,128)S(1)}, u32[]{:S(2)}, u32[]{:S(2)}) collective-permute-start(f32[12,128]{1,0:T(8,128)S(1)} %add.22), channel_id=1, source_target_pairs={{0,32},{32,0},{1,33},{33,1},{2,34},{34,2},{3,35},{35,3},{4,36},{36... | collective-permute-start | bytes 18440 | tf_op jit(solution)/shard_map/ppermute | solution.py:232
  100.5 20.5 %all-to-all-start.2 = ((f32[16,1,1536]{2,1,0:T(1,128)}), f32[16,1,1536]{2,1,0:T(1,128)S(1)}, u32[]{:S(2)}, u32[]{:S(2)}) async-start(f32[16,1,1536]{2,1,0:T(1,128)} %broadcast_in_dim.8), calls=%async_computation.2 | async-start | bytes 196608 | tf_op jit(solution)/shard_map/all_to_all | solution.py:237
  108.0 1.2 copy-start.4
  109.2 0.9 copy-start.8
  110.1 0.9 copy-start.10
  111.0 0.9 copy-start.12
  111.9 0.9 copy-start.14
  112.8 0.9 copy-start.16
  113.7 0.9 copy-start.18
  114.6 0.9 copy-start.20
  115.5 0.9 copy-start.22
  116.4 1.4 %copy-start.5 = (bf16[2,512,512]{2,1,0:T(8,128)(2,1)S(1)}, bf16[2,512,512]{2,1,0:T(8,128)(2,1)}, u32[]{:S(2)}) copy-start(bf16[2,512,512]{2,1,0:T(8,128)(2,1)} %c_ref.3) | copy-start | bytes 3145732
  117.9 3.1 %copy-start.24 = (f32[2,512]{1,0:T(2,128)S(1)}, f32[2,512]{1,0:T(2,128)}, u32[]{:S(2)}) copy-start(f32[2,512]{1,0:T(2,128)} %wav_ref.1) | copy-start | bytes 12292
  117.9 3.1 %copy-start.25 = (f32[512]{0:T(512)S(1)}, f32[512]{0:T(512)}, u32[]{:S(2)}) copy-start(f32[512]{0:T(512)} %param.15) | copy-start | bytes 6148
  119.6 1.4 %copy-start = (f32[2,8,64,512]{3,2,1,0:T(8,128)}, f32[2,8,64,512]{3,2,1,0:T(8,128)S(1)}, u32[]{:S(2)}) copy-start(f32[2,8,64,512]{3,2,1,0:T(8,128)S(1)} %shard_map.98.wd_ref) | copy-start | bytes 6291460
  121.0 1.6 %copy-start.1 = (f32[2,8,64,512]{3,2,1,0:T(8,128)S(1)}, f32[2,8,64,512]{3,2,1,0:T(8,128)}, u32[]{:S(2)}) copy-start(f32[2,8,64,512]{3,2,1,0:T(8,128)} %copy-done) | copy-start | bytes 6291460
  (8 other events, 5.2 us)

commit v3 on v2

--- a/solution.py
+++ b/solution.py
@@ -9,7 +9,7 @@
 BF16 = jnp.bfloat16
 SHOT = ("xh", "yh", "yl")
 RCV = ("xl", "zh", "zm", "zl", "c")
-REST = ("xh", "yh", "xl", "zh")
+REST = ("xh", "yh", "yl", "xl")
 SWAPS = (4, 5, 6, 7, 1, 2, 3)
 
 VM = pl.BlockSpec(memory_space=pltpu.VMEM)
@@ -34,16 +34,21 @@
 CHUNKS = 4
 BIG = 62 << 20
 MID = 40 << 20
+WIN = 61 << 20
+CRS = 50 << 20
+FIN = 50 << 20
 
 
 def k_spread(obs_ref, out_ref, buf, sem_in, sem_out):
     parts, pieces = obs_ref.shape[:2]
+    held = parts // 2
     step = pieces // CHUNKS
     ins, outs = [], []
     for q in range(CHUNKS):
         rows = pl.ds(q * step, step)
         for i in range(parts):
-            ins.append(pltpu.make_async_copy(obs_ref.at[i, rows], buf.at[rows, i], sem_in.at[q, i]))
+            to = i % held * 2 + i // held
+            ins.append(pltpu.make_async_copy(obs_ref.at[i, rows], buf.at[rows, to], sem_in.at[q, i]))
         outs.append(pltpu.make_async_copy(buf.at[rows], out_ref.at[rows], sem_out.at[q]))
     for c in ins:
         c.start()
@@ -82,11 +87,15 @@
                 out_ref[c, rows] = jnp.where(live, x, 0.0).astype(BF16)
 
 
+def window(x_ref, b_ref, d):
+    x = jnp.concatenate([x_ref[0], x_ref[1]], axis=1)
+    return jnp.dot(x, b_ref[d], preferred_element_type=F32)
+
+
 def window_out(x_ref, b_ref, out_ref, buf, sem):
     copies = []
     for d in range(2):
-        w = jnp.dot(x_ref[...], b_ref[d], preferred_element_type=F32)
-        buf[d] = w.reshape(buf.shape[1:])
+        buf[d] = window(x_ref, b_ref, d).reshape(buf.shape[1:])
         copies.append(pltpu.make_async_copy(buf.at[d], out_ref.at[d], sem.at[d]))
         if d:
             copies[d - 1].start()
@@ -95,13 +104,21 @@
         c.wait()
 
 
-def k_window_here(*refs):
-    xs, c_ref, out_ref, x_ref, b_ref, buf, sem = refs[:-6], *refs[-6:]
-    couple(c_ref, b_ref)
-    rows, f = xs[0].shape[1:]
-    for b, x in enumerate(xs):
-        for c in range(2):
-            x_ref[b * rows : (b + 1) * rows, c * f : (c + 1) * f] = x[c]
+def k_window(*refs):
+    xs, c_ref, (out_ref, coup, x_ref, b_ref, buf, csem, isem, sem) = refs[:-9], refs[-9], refs[-8:]
+    rows = xs[0].shape[1]
+    first = pltpu.make_async_copy(c_ref, coup, csem)
+    first.start()
+    ins = [
+        pltpu.make_async_copy(x, x_ref.at[:, pl.ds(b * rows, rows)], isem.at[b])
+        for b, x in enumerate(xs)
+    ]
+    for c in ins:
+        c.start()
+    first.wait()
+    couple(coup, b_ref)
+    for c in ins:
+        c.wait()
     window_out(x_ref, b_ref, out_ref, buf, sem)
 
 
@@ -123,65 +140,50 @@
         alive = jnp.concatenate([live[b]] * (f // live.shape[2]), axis=1) > 0.5
         for c in range(2):
             x = own[k, c].astype(F32)
-            x_ref[b * rows : (b + 1) * rows, c * f : (c + 1) * f] = jnp.where(alive, x, 0.0).astype(BF16)
+            x_ref[c, b * rows : (b + 1) * rows] = jnp.where(alive, x, 0.0).astype(BF16)
     window_out(x_ref, b_ref, out_ref, buf, sem)
 
 
-def k_group(order_ref, own_ref, out_ref, buf, isem, sem):
-    groups, _, size = out_ref.shape[:3]
-    for g in range(groups):
+def fold(x):
+    return x.reshape(x.shape[0] // 8, 8, x.shape[1]).sum(axis=0).sum(axis=0, keepdims=True)
+
+
+def k_cross(me_ref, order_ref, own_ref, c_ref, wg_ref, sum_ref, out_ref, coup, wg, x_ref, b_ref, csem, wsem, isem, osem):
+    me = me_ref[0]
+    rb, _ = own_ref.shape[3:]
+    groups, _, rows, _ = out_ref.shape
+    size = rows // rb
+    first = pltpu.make_async_copy(c_ref, coup, csem)
+    first.start()
+    for b in range(groups):
+        g = lax.bitwise_xor(me, b)
         for s in range(size):
             n = order_ref[g * size + s]
             j = lax.shift_right_logical(n, 1)
             h = lax.bitwise_and(n, 1)
-            for c in range(2):
-                pltpu.make_async_copy(own_ref.at[j, 2 * c + h], buf.at[g, c, s], isem.at[g]).start()
-    copies = [pltpu.make_async_copy(buf.at[g], out_ref.at[g], sem.at[g]) for g in range(groups)]
-    for g in range(groups):
-        pltpu.make_async_copy(out_ref.at[g], buf.at[g], isem.at[g]).wait()
-        copies[g].start()
-    for c in copies:
-        c.wait()
-
-
-def fold(x):
-    return x.reshape(x.shape[0] // 8, 8, x.shape[1]).sum(axis=0).sum(axis=0, keepdims=True)
-
-
-def k_cross(me_ref, own_ref, c_ref, *refs):
-    mods, (out_ref, x_ref, m_ref, coup, b_ref, csem, osem, msem) = refs[:-8], refs[-8:]
-    me = me_ref[0]
-    groups = len(mods)
-    rows, f = mods[0].shape[1:]
-
-    def rows_of(dst, b, c):
-        return dst.at[pl.ds(b * rows, rows), pl.ds(c * f, f)]
-
-    first = pltpu.make_async_copy(c_ref, coup, csem)
-    first.start()
-    pairs = [(b, c) for b in range(groups) for c in range(2)]
-    owns = [
-        pltpu.make_async_copy(own_ref.at[lax.bitwise_xor(me, b), c], rows_of(x_ref, b, c), osem.at[b, c])
-        for b, c in pairs
-    ]
-    for c in owns:
-        c.start()
-    copies = [pltpu.make_async_copy(mods[b].at[c], rows_of(m_ref, b, c), msem.at[b, c]) for b, c in pairs]
-    for c in copies:
+            to = pl.ds((b * size + s) * rb, rb)
+            pltpu.make_async_copy(own_ref.at[j, h], x_ref.at[:, to], isem.at[b]).start()
+    wgs = [pltpu.make_async_copy(wg_ref.at[d], wg.at[d], wsem.at[d]) for d in range(2)]
+    for c in wgs:
         c.start()
     first.wait()
     couple(coup, b_ref)
-    for c in owns:
-        c.wait()
-    wd_re = jnp.dot(x_ref[...], b_ref[0], preferred_element_type=F32)
-    wd_im = jnp.dot(x_ref[...], b_ref[1], preferred_element_type=F32)
-    for c in copies:
-        c.wait()
-    wg_re = jnp.dot(m_ref[...], b_ref[0], preferred_element_type=F32)
-    wg_im = jnp.dot(m_ref[...], b_ref[1], preferred_element_type=F32)
-    out_ref[0:1] = fold(wg_re * wd_re + wg_im * wd_im)
-    out_ref[1:2] = fold(wg_re * wd_im - wg_im * wd_re)
-    out_ref[2:3] = fold(wg_re * wg_re + wg_im * wg_im)
+    outs = []
+    for b in range(groups):
+        part = x_ref.at[:, pl.ds(b * rows, rows)]
+        pltpu.make_async_copy(part, part, isem.at[b]).wait()
+        outs.append(pltpu.make_async_copy(part, out_ref.at[lax.bitwise_xor(me, b)], osem.at[b]))
+        outs[b].start()
+    wd_re = window(x_ref, b_ref, 0)
+    wd_im = window(x_ref, b_ref, 1)
+    for c in wgs:
+        c.wait()
+    wg_re, wg_im = wg[0].reshape(wd_re.shape), wg[1].reshape(wd_re.shape)
+    sum_ref[0:1] = fold(wg_re * wd_re + wg_im * wd_im)
+    sum_ref[1:2] = fold(wg_re * wd_im - wg_im * wd_re)
+    sum_ref[2:3] = fold(wg_re * wg_re + wg_im * wg_im)
+    for c in outs:
+        c.wait()
 
 
 def k_final(me_ref, slot_ref, wd_ref, wg_ref, sums_ref, wav_ref, damp_ref, nw_ref, out_ref, wd, wg, buf, sem, osem):
@@ -266,52 +268,48 @@
         [SM, SM, VM, VM],
     )(me, line_of_slot, modeled, mask)
     wide = jax.ShapeDtypeStruct((2, slots, rows, f), F32)
-    x_block = pltpu.VMEM((traces, 2 * f), BF16)
+    dma = pltpu.SemaphoreType.DMA
+    coup = pltpu.VMEM(coupling.shape, BF16)
+    x_block = pltpu.VMEM((2, traces, f), BF16)
     b_block = pltpu.VMEM((2, 2 * f, f), BF16)
-    window_scratch = [x_block, b_block, pltpu.VMEM((2, slots, rows, f), F32), pltpu.SemaphoreType.DMA((2,))]
+    w_block = pltpu.VMEM(wide.shape, F32)
+    window_scratch = [coup, x_block, b_block, w_block, dma, dma((slots,)), dma((2,))]
     arrived = {0: masked[0]}
     for b in SWAPS:
         arrived[b] = swapped(masked[b], SHOT, b)
     wg_here = call(
-        k_window_here, wide, [VM] * (slots + 1), HBM, flops=flops,
-        scratch=window_scratch,
+        k_window, wide, [ANY] * (slots + 1), HBM, flops=flops,
+        scratch=window_scratch, limit=WIN,
     )(*masked, coupling)
-
-    own_group = call(
-        k_group, jax.ShapeDtypeStruct((slots, 2, shots, rb, f), BF16), [SM, ANY], HBM,
-        scratch=[
-            pltpu.VMEM((slots, 2, shots, rb, f), BF16),
-            pltpu.SemaphoreType.DMA((slots,)),
-            pltpu.SemaphoreType.DMA((slots,)),
-        ],
-        limit=BIG,
-    )(shot_order, own_natural).reshape(slots, 2, rows, f)
+    wg_slot = call(
+        k_window, wide, [ANY] * (slots + 1), HBM, flops=flops,
+        scratch=window_scratch, limit=WIN,
+    )(*[arrived[b] for b in range(slots)], coupling)
+
+    sums, own_group = call(
+        k_cross,
+        (jax.ShapeDtypeStruct((3, f), F32), jax.ShapeDtypeStruct((slots, 2, rows, f), BF16)),
+        [SM, SM, ANY, ANY, HBM], [VM, HBM],
+        scratch=[coup, w_block, x_block, b_block, dma, dma((2,)), dma((slots,)), dma((slots,))],
+        limit=CRS, flops=flops,
+    )(me, shot_order, own_natural.reshape(pieces, held, 2, rb, f), coupling, wg_slot)
     own_here = lax.all_to_all(own_group, SHOT, 0, 0, tiled=True)
-    coup = pltpu.VMEM(coupling.shape, BF16)
-    sums = call(
-        k_cross, jax.ShapeDtypeStruct((3, f), F32), [SM, ANY, ANY] + [ANY] * slots,
-        scratch=[
-            x_block, x_block, coup, b_block, pltpu.SemaphoreType.DMA,
-            pltpu.SemaphoreType.DMA((slots, 2)), pltpu.SemaphoreType.DMA((slots, 2)),
-        ],
-        limit=MID, flops=2 * flops,
-    )(me, own_group, coupling, *[arrived[b] for b in range(slots)])
     sums = sums.reshape(3 * f // 128, 128)
-    for axis in ("c", "zl", "zm", "yl"):
+    for axis in ("c", "zl", "zm", "zh"):
         sums = sums + swapped(sums, axis, 1)
     parts = sent_to_all(sums.reshape(1, 3 * f), REST)
     wd_here = call(
         k_window_own, wide, [SM, ANY, ANY, ANY], HBM, flops=flops, limit=MID,
         scratch=[
             pltpu.VMEM(own_here.shape, BF16), pltpu.VMEM(live.shape, F32), coup, x_block, b_block,
-            window_scratch[2], pltpu.SemaphoreType.DMA((3,)), pltpu.SemaphoreType.DMA((2,)),
+            w_block, dma((3,)), dma((2,)),
         ],
     )(me, own_here, live, coupling)
 
     new_wavelet, residual = call(
         k_final,
         (jax.ShapeDtypeStruct((2, f), F32), jax.ShapeDtypeStruct(modeled.shape, BF16)),
-        [SM, SM, ANY, ANY, VM, VM, VM], [VM, HBM],
+        [SM, SM, HBM, HBM, VM, VM, VM], [VM, HBM],
         scratch=[
             pltpu.VMEM((2, slots, rows, f), F32),
             pltpu.VMEM((2, slots, rows, f), F32),
@@ -319,7 +317,7 @@
             pltpu.SemaphoreType.DMA((2, slots)),
             pltpu.SemaphoreType.DMA((slots,)),
         ],
-        limit=MID,
+        limit=FIN,
     )(me, line_of_slot, wd_here, wg_here, parts, wavelet, damping.reshape(1, f))
     return new_wavelet, residual
 

time: 127 us -> 98.2 us (0.77)
  blocking collectives: 38.4 us -> 0 us
  local copies, waits for them, and re-layouts: 18.5 us -> 5.94 us
  starting transfers between devices: 34.4 us -> 45.4 us
  Pallas kernels: 15.4 us -> 21.8 us
  waiting for transfers between devices: 17.8 us -> 23.3 us
    all_to_all x1 -> x0, blocking collectives: 38.4 us -> none  [update(): own_natural = lax.all_to_all(own_spread, RCV, 0, 0, tiled=True)]
    unnamed x54 -> x52, local copies, waits for them, and re-layouts: 17.8 us -> 5.24 us
    all_to_all x0 -> x1, starting transfers between devices: none -> 9.93 us  [update(): own_natural = lax.all_to_all(own_spread, RCV, 0, 0, tiled=True)]
    pallas_call x3, Pallas kernels: 8 us -> 13.5 us  [the longest x2 8.84 us: update(): call(k_window, wide, [ANY] * (slots + 1), HBM, flops=flops, scratch=windo...]
    all_to_all x1, waiting for transfers between devices: 0.01 us -> 3.24 us  [sent_to_all(): lax.all_to_all(jnp.broadcast_to(array[None], (size, *array.shape)), axis,...]
    ppermute x11, waiting for transfers between devices: 17.8 us -> 20.1 us  [swapped(): return lax.ppermute(x, axis, [(i, i ^ bit) for i in range(size)])]
    ppermute x11, starting transfers between devices: 19.7 us -> 21.7 us  [swapped(): return lax.ppermute(x, axis, [(i, i ^ bit) for i in range(size)])]
  transfers between devices with their start and end apart: 13 -> 14, of which waited for: 7 -> 7; matrix products, arithmetic and copies ran while one was open for 0% -> 0% of each run, Pallas kernels for 6% -> 12%
where the time goes in v3:
time: 98.2 us; the launch traced here: 97.4 us
  starting transfers between devices  45.4 us (46%)
  waiting for transfers between devices  23.3 us (24%)
  Pallas kernels  21.8 us (22%)
  local copies, waits for them, and re-layouts  5.94 us (6%)
  between operations  0.99 us (1%)
    ppermute x11, starting transfers between devices, swapped(): return lax.ppermute(x, axis, [(i, i ^ bit) for i in range(size)])  21.7 us
    ppermute x11, waiting for transfers between devices, swapped(): return lax.ppermute(x, axis, [(i, i ^ bit) for i in range(size)])  20.1 us
    all_to_all x1, starting transfers between devices, update(): own_natural = lax.all_to_all(own_spread, RCV, 0, 0, tiled=True)  9.93 us
    pallas_call x2, Pallas kernels, update(): call(k_window, wide, [ANY] * (slots + 1), HBM, flops=flops, scratch=windo...  8.84 us
    all_to_all x1, starting transfers between devices, sent_to_all(): lax.all_to_all(jnp.broadcast_to(array[None], (size, *array.shape)), axis,...  7.59 us
    all_to_all x1, starting transfers between devices, update(): own_here = lax.all_to_all(own_group, SHOT, 0, 0, tiled=True)  6.18 us
    unnamed x52, local copies, waits for them, and re-layouts  5.24 us
    pallas_call x1, Pallas kernels, update(): call(k_cross, (jax.ShapeDtypeStruct((3, f), F32), jax.ShapeDtypeStruct((s...  4.7 us
  transfers between devices with their start and end apart: 14, of which 7 were waited for; matrix products, arithmetic and copies ran while one was open for 0% of the time, Pallas kernels for 12%

profile of v3, /device:TPU:8, one launch (start us, length us, event | category | flops | bytes accessed | tf_op | source)
XLA Modules:
  0.0 97.4 jit_solution(13369546372419461624)
XLA Ops:
  0.7 2.1 %shard_map.95 = bf16[32,4,8,512]{3,2,1,0:T(8,128)(2,1)} custom-call(bf16[4,32,8,512]{3,2,1,0:T(8,128)(2,1)} %bitcast.8), custom_call_target="tpu_custom_call" | custom-call | bytes 1048576 | tf_op jit(solution)/shard_map/pallas_call | solution.py:254
  2.8 9.9 %all-to-all-start = ((bf16[32,4,8,512]{3,2,1,0:T(8,128)(2,1)}), bf16[32,4,8,512]{3,2,1,0:T(8,128)(2,1)S(1)}, u32[]{:S(2)}, u32[]{:S(2)}) async-start(bf16[32,4,8,512]{3,2,1,0:T(8,128)(2,1)} %shard_map.95), calls=%async_computation | async-start | bytes 2097152 | tf_op jit(solution)/shard_map/all_to_all | solution.py:263
  12.8 0.8 shard_map.96
  13.6 0.6 copy-done.6
  14.3 0.5 collective-permute-start
  14.8 2.6 %collective-permute-start.1 = (bf16[2,64,512]{2,1,0:T(8,128)(2,1)S(1)}, bf16[2,64,512]{2,1,0:T(8,128)(2,1)S(1)}, u32[]{:S(2)}, u32[]{:S(2)}) collective-permute-start(bf16[2,64,512]{2,1,0:T(8,128)(2,1)S(1)} %get-tuple-element.15.refs_2_), channel_id=1, source_target_pairs={{0,64},{32,96},{64,0},{96,32},{128,192},{160,224},{192,128},{224,1... | collective-permute-start | bytes 393224 | tf_op jit(solution)/shard_map/ppermute | solution.py:234
  17.8 2.7 %collective-permute-start.3 = (bf16[2,64,512]{2,1,0:T(8,128)(2,1)S(1)}, bf16[2,64,512]{2,1,0:T(8,128)(2,1)S(1)}, u32[]{:S(2)}, u32[]{:S(2)}) collective-permute-start(bf16[2,64,512]{2,1,0:T(8,128)(2,1)S(1)} %get-tuple-element.17.refs_4_), channel_id=1, source_target_pairs={{0,128},{32,160},{64,192},{96,224},{128,0},{160,32},{192,64},{224,... | collective-permute-start | bytes 393224 | tf_op jit(solution)/shard_map/ppermute | solution.py:234
  20.6 1.9 %collective-permute-start.4 = (bf16[2,64,512]{2,1,0:T(8,128)(2,1)S(1)}, bf16[2,64,512]{2,1,0:T(8,128)(2,1)S(1)}, u32[]{:S(2)}, u32[]{:S(2)}) collective-permute-start(bf16[2,64,512]{2,1,0:T(8,128)(2,1)S(1)} %get-tuple-element.18.refs_5_), channel_id=1, source_target_pairs={{0,160},{32,128},{64,224},{96,192},{128,32},{160,0},{192,96},{224,... | collective-permute-start | bytes 393224 | tf_op jit(solution)/shard_map/ppermute | solution.py:234
  22.5 3.5 %collective-permute-start.5 = (bf16[2,64,512]{2,1,0:T(8,128)(2,1)S(1)}, bf16[2,64,512]{2,1,0:T(8,128)(2,1)S(1)}, u32[]{:S(2)}, u32[]{:S(2)}) collective-permute-start(bf16[2,64,512]{2,1,0:T(8,128)(2,1)S(1)} %get-tuple-element.19.refs_6_), channel_id=1, source_target_pairs={{0,192},{32,224},{64,128},{96,160},{128,64},{160,96},{192,0},{224,... | collective-permute-start | bytes 393224 | tf_op jit(solution)/shard_map/ppermute | solution.py:234
  26.0 1.1 %collective-permute-start.6 = (bf16[2,64,512]{2,1,0:T(8,128)(2,1)S(1)}, bf16[2,64,512]{2,1,0:T(8,128)(2,1)S(1)}, u32[]{:S(2)}, u32[]{:S(2)}) collective-permute-start(bf16[2,64,512]{2,1,0:T(8,128)(2,1)S(1)} %get-tuple-element.20.refs_7_), channel_id=1, source_target_pairs={{0,224},{32,192},{64,160},{96,128},{128,96},{160,64},{192,32},{224... | collective-permute-start | bytes 393224 | tf_op jit(solution)/shard_map/ppermute | solution.py:234
  27.2 6.7 %collective-permute-done.4.refs_5_ = bf16[2,64,512]{2,1,0:T(8,128)(2,1)S(1)} collective-permute-done((bf16[2,64,512]{2,1,0:T(8,128)(2,1)S(1)}, bf16[2,64,512]{2,1,0:T(8,128)(2,1)S(1)}, u32[]{:S(2)}, u32[]{:S(2)}) %collective-permute-start.4) | collective-permute-done | bytes 131104 | tf_op jit(solution)/shard_map/ppermute | solution.py:234
  33.9 7.0 %collective-permute-done.5.refs_6_ = bf16[2,64,512]{2,1,0:T(8,128)(2,1)S(1)} collective-permute-done((bf16[2,64,512]{2,1,0:T(8,128)(2,1)S(1)}, bf16[2,64,512]{2,1,0:T(8,128)(2,1)S(1)}, u32[]{:S(2)}, u32[]{:S(2)}) %collective-permute-start.5) | collective-permute-done | bytes 131104 | tf_op jit(solution)/shard_map/ppermute | solution.py:234
  40.9 0.9 collective-permute-done.6.refs_7_
  41.8 0.6 copy-done.25
  42.5 4.5 %shard_map.97.wg_ref = f32[2,8,64,512]{3,2,1,0:T(8,128)} custom-call(bf16[2,64,512]{2,1,0:T(8,128)(2,1)} %copy-done.6, bf16[2,64,512]{2,1,0:T(8,128)(2,1)} %copy-done.19, bf16[2,64,512]{2,1,0:T(8,128)(2,1)} %copy-done.20, bf16[2,64,512]{2,1,0:T(8,128)(2,1)} %copy-done.21, bf16[2,64,512]{2,1,0:T(8,128)(2,1)} %copy-done.22, bf16[2,64,512]{2,1,0:T(8,128)(2,1)} %copy-done.23, ...), custom_call_target="tpu_custom_call" | custom-call | flops 1073741824 | bytes 1048576 | tf_op jit(solution)/shard_map/pallas_call | solution.py:284
  47.0 4.7 %shard_map.98 = (f32[3,512]{1,0:T(4,128)S(1)}, bf16[8,2,64,512]{3,2,1,0:T(8,128)(2,1)S(1)}) custom-call(s32[1]{0:T(128)} %bitcast.me_ref, s32[64]{0:T(128)S(1)} %copy-done.18, bf16[32,2,2,8,512]{4,3,2,1,0:T(8,128)(2,1)S(1)} %bitcast.6, bf16[2,512,512]{2,1,0:T(8,128)(2,1)S(1)} %copy-done, f32[2,8,64,512]{3,2,1,0:T(8,128)} %shard_map.97.wg_ref), custom_call_target="tpu_custom_call" | custom-call | flops 1073741824 | bytes 1048576 | tf_op jit(solution)/shard_map/pallas_call | solution.py:289
  51.7 1.0 copy-done.5
  52.7 6.2 %all-to-all-start.1 = ((bf16[8,2,64,512]{3,2,1,0:T(8,128)(2,1)}), bf16[8,2,64,512]{3,2,1,0:T(8,128)(2,1)S(1)}, u32[]{:S(2)}, u32[]{:S(2)}) async-start(bf16[8,2,64,512]{3,2,1,0:T(8,128)(2,1)} %copy-done.5), calls=%async_computation.1 | async-start | bytes 2097152 | tf_op jit(solution)/shard_map/all_to_all | solution.py:296
  59.0 1.2 %collective-permute-done.7 = f32[12,128]{1,0:T(8,128)S(1)} collective-permute-done((f32[12,128]{1,0:T(8,128)S(1)}, f32[12,128]{1,0:T(8,128)S(1)}, u32[]{:S(2)}, u32[]{:S(2)}) %collective-permute-start.7) | collective-permute-done | bytes 6176 | tf_op jit(solution)/shard_map/ppermute | solution.py:234
  60.1 1.5 %collective-permute-start.8 = (f32[12,128]{1,0:T(8,128)S(1)}, f32[12,128]{1,0:T(8,128)S(1)}, u32[]{:S(2)}, u32[]{:S(2)}) collective-permute-start(f32[12,128]{1,0:T(8,128)S(1)} %add.20), channel_id=1, source_target_pairs={{0,2},{2,0},{1,3},{3,1},{4,6},{6,4},{5,7},{7,5},{8,10},{10,8},{9,1... | collective-permute-start | bytes 18440 | tf_op jit(solution)/shard_map/ppermute | solution.py:234
  61.7 2.1 %collective-permute-done.8 = f32[12,128]{1,0:T(8,128)S(1)} collective-permute-done((f32[12,128]{1,0:T(8,128)S(1)}, f32[12,128]{1,0:T(8,128)S(1)}, u32[]{:S(2)}, u32[]{:S(2)}) %collective-permute-start.8) | collective-permute-done | bytes 6176 | tf_op jit(solution)/shard_map/ppermute | solution.py:234
  63.8 2.3 %collective-permute-start.9 = (f32[12,128]{1,0:T(8,128)S(1)}, f32[12,128]{1,0:T(8,128)S(1)}, u32[]{:S(2)}, u32[]{:S(2)}) collective-permute-start(f32[12,128]{1,0:T(8,128)S(1)} %add.21), channel_id=1, source_target_pairs={{0,4},{4,0},{1,5},{5,1},{2,6},{6,2},{3,7},{7,3},{8,12},{12,8},{9,1... | collective-permute-start | bytes 18440 | tf_op jit(solution)/shard_map/ppermute | solution.py:234
  66.1 2.2 %collective-permute-done.9 = f32[12,128]{1,0:T(8,128)S(1)} collective-permute-done((f32[12,128]{1,0:T(8,128)S(1)}, f32[12,128]{1,0:T(8,128)S(1)}, u32[]{:S(2)}, u32[]{:S(2)}) %collective-permute-start.9) | collective-permute-done | bytes 6176 | tf_op jit(solution)/shard_map/ppermute | solution.py:234
  68.4 4.8 %collective-permute-start.10 = (f32[12,128]{1,0:T(8,128)S(1)}, f32[12,128]{1,0:T(8,128)S(1)}, u32[]{:S(2)}, u32[]{:S(2)}) collective-permute-start(f32[12,128]{1,0:T(8,128)S(1)} %add.22), channel_id=1, source_target_pairs={{0,8},{8,0},{1,9},{9,1},{2,10},{10,2},{3,11},{11,3},{4,12},{12,4},... | collective-permute-start | bytes 18440 | tf_op jit(solution)/shard_map/ppermute | solution.py:234
  73.2 4.4 %shard_map.100.wg_ref = f32[2,8,64,512]{3,2,1,0:T(8,128)} custom-call(bf16[2,64,512]{2,1,0:T(8,128)(2,1)} %copy-done.6, bf16[2,64,512]{2,1,0:T(8,128)(2,1)} %copy-done.7, bf16[2,64,512]{2,1,0:T(8,128)(2,1)} %copy-done.8, bf16[2,64,512]{2,1,0:T(8,128)(2,1)} %copy-done.9, bf16[2,64,512]{2,1,0:T(8,128)(2,1)} %copy-done.10, bf16[2,64,512]{2,1,0:T(8,128)(2,1)} %copy-done.11, ...), custom_call_target="tpu_custom_call" | custom-call | flops 1073741824 | bytes 1048576 | tf_op jit(solution)/shard_map/pallas_call | solution.py:280
  77.6 0.7 broadcast_in_dim.8
  78.3 7.6 %all-to-all-start.2 = ((f32[16,1,1536]{2,1,0:T(1,128)}), f32[16,1,1536]{2,1,0:T(1,128)S(1)}, u32[]{:S(2)}, u32[]{:S(2)}) async-start(f32[16,1,1536]{2,1,0:T(1,128)} %broadcast_in_dim.8), calls=%async_computation.2 | async-start | bytes 196608 | tf_op jit(solution)/shard_map/all_to_all | solution.py:239
  85.9 1.7 %shard_map.99.wd_ref = f32[2,8,64,512]{3,2,1,0:T(8,128)S(1)} custom-call(s32[1]{0:T(128)} %bitcast.me_ref, bf16[8,2,64,512]{3,2,1,0:T(8,128)(2,1)S(1)} %all-to-all-done.1.own_ref, f32[8,64,128]{2,1,0:T(8,128)S(1)} %get-tuple-element.22.live_ref, bf16[2,512,512]{2,1,0:T(8,128)(2,1)S(1)} %copy-done.1), custom_call_target="tpu_custom_call" | custom-call | flops 1073741824 | bytes 1048576 | tf_op jit(solution)/shard_map/pallas_call | solution.py:301
  87.6 1.3 %copy-done.2 = f32[2,8,64,512]{3,2,1,0:T(8,128)} copy-done((f32[2,8,64,512]{3,2,1,0:T(8,128)}, f32[2,8,64,512]{3,2,1,0:T(8,128)S(1)}, u32[]{:S(2)}) %copy-start.2) | copy-done | bytes 2097176
  88.9 3.2 %all-to-all-done.2.sums_ref = f32[16,1,1536]{2,1,0:T(1,128)S(1)} async-done(((f32[16,1,1536]{2,1,0:T(1,128)}), f32[16,1,1536]{2,1,0:T(1,128)S(1)}, u32[]{:S(2)}, u32[]{:S(2)}) %all-to-all-start.2) | async-done | bytes 98336 | tf_op jit(solution)/shard_map/all_to_all | solution.py:239
  92.2 1.6 %copy-done.3 = f32[2,8,64,512]{3,2,1,0:T(8,128)S(1)} copy-done((f32[2,8,64,512]{3,2,1,0:T(8,128)S(1)}, f32[2,8,64,512]{3,2,1,0:T(8,128)}, u32[]{:S(2)}) %copy-start.3) | copy-done | bytes 2097176
  93.8 3.6 %shard_map.101 = (f32[2,512]{1,0:T(2,128)}, bf16[2,8,8,8,512]{4,3,2,1,0:T(8,128)(2,1)}) custom-call(s32[1]{0:T(128)} %bitcast.me_ref, s32[8]{0:T(128)S(1)} %copy-done.17, f32[2,8,64,512]{3,2,1,0:T(8,128)S(1)} %copy-done.3, f32[2,8,64,512]{3,2,1,0:T(8,128)} %shard_map.100.wg_ref, f32[16,1,1536]{2,1,0:T(1,128)S(1)} %all-to-all-done.2.sums_ref, ...), custom_call_target="tpu_custom_call" | custom-call | bytes 1048576 | tf_op jit(solution)/shard_map/pallas_call | solution.py:309
  (61 shorter events, 0.7 us)
Async XLA Ops:
  0.6 12.1 %copy-start.14 = (s32[8,8,8]{2,1,0:T(8,128)S(1)}, s32[8,8,8]{2,1,0:T(8,128)}, u32[]{:S(2)}) copy-start(s32[8,8,8]{2,1,0:T(8,128)} %mask_ref.1) | copy-start | bytes 6148
  0.6 12.1 %copy-start.17 = (s32[8]{0:T(128)S(1)}, s32[8]{0:T(128)}, u32[]{:S(2)}) copy-start(s32[8]{0:T(128)} %slot_ref.3) | copy-start | bytes 100
  2.8 10.0 %copy-start.4 = (bf16[2,8,8,8,512]{4,3,2,1,0:T(8,128)(2,1)S(1)}, bf16[2,8,8,8,512]{4,3,2,1,0:T(8,128)(2,1)}, u32[]{:S(2)}) copy-start(bf16[2,8,8,8,512]{4,3,2,1,0:T(8,128)(2,1)} %mod_ref.1) | copy-start | bytes 3145732
  2.8 44.2 %all-to-all-start = ((bf16[32,4,8,512]{3,2,1,0:T(8,128)(2,1)}), bf16[32,4,8,512]{3,2,1,0:T(8,128)(2,1)S(1)}, u32[]{:S(2)}, u32[]{:S(2)}) async-start(bf16[32,4,8,512]{3,2,1,0:T(8,128)(2,1)} %shard_map.95), calls=%async_computation | async-start | bytes 2097152 | tf_op jit(solution)/shard_map/all_to_all | solution.py:263
  14.2 27.5 %copy-start.12 = (bf16[2,64,512]{2,1,0:T(8,128)(2,1)}, bf16[2,64,512]{2,1,0:T(8,128)(2,1)S(1)}, u32[]{:S(2)}) copy-start(bf16[2,64,512]{2,1,0:T(8,128)(2,1)S(1)} %get-tuple-element.19.refs_6_) | copy-start | bytes 393220
  14.2 27.5 %copy-start.13 = (bf16[2,64,512]{2,1,0:T(8,128)(2,1)}, bf16[2,64,512]{2,1,0:T(8,128)(2,1)S(1)}, u32[]{:S(2)}) copy-start(bf16[2,64,512]{2,1,0:T(8,128)(2,1)S(1)} %get-tuple-element.20.refs_7_) | copy-start | bytes 393220
  14.2 32.7 %copy-start.7 = (bf16[2,64,512]{2,1,0:T(8,128)(2,1)}, bf16[2,64,512]{2,1,0:T(8,128)(2,1)S(1)}, u32[]{:S(2)}) copy-start(bf16[2,64,512]{2,1,0:T(8,128)(2,1)S(1)} %get-tuple-element.14.refs_1_) | copy-start | bytes 393220
  14.2 32.7 %copy-start.8 = (bf16[2,64,512]{2,1,0:T(8,128)(2,1)}, bf16[2,64,512]{2,1,0:T(8,128)(2,1)S(1)}, u32[]{:S(2)}) copy-start(bf16[2,64,512]{2,1,0:T(8,128)(2,1)S(1)} %get-tuple-element.15.refs_2_) | copy-start | bytes 393220
  14.2 32.7 %copy-start.9 = (bf16[2,64,512]{2,1,0:T(8,128)(2,1)}, bf16[2,64,512]{2,1,0:T(8,128)(2,1)S(1)}, u32[]{:S(2)}) copy-start(bf16[2,64,512]{2,1,0:T(8,128)(2,1)S(1)} %get-tuple-element.16.refs_3_) | copy-start | bytes 393220
  14.2 32.7 %copy-start.10 = (bf16[2,64,512]{2,1,0:T(8,128)(2,1)}, bf16[2,64,512]{2,1,0:T(8,128)(2,1)S(1)}, u32[]{:S(2)}) copy-start(bf16[2,64,512]{2,1,0:T(8,128)(2,1)S(1)} %get-tuple-element.17.refs_4_) | copy-start | bytes 393220
  14.3 32.7 %copy-start.11 = (bf16[2,64,512]{2,1,0:T(8,128)(2,1)}, bf16[2,64,512]{2,1,0:T(8,128)(2,1)S(1)}, u32[]{:S(2)}) copy-start(bf16[2,64,512]{2,1,0:T(8,128)(2,1)S(1)} %get-tuple-element.18.refs_5_) | copy-start | bytes 393220
  14.3 8.2 %collective-permute-start = (bf16[2,64,512]{2,1,0:T(8,128)(2,1)S(1)}, bf16[2,64,512]{2,1,0:T(8,128)(2,1)S(1)}, u32[]{:S(2)}, u32[]{:S(2)}) collective-permute-start(bf16[2,64,512]{2,1,0:T(8,128)(2,1)S(1)} %get-tuple-element.14.refs_1_), channel_id=1, source_target_pairs={{0,32},{32,0},{64,96},{96,64},{128,160},{160,128},{192,224},{224,1... | collective-permute-start | bytes 393224 | tf_op jit(solution)/shard_map/ppermute | solution.py:234
  14.8 11.2 %collective-permute-start.1 = (bf16[2,64,512]{2,1,0:T(8,128)(2,1)S(1)}, bf16[2,64,512]{2,1,0:T(8,128)(2,1)S(1)}, u32[]{:S(2)}, u32[]{:S(2)}) collective-permute-start(bf16[2,64,512]{2,1,0:T(8,128)(2,1)S(1)} %get-tuple-element.15.refs_2_), channel_id=1, source_target_pairs={{0,64},{32,96},{64,0},{96,32},{128,192},{160,224},{192,128},{224,1... | collective-permute-start | bytes 393224 | tf_op jit(solution)/shard_map/ppermute | solution.py:234
  17.4 9.8 %collective-permute-start.2 = (bf16[2,64,512]{2,1,0:T(8,128)(2,1)S(1)}, bf16[2,64,512]{2,1,0:T(8,128)(2,1)S(1)}, u32[]{:S(2)}, u32[]{:S(2)}) collective-permute-start(bf16[2,64,512]{2,1,0:T(8,128)(2,1)S(1)} %get-tuple-element.16.refs_3_), channel_id=1, source_target_pairs={{0,96},{32,64},{64,32},{96,0},{128,224},{160,192},{192,160},{224,1... | collective-permute-start | bytes 393224 | tf_op jit(solution)/shard_map/ppermute | solution.py:234
  17.8 9.3 %collective-permute-start.3 = (bf16[2,64,512]{2,1,0:T(8,128)(2,1)S(1)}, bf16[2,64,512]{2,1,0:T(8,128)(2,1)S(1)}, u32[]{:S(2)}, u32[]{:S(2)}) collective-permute-start(bf16[2,64,512]{2,1,0:T(8,128)(2,1)S(1)} %get-tuple-element.17.refs_4_), channel_id=1, source_target_pairs={{0,128},{32,160},{64,192},{96,224},{128,0},{160,32},{192,64},{224,... | collective-permute-start | bytes 393224 | tf_op jit(solution)/shard_map/ppermute | solution.py:234
  20.6 13.3 %collective-permute-start.4 = (bf16[2,64,512]{2,1,0:T(8,128)(2,1)S(1)}, bf16[2,64,512]{2,1,0:T(8,128)(2,1)S(1)}, u32[]{:S(2)}, u32[]{:S(2)}) collective-permute-start(bf16[2,64,512]{2,1,0:T(8,128)(2,1)S(1)} %get-tuple-element.18.refs_5_), channel_id=1, source_target_pairs={{0,160},{32,128},{64,224},{96,192},{128,32},{160,0},{192,96},{224,... | collective-permute-start | bytes 393224 | tf_op jit(solution)/shard_map/ppermute | solution.py:234
  22.5 19.3 %copy-start.19 = (bf16[2,64,512]{2,1,0:T(8,128)(2,1)}, bf16[2,64,512]{2,1,0:T(8,128)(2,1)S(1)}, u32[]{:S(2)}) copy-start(bf16[2,64,512]{2,1,0:T(8,128)(2,1)S(1)} %collective-permute-done.refs_1_) | copy-start | bytes 393220
  22.5 18.4 %collective-permute-start.5 = (bf16[2,64,512]{2,1,0:T(8,128)(2,1)S(1)}, bf16[2,64,512]{2,1,0:T(8,128)(2,1)S(1)}, u32[]{:S(2)}, u32[]{:S(2)}) collective-permute-start(bf16[2,64,512]{2,1,0:T(8,128)(2,1)S(1)} %get-tuple-element.19.refs_6_), channel_id=1, source_target_pairs={{0,192},{32,224},{64,128},{96,160},{128,64},{160,96},{192,0},{224,... | collective-permute-start | bytes 393224 | tf_op jit(solution)/shard_map/ppermute | solution.py:234
  26.0 15.7 %copy-start.20 = (bf16[2,64,512]{2,1,0:T(8,128)(2,1)}, bf16[2,64,512]{2,1,0:T(8,128)(2,1)S(1)}, u32[]{:S(2)}) copy-start(bf16[2,64,512]{2,1,0:T(8,128)(2,1)S(1)} %collective-permute-done.1.refs_2_) | copy-start | bytes 393220
  26.0 15.7 %collective-permute-start.6 = (bf16[2,64,512]{2,1,0:T(8,128)(2,1)S(1)}, bf16[2,64,512]{2,1,0:T(8,128)(2,1)S(1)}, u32[]{:S(2)}, u32[]{:S(2)}) collective-permute-start(bf16[2,64,512]{2,1,0:T(8,128)(2,1)S(1)} %get-tuple-element.20.refs_7_), channel_id=1, source_target_pairs={{0,224},{32,192},{64,160},{96,128},{128,96},{160,64},{192,32},{224... | collective-permute-start | bytes 393224 | tf_op jit(solution)/shard_map/ppermute | solution.py:234
  27.2 14.6 %copy-start.21 = (bf16[2,64,512]{2,1,0:T(8,128)(2,1)}, bf16[2,64,512]{2,1,0:T(8,128)(2,1)S(1)}, u32[]{:S(2)}) copy-start(bf16[2,64,512]{2,1,0:T(8,128)(2,1)S(1)} %collective-permute-done.2.refs_3_) | copy-start | bytes 393220
  27.2 14.6 %copy-start.22 = (bf16[2,64,512]{2,1,0:T(8,128)(2,1)}, bf16[2,64,512]{2,1,0:T(8,128)(2,1)S(1)}, u32[]{:S(2)}) copy-start(bf16[2,64,512]{2,1,0:T(8,128)(2,1)S(1)} %collective-permute-done.3.refs_4_) | copy-start | bytes 393220
  33.9 7.9 %copy-start.23 = (bf16[2,64,512]{2,1,0:T(8,128)(2,1)}, bf16[2,64,512]{2,1,0:T(8,128)(2,1)S(1)}, u32[]{:S(2)}) copy-start(bf16[2,64,512]{2,1,0:T(8,128)(2,1)S(1)} %collective-permute-done.4.refs_5_) | copy-start | bytes 393220
  52.7 24.9 %all-to-all-start.1 = ((bf16[8,2,64,512]{3,2,1,0:T(8,128)(2,1)}), bf16[8,2,64,512]{3,2,1,0:T(8,128)(2,1)S(1)}, u32[]{:S(2)}, u32[]{:S(2)}) async-start(bf16[8,2,64,512]{3,2,1,0:T(8,128)(2,1)} %copy-done.5), calls=%async_computation.1 | async-start | bytes 2097152 | tf_op jit(solution)/shard_map/all_to_all | solution.py:296
  58.9 1.3 %collective-permute-start.7 = (f32[12,128]{1,0:T(8,128)S(1)}, f32[12,128]{1,0:T(8,128)S(1)}, u32[]{:S(2)}, u32[]{:S(2)}) collective-permute-start(f32[12,128]{1,0:T(8,128)S(1)} %reshape.25), channel_id=1, source_target_pairs={{0,1},{1,0},{2,3},{3,2},{4,5},{5,4},{6,7},{7,6},{8,9},{9,8},{10,11... | collective-permute-start | bytes 18440 | tf_op jit(solution)/shard_map/ppermute | solution.py:234
  60.1 3.7 %collective-permute-start.8 = (f32[12,128]{1,0:T(8,128)S(1)}, f32[12,128]{1,0:T(8,128)S(1)}, u32[]{:S(2)}, u32[]{:S(2)}) collective-permute-start(f32[12,128]{1,0:T(8,128)S(1)} %add.20), channel_id=1, source_target_pairs={{0,2},{2,0},{1,3},{3,1},{4,6},{6,4},{5,7},{7,5},{8,10},{10,8},{9,1... | collective-permute-start | bytes 18440 | tf_op jit(solution)/shard_map/ppermute | solution.py:234
  63.8 4.5 %collective-permute-start.9 = (f32[12,128]{1,0:T(8,128)S(1)}, f32[12,128]{1,0:T(8,128)S(1)}, u32[]{:S(2)}, u32[]{:S(2)}) collective-permute-start(f32[12,128]{1,0:T(8,128)S(1)} %add.21), channel_id=1, source_target_pairs={{0,4},{4,0},{1,5},{5,1},{2,6},{6,2},{3,7},{7,3},{8,12},{12,8},{9,1... | collective-permute-start | bytes 18440 | tf_op jit(solution)/shard_map/ppermute | solution.py:234
  68.4 17.5 %copy-start.1 = (bf16[2,512,512]{2,1,0:T(8,128)(2,1)S(1)}, bf16[2,512,512]{2,1,0:T(8,128)(2,1)}, u32[]{:S(2)}) copy-start(bf16[2,512,512]{2,1,0:T(8,128)(2,1)} %refs_8_.3) | copy-start | bytes 3145732
  68.4 9.2 %collective-permute-start.10 = (f32[12,128]{1,0:T(8,128)S(1)}, f32[12,128]{1,0:T(8,128)S(1)}, u32[]{:S(2)}, u32[]{:S(2)}) collective-permute-start(f32[12,128]{1,0:T(8,128)S(1)} %add.22), channel_id=1, source_target_pairs={{0,8},{8,0},{1,9},{9,1},{2,10},{10,2},{3,11},{11,3},{4,12},{12,4},... | collective-permute-start | bytes 18440 | tf_op jit(solution)/shard_map/ppermute | solution.py:234
  78.3 13.9 %all-to-all-start.2 = ((f32[16,1,1536]{2,1,0:T(1,128)}), f32[16,1,1536]{2,1,0:T(1,128)S(1)}, u32[]{:S(2)}, u32[]{:S(2)}) async-start(f32[16,1,1536]{2,1,0:T(1,128)} %broadcast_in_dim.8), calls=%async_computation.2 | async-start | bytes 196608 | tf_op jit(solution)/shard_map/all_to_all | solution.py:239
  85.9 6.3 %copy-start.15 = (f32[2,512]{1,0:T(2,128)S(1)}, f32[2,512]{1,0:T(2,128)}, u32[]{:S(2)}) copy-start(f32[2,512]{1,0:T(2,128)} %wav_ref.1) | copy-start | bytes 12292
  85.9 6.3 %copy-start.16 = (f32[512]{0:T(512)S(1)}, f32[512]{0:T(512)}, u32[]{:S(2)}) copy-start(f32[512]{0:T(512)} %param.15) | copy-start | bytes 6148
  (8 other events, 15.2 us)

commit v4 on v3

--- a/solution.py
+++ b/solution.py
@@ -36,6 +36,7 @@
 MID = 40 << 20
 WIN = 61 << 20
 CRS = 50 << 20
+GRP = 51 << 20
 FIN = 50 << 20
 
 
@@ -148,42 +149,59 @@
     return x.reshape(x.shape[0] // 8, 8, x.shape[1]).sum(axis=0).sum(axis=0, keepdims=True)
 
 
-def k_cross(me_ref, order_ref, own_ref, c_ref, wg_ref, sum_ref, out_ref, coup, wg, x_ref, b_ref, csem, wsem, isem, osem):
-    me = me_ref[0]
-    rb, _ = own_ref.shape[3:]
+def k_group(order_ref, own_ref, out_ref, buf, sem):
     groups, _, rows, _ = out_ref.shape
+    rb = own_ref.shape[3]
     size = rows // rb
-    first = pltpu.make_async_copy(c_ref, coup, csem)
-    first.start()
-    for b in range(groups):
-        g = lax.bitwise_xor(me, b)
+    copies = [pltpu.make_async_copy(buf.at[g], out_ref.at[g], sem.at[g]) for g in range(groups)]
+    for g in range(groups):
         for s in range(size):
             n = order_ref[g * size + s]
             j = lax.shift_right_logical(n, 1)
             h = lax.bitwise_and(n, 1)
-            to = pl.ds((b * size + s) * rb, rb)
-            pltpu.make_async_copy(own_ref.at[j, h], x_ref.at[:, to], isem.at[b]).start()
-    wgs = [pltpu.make_async_copy(wg_ref.at[d], wg.at[d], wsem.at[d]) for d in range(2)]
-    for c in wgs:
+            for c in range(2):
+                buf[g, c, s * rb : (s + 1) * rb] = own_ref[j, h, c]
+        if g:
+            copies[g - 1].start()
+    copies[-1].start()
+    for c in copies:
+        c.wait()
+
+
+def k_cross(me_ref, own_ref, c_ref, *refs):
+    mods, (sum_ref, coup, x_ref, m_ref, b_ref, csem, osem, msem) = refs[:-8], refs[-8:]
+    me = me_ref[0]
+    groups = len(mods)
+    rows = mods[0].shape[1]
+    first = pltpu.make_async_copy(c_ref, coup, csem)
+    first.start()
+    owns = [
+        pltpu.make_async_copy(
+            own_ref.at[lax.bitwise_xor(me, b)], x_ref.at[:, pl.ds(b * rows, rows)], osem.at[b]
+        )
+        for b in range(groups)
+    ]
+    for c in owns:
+        c.start()
+    copies = [
+        pltpu.make_async_copy(mods[b], m_ref.at[:, pl.ds(b * rows, rows)], msem.at[b])
+        for b in range(groups)
+    ]
+    for c in copies:
         c.start()
     first.wait()
     couple(coup, b_ref)
-    outs = []
-    for b in range(groups):
-        part = x_ref.at[:, pl.ds(b * rows, rows)]
-        pltpu.make_async_copy(part, part, isem.at[b]).wait()
-        outs.append(pltpu.make_async_copy(part, out_ref.at[lax.bitwise_xor(me, b)], osem.at[b]))
-        outs[b].start()
+    for c in owns:
+        c.wait()
     wd_re = window(x_ref, b_ref, 0)
     wd_im = window(x_ref, b_ref, 1)
-    for c in wgs:
-        c.wait()
-    wg_re, wg_im = wg[0].reshape(wd_re.shape), wg[1].reshape(wd_re.shape)
+    for c in copies:
+        c.wait()
+    wg_re = window(m_ref, b_ref, 0)
+    wg_im = window(m_ref, b_ref, 1)
     sum_ref[0:1] = fold(wg_re * wd_re + wg_im * wd_im)
     sum_ref[1:2] = fold(wg_re * wd_im - wg_im * wd_re)
     sum_ref[2:3] = fold(wg_re * wg_re + wg_im * wg_im)
-    for c in outs:
-        c.wait()
 
 
 def k_final(me_ref, slot_ref, wd_ref, wg_ref, sums_ref, wav_ref, damp_ref, nw_ref, out_ref, wd, wg, buf, sem, osem):
@@ -281,22 +299,23 @@
         k_window, wide, [ANY] * (slots + 1), HBM, flops=flops,
         scratch=window_scratch, limit=WIN,
     )(*masked, coupling)
-    wg_slot = call(
-        k_window, wide, [ANY] * (slots + 1), HBM, flops=flops,
-        scratch=window_scratch, limit=WIN,
-    )(*[arrived[b] for b in range(slots)], coupling)
-
-    sums, own_group = call(
-        k_cross,
-        (jax.ShapeDtypeStruct((3, f), F32), jax.ShapeDtypeStruct((slots, 2, rows, f), BF16)),
-        [SM, SM, ANY, ANY, HBM], [VM, HBM],
-        scratch=[coup, w_block, x_block, b_block, dma, dma((2,)), dma((slots,)), dma((slots,))],
-        limit=CRS, flops=flops,
-    )(me, shot_order, own_natural.reshape(pieces, held, 2, rb, f), coupling, wg_slot)
+    own_group = call(
+        k_group, jax.ShapeDtypeStruct((slots, 2, rows, f), BF16), [SM, VM], HBM,
+        scratch=[pltpu.VMEM((slots, 2, rows, f), BF16), dma((slots,))], limit=GRP,
+    )(shot_order, own_natural.reshape(pieces, held, 2, rb, f))
     own_here = lax.all_to_all(own_group, SHOT, 0, 0, tiled=True)
+    sums = call(
+        k_cross, jax.ShapeDtypeStruct((3, f), F32), [SM] + [ANY] * (slots + 2),
+        scratch=[coup, x_block, x_block, b_block, dma, dma((slots,)), dma((slots,))],
+        limit=CRS, flops=2 * flops,
+    )(me, own_group, coupling, *[arrived[b] for b in range(slots)])
     sums = sums.reshape(3 * f // 128, 128)
-    for axis in ("c", "zl", "zm", "zh"):
+    for axis in ("c", "zl"):
         sums = sums + swapped(sums, axis, 1)
+    others = {}
+    for bit in (2, 1, 3):
+        others[bit] = swapped(sums, ("zh", "zm"), bit)
+    sums = (sums + others[1]) + (others[2] + others[3])
     parts = sent_to_all(sums.reshape(1, 3 * f), REST)
     wd_here = call(
         k_window_own, wide, [SM, ANY, ANY, ANY], HBM, flops=flops, limit=MID,

time: 98.2 us -> 120 us (1.22)
  blocking collectives: 0 us -> 38.3 us
  starting transfers between devices: 45.4 us -> 38.3 us
  waiting for transfers between devices: 23.3 us -> 19 us
  Pallas kernels: 21.8 us -> 18.5 us
  local copies, waits for them, and re-layouts: 5.94 us -> 3.2 us
    all_to_all x0 -> x1, blocking collectives: none -> 38.3 us  [update(): own_natural = lax.all_to_all(own_spread, RCV, 0, 0, tiled=True)]
    all_to_all x1 -> x0, starting transfers between devices: 9.93 us -> none  [update(): own_natural = lax.all_to_all(own_spread, RCV, 0, 0, tiled=True)]
    pallas_call x2 -> x1, Pallas kernels: 8.84 us -> 4.39 us  [update(): call(k_window, wide, [ANY] * (slots + 1), HBM, flops=flops, scratch=windo...]
    ppermute x11 -> x12, waiting for transfers between devices: 20.1 us -> 15.6 us  [swapped(): return lax.ppermute(x, axis, [(i, i ^ bit) for i in range(size)])]
    unnamed x52 -> x32, local copies, waits for them, and re-layouts: 5.24 us -> 2.5 us
    ppermute x11 -> x12, starting transfers between devices: 21.7 us -> 24.1 us  [swapped(): return lax.ppermute(x, axis, [(i, i ^ bit) for i in range(size)])]
    pallas_call x1 -> x2, Pallas kernels: 4.7 us -> 5.91 us  [the longest x1 4.31 us: update(): call(k_cross, jax.ShapeDtypeStruct((3, f), F32), [SM] + [ANY] * (slots +...]
  transfers between devices with their start and end apart: 14 -> 14, of which waited for: 7 -> 6; matrix products, arithmetic and copies ran while one was open for 0% -> 0% of each run, Pallas kernels for 12% -> 9%
where the time goes in v4:
time: 120 us; the launch traced here: 118 us
  blocking collectives  38.3 us (32%)
  starting transfers between devices  38.3 us (32%)
  waiting for transfers between devices  19 us (16%)
  Pallas kernels  18.5 us (15%)
  local copies, waits for them, and re-layouts  3.2 us (3%)
    all_to_all x1, blocking collectives, update(): own_natural = lax.all_to_all(own_spread, RCV, 0, 0, tiled=True)  38.3 us
    ppermute x12, starting transfers between devices, swapped(): return lax.ppermute(x, axis, [(i, i ^ bit) for i in range(size)])  24.1 us
    ppermute x12, waiting for transfers between devices, swapped(): return lax.ppermute(x, axis, [(i, i ^ bit) for i in range(size)])  15.6 us
    all_to_all x1, starting transfers between devices, update(): own_here = lax.all_to_all(own_group, SHOT, 0, 0, tiled=True)  7.23 us
    all_to_all x1, starting transfers between devices, sent_to_all(): lax.all_to_all(jnp.broadcast_to(array[None], (size, *array.shape)), axis,...  6.99 us
    pallas_call x1, Pallas kernels, update(): call(k_window, wide, [ANY] * (slots + 1), HBM, flops=flops, scratch=windo...  4.39 us
    pallas_call x1, Pallas kernels, update(): call(k_cross, jax.ShapeDtypeStruct((3, f), F32), [SM] + [ANY] * (slots +...  4.31 us
    pallas_call x1, Pallas kernels, update(): call(k_final, (jax.ShapeDtypeStruct((2, f), F32), jax.ShapeDtypeStruct(mo...  3.64 us
  transfers between devices with their start and end apart: 14, of which 6 were waited for; matrix products, arithmetic and copies ran while one was open for 0% of the time, Pallas kernels for 9%

profile of v4, /device:TPU:8, one launch (start us, length us, event | category | flops | bytes accessed | tf_op | source)
XLA Modules:
  0.0 118.2 jit_solution(2826057253455196686)
XLA Ops:
  0.6 2.1 %shard_map.95 = bf16[32,4,8,512]{3,2,1,0:T(8,128)(2,1)} custom-call(bf16[4,32,8,512]{3,2,1,0:T(8,128)(2,1)} %bitcast.8), custom_call_target="tpu_custom_call" | custom-call | bytes 1048576 | tf_op jit(solution)/shard_map/pallas_call | solution.py:272
  2.8 38.3 %all_to_all.15 = bf16[32,4,8,512]{3,2,1,0:T(8,128)(2,1)S(1)} all-to-all(bf16[32,4,8,512]{3,2,1,0:T(8,128)(2,1)} %shard_map.95), channel_id=1, replica_groups=mesh['xh'=2,'yh'=2,'yl'=2,'xl'=2,'zh'=2,'zm'=2,'zl'=2,'c'=2] {'xl','zh',..., dimensions={0} | all-to-all | bytes 2097152 | tf_op jit(solution)/shard_map/all_to_all | solution.py:281
  41.0 1.6 %shard_map.96.own_ref = bf16[8,2,64,512]{3,2,1,0:T(8,128)(2,1)} custom-call(s32[64]{0:T(128)S(1)} %copy-done.15, bf16[32,2,2,8,512]{4,3,2,1,0:T(8,128)(2,1)S(1)} %bitcast.6), custom_call_target="tpu_custom_call" | custom-call | bytes 1048576 | tf_op jit(solution)/shard_map/pallas_call | solution.py:302
  42.7 7.2 %all-to-all-start.1 = ((bf16[8,2,64,512]{3,2,1,0:T(8,128)(2,1)}), bf16[8,2,64,512]{3,2,1,0:T(8,128)(2,1)S(1)}, u32[]{:S(2)}, u32[]{:S(2)}) async-start(bf16[8,2,64,512]{3,2,1,0:T(8,128)(2,1)} %shard_map.96.own_ref), calls=%async_computation.1 | async-start | bytes 2097152 | tf_op jit(solution)/shard_map/all_to_all | solution.py:306
  49.9 0.0 copy-start.2
  49.9 1.2 %copy-done.2 = bf16[2,8,8,8,512]{4,3,2,1,0:T(8,128)(2,1)S(1)} copy-done((bf16[2,8,8,8,512]{4,3,2,1,0:T(8,128)(2,1)S(1)}, bf16[2,8,8,8,512]{4,3,2,1,0:T(8,128)(2,1)}, u32[]{:S(2)}) %copy-start.2) | copy-done | bytes 1048600
  51.1 0.8 shard_map.97
  52.0 0.1 collective-permute-start
  52.1 2.9 %collective-permute-start.1 = (bf16[2,64,512]{2,1,0:T(8,128)(2,1)S(1)}, bf16[2,64,512]{2,1,0:T(8,128)(2,1)S(1)}, u32[]{:S(2)}, u32[]{:S(2)}) collective-permute-start(bf16[2,64,512]{2,1,0:T(8,128)(2,1)S(1)} %get-tuple-element.14.refs_2_), channel_id=1, source_target_pairs={{0,64},{32,96},{64,0},{96,32},{128,192},{160,224},{192,128},{224,1... | collective-permute-start | bytes 393224 | tf_op jit(solution)/shard_map/ppermute | solution.py:252
  55.0 0.6 collective-permute-start.2
  55.6 3.0 %collective-permute-start.3 = (bf16[2,64,512]{2,1,0:T(8,128)(2,1)S(1)}, bf16[2,64,512]{2,1,0:T(8,128)(2,1)S(1)}, u32[]{:S(2)}, u32[]{:S(2)}) collective-permute-start(bf16[2,64,512]{2,1,0:T(8,128)(2,1)S(1)} %get-tuple-element.16.refs_4_), channel_id=1, source_target_pairs={{0,128},{32,160},{64,192},{96,224},{128,0},{160,32},{192,64},{224,... | collective-permute-start | bytes 393224 | tf_op jit(solution)/shard_map/ppermute | solution.py:252
  58.6 1.3 %collective-permute-start.4 = (bf16[2,64,512]{2,1,0:T(8,128)(2,1)S(1)}, bf16[2,64,512]{2,1,0:T(8,128)(2,1)S(1)}, u32[]{:S(2)}, u32[]{:S(2)}) collective-permute-start(bf16[2,64,512]{2,1,0:T(8,128)(2,1)S(1)} %get-tuple-element.17.refs_5_), channel_id=1, source_target_pairs={{0,160},{32,128},{64,224},{96,192},{128,32},{160,0},{192,96},{224,... | collective-permute-start | bytes 393224 | tf_op jit(solution)/shard_map/ppermute | solution.py:252
  59.9 6.0 %collective-permute-done.refs_1_ = bf16[2,64,512]{2,1,0:T(8,128)(2,1)S(1)} collective-permute-done((bf16[2,64,512]{2,1,0:T(8,128)(2,1)S(1)}, bf16[2,64,512]{2,1,0:T(8,128)(2,1)S(1)}, u32[]{:S(2)}, u32[]{:S(2)}) %collective-permute-start) | collective-permute-done | bytes 131104 | tf_op jit(solution)/shard_map/ppermute | solution.py:252
  65.8 6.5 %collective-permute-start.5 = (bf16[2,64,512]{2,1,0:T(8,128)(2,1)S(1)}, bf16[2,64,512]{2,1,0:T(8,128)(2,1)S(1)}, u32[]{:S(2)}, u32[]{:S(2)}) collective-permute-start(bf16[2,64,512]{2,1,0:T(8,128)(2,1)S(1)} %get-tuple-element.18.refs_6_), channel_id=1, source_target_pairs={{0,192},{32,224},{64,128},{96,160},{128,64},{160,96},{192,0},{224,... | collective-permute-start | bytes 393224 | tf_op jit(solution)/shard_map/ppermute | solution.py:252
  72.3 0.5 collective-permute-start.6
  72.9 3.1 %collective-permute-done.5.refs_6_ = bf16[2,64,512]{2,1,0:T(8,128)(2,1)S(1)} collective-permute-done((bf16[2,64,512]{2,1,0:T(8,128)(2,1)S(1)}, bf16[2,64,512]{2,1,0:T(8,128)(2,1)S(1)}, u32[]{:S(2)}, u32[]{:S(2)}) %collective-permute-start.5) | collective-permute-done | bytes 131104 | tf_op jit(solution)/shard_map/ppermute | solution.py:252
  76.0 3.7 %collective-permute-done.6.refs_7_ = bf16[2,64,512]{2,1,0:T(8,128)(2,1)S(1)} collective-permute-done((bf16[2,64,512]{2,1,0:T(8,128)(2,1)S(1)}, bf16[2,64,512]{2,1,0:T(8,128)(2,1)S(1)}, u32[]{:S(2)}, u32[]{:S(2)}) %collective-permute-start.6) | collective-permute-done | bytes 131104 | tf_op jit(solution)/shard_map/ppermute | solution.py:252
  79.7 4.3 %shard_map.100 = f32[3,512]{1,0:T(4,128)S(1)} custom-call(s32[1]{0:T(128)} %bitcast.me_ref, bf16[8,2,64,512]{3,2,1,0:T(8,128)(2,1)} %shard_map.96.own_ref, bf16[2,512,512]{2,1,0:T(8,128)(2,1)S(1)} %copy-done, bf16[2,64,512]{2,1,0:T(8,128)(2,1)S(1)} %get-tuple-element.12.refs_0_, bf16[2,64,512]{2,1,0:T(8,128)(2,1)S(1)} %collective-permute-done.refs_1_, ...), custom_call_target="tpu_custom_call" | custom-call | flops 2147483648 | bytes 1048576 | tf_op jit(solution)/shard_map/pallas_call | solution.py:307
  84.1 0.1 collective-permute-start.7
  84.2 1.2 collective-permute-done.7
  85.4 2.6 %collective-permute-start.8 = (f32[12,128]{1,0:T(8,128)S(1)}, f32[12,128]{1,0:T(8,128)S(1)}, u32[]{:S(2)}, u32[]{:S(2)}) collective-permute-start(f32[12,128]{1,0:T(8,128)S(1)} %add.23), channel_id=1, source_target_pairs={{0,2},{2,0},{1,3},{3,1},{4,6},{6,4},{5,7},{7,5},{8,10},{10,8},{9,1... | collective-permute-start | bytes 18440 | tf_op jit(solution)/shard_map/ppermute | solution.py:252
  88.0 1.6 %collective-permute-done.8 = f32[12,128]{1,0:T(8,128)S(1)} collective-permute-done((f32[12,128]{1,0:T(8,128)S(1)}, f32[12,128]{1,0:T(8,128)S(1)}, u32[]{:S(2)}, u32[]{:S(2)}) %collective-permute-start.8) | collective-permute-done | bytes 6176 | tf_op jit(solution)/shard_map/ppermute | solution.py:252
  89.6 2.3 %collective-permute-start.11 = (f32[12,128]{1,0:T(8,128)S(1)}, f32[12,128]{1,0:T(8,128)S(1)}, u32[]{:S(2)}, u32[]{:S(2)}) collective-permute-start(f32[12,128]{1,0:T(8,128)S(1)} %add.24), channel_id=1, source_target_pairs={{0,12},{4,8},{8,4},{12,0},{1,13},{5,9},{9,5},{13,1},{2,14},{6,10},... | collective-permute-start | bytes 18440 | tf_op jit(solution)/shard_map/ppermute | solution.py:252
  91.9 2.7 %collective-permute-start.10 = (f32[12,128]{1,0:T(8,128)S(1)}, f32[12,128]{1,0:T(8,128)S(1)}, u32[]{:S(2)}, u32[]{:S(2)}) collective-permute-start(f32[12,128]{1,0:T(8,128)S(1)} %add.24), channel_id=1, source_target_pairs={{0,8},{4,12},{8,0},{12,4},{1,9},{5,13},{9,1},{13,5},{2,10},{6,14},... | collective-permute-start | bytes 18440 | tf_op jit(solution)/shard_map/ppermute | solution.py:252
  94.6 1.5 %collective-permute-start.9 = (f32[12,128]{1,0:T(8,128)S(1)}, f32[12,128]{1,0:T(8,128)S(1)}, u32[]{:S(2)}, u32[]{:S(2)}) collective-permute-start(f32[12,128]{1,0:T(8,128)S(1)} %add.24), channel_id=1, source_target_pairs={{0,4},{4,0},{8,12},{12,8},{1,5},{5,1},{9,13},{13,9},{2,6},{6,2},{1... | collective-permute-start | bytes 18440 | tf_op jit(solution)/shard_map/ppermute | solution.py:252
  96.1 4.4 %shard_map.99.wg_ref = f32[2,8,64,512]{3,2,1,0:T(8,128)} custom-call(bf16[2,64,512]{2,1,0:T(8,128)(2,1)} %copy-done.3, bf16[2,64,512]{2,1,0:T(8,128)(2,1)} %copy-done.4, bf16[2,64,512]{2,1,0:T(8,128)(2,1)} %copy-done.5, bf16[2,64,512]{2,1,0:T(8,128)(2,1)} %copy-done.6, bf16[2,64,512]{2,1,0:T(8,128)(2,1)} %copy-done.7, bf16[2,64,512]{2,1,0:T(8,128)(2,1)} %copy-done.8, ...), custom_call_target="tpu_custom_call" | custom-call | flops 1073741824 | bytes 1048576 | tf_op jit(solution)/shard_map/pallas_call | solution.py:298
  100.6 0.7 broadcast_in_dim.8
  101.3 7.0 %all-to-all-start.2 = ((f32[16,1,1536]{2,1,0:T(1,128)}), f32[16,1,1536]{2,1,0:T(1,128)S(1)}, u32[]{:S(2)}, u32[]{:S(2)}) async-start(f32[16,1,1536]{2,1,0:T(1,128)} %broadcast_in_dim.8), calls=%async_computation.2 | async-start | bytes 196608 | tf_op jit(solution)/shard_map/all_to_all | solution.py:257
  108.3 1.2 %copy-done.1 = bf16[2,512,512]{2,1,0:T(8,128)(2,1)S(1)} copy-done((bf16[2,512,512]{2,1,0:T(8,128)(2,1)S(1)}, bf16[2,512,512]{2,1,0:T(8,128)(2,1)}, u32[]{:S(2)}) %copy-start.1) | copy-done | bytes 1048600
  109.5 1.7 %shard_map.98.wd_ref = f32[2,8,64,512]{3,2,1,0:T(8,128)S(1)} custom-call(s32[1]{0:T(128)} %bitcast.me_ref, bf16[8,2,64,512]{3,2,1,0:T(8,128)(2,1)S(1)} %all-to-all-done.1.own_ref, f32[8,64,128]{2,1,0:T(8,128)S(1)} %get-tuple-element.11.live_ref, bf16[2,512,512]{2,1,0:T(8,128)(2,1)S(1)} %copy-done.1), custom_call_target="tpu_custom_call" | custom-call | flops 1073741824 | bytes 1048576 | tf_op jit(solution)/shard_map/pallas_call | solution.py:320
  111.2 3.4 %all-to-all-done.2.sums_ref = f32[16,1,1536]{2,1,0:T(1,128)S(1)} async-done(((f32[16,1,1536]{2,1,0:T(1,128)}), f32[16,1,1536]{2,1,0:T(1,128)S(1)}, u32[]{:S(2)}, u32[]{:S(2)}) %all-to-all-start.2) | async-done | bytes 98336 | tf_op jit(solution)/shard_map/all_to_all | solution.py:257
  114.5 3.6 %shard_map.101 = (f32[2,512]{1,0:T(2,128)}, bf16[2,8,8,8,512]{4,3,2,1,0:T(8,128)(2,1)}) custom-call(s32[1]{0:T(128)} %bitcast.me_ref, s32[8]{0:T(128)S(1)} %copy-done.14, f32[2,8,64,512]{3,2,1,0:T(8,128)S(1)} %shard_map.98.wd_ref, f32[2,8,64,512]{3,2,1,0:T(8,128)} %shard_map.99.wg_ref, f32[16,1,1536]{2,1,0:T(1,128)S(1)} %all-to-all-done.2.sums_ref, ...), custom_call_target="tpu_custom_call" | custom-call | bytes 1048576 | tf_op jit(solution)/shard_map/pallas_call | solution.py:328
  (41 shorter events, 0.1 us)
Async XLA Ops:
  0.6 40.4 %copy-start.15 = (s32[64]{0:T(128)S(1)}, s32[64]{0:T(128)}, u32[]{:S(2)}) copy-start(s32[64]{0:T(128)} %order_ref.1) | copy-start | bytes 772
  41.0 8.9 %copy-start.11 = (s32[8,8,8]{2,1,0:T(8,128)S(1)}, s32[8,8,8]{2,1,0:T(8,128)}, u32[]{:S(2)}) copy-start(s32[8,8,8]{2,1,0:T(8,128)} %mask_ref.1) | copy-start | bytes 6148
  41.0 8.9 %copy-start.14 = (s32[8]{0:T(128)S(1)}, s32[8]{0:T(128)}, u32[]{:S(2)}) copy-start(s32[8]{0:T(128)} %slot_ref.3) | copy-start | bytes 100
  42.7 37.1 %copy-start = (bf16[2,512,512]{2,1,0:T(8,128)(2,1)S(1)}, bf16[2,512,512]{2,1,0:T(8,128)(2,1)}, u32[]{:S(2)}) copy-start(bf16[2,512,512]{2,1,0:T(8,128)(2,1)} %c_ref.3) | copy-start | bytes 3145732
  42.7 57.9 %all-to-all-start.1 = ((bf16[8,2,64,512]{3,2,1,0:T(8,128)(2,1)}), bf16[8,2,64,512]{3,2,1,0:T(8,128)(2,1)S(1)}, u32[]{:S(2)}, u32[]{:S(2)}) async-start(bf16[8,2,64,512]{3,2,1,0:T(8,128)(2,1)} %shard_map.96.own_ref), calls=%async_computation.1 | async-start | bytes 2097152 | tf_op jit(solution)/shard_map/all_to_all | solution.py:306
  49.9 1.2 %copy-start.2 = (bf16[2,8,8,8,512]{4,3,2,1,0:T(8,128)(2,1)S(1)}, bf16[2,8,8,8,512]{4,3,2,1,0:T(8,128)(2,1)}, u32[]{:S(2)}) copy-start(bf16[2,8,8,8,512]{4,3,2,1,0:T(8,128)(2,1)} %mod_ref.1) | copy-start | bytes 3145732
  51.9 20.9 %copy-start.7 = (bf16[2,64,512]{2,1,0:T(8,128)(2,1)}, bf16[2,64,512]{2,1,0:T(8,128)(2,1)S(1)}, u32[]{:S(2)}) copy-start(bf16[2,64,512]{2,1,0:T(8,128)(2,1)S(1)} %get-tuple-element.16.refs_4_) | copy-start | bytes 393220
  51.9 20.9 %copy-start.8 = (bf16[2,64,512]{2,1,0:T(8,128)(2,1)}, bf16[2,64,512]{2,1,0:T(8,128)(2,1)S(1)}, u32[]{:S(2)}) copy-start(bf16[2,64,512]{2,1,0:T(8,128)(2,1)S(1)} %get-tuple-element.17.refs_5_) | copy-start | bytes 393220
  52.0 20.9 %copy-start.9 = (bf16[2,64,512]{2,1,0:T(8,128)(2,1)}, bf16[2,64,512]{2,1,0:T(8,128)(2,1)S(1)}, u32[]{:S(2)}) copy-start(bf16[2,64,512]{2,1,0:T(8,128)(2,1)S(1)} %get-tuple-element.18.refs_6_) | copy-start | bytes 393220
  52.0 24.1 %copy-start.10 = (bf16[2,64,512]{2,1,0:T(8,128)(2,1)}, bf16[2,64,512]{2,1,0:T(8,128)(2,1)S(1)}, u32[]{:S(2)}) copy-start(bf16[2,64,512]{2,1,0:T(8,128)(2,1)S(1)} %get-tuple-element.19.refs_7_) | copy-start | bytes 393220
  52.0 32.1 %copy-start.3 = (bf16[2,64,512]{2,1,0:T(8,128)(2,1)}, bf16[2,64,512]{2,1,0:T(8,128)(2,1)S(1)}, u32[]{:S(2)}) copy-start(bf16[2,64,512]{2,1,0:T(8,128)(2,1)S(1)} %get-tuple-element.12.refs_0_) | copy-start | bytes 393220
  52.0 32.1 %copy-start.4 = (bf16[2,64,512]{2,1,0:T(8,128)(2,1)}, bf16[2,64,512]{2,1,0:T(8,128)(2,1)S(1)}, u32[]{:S(2)}) copy-start(bf16[2,64,512]{2,1,0:T(8,128)(2,1)S(1)} %get-tuple-element.13.refs_1_) | copy-start | bytes 393220
  52.0 32.1 %copy-start.5 = (bf16[2,64,512]{2,1,0:T(8,128)(2,1)}, bf16[2,64,512]{2,1,0:T(8,128)(2,1)S(1)}, u32[]{:S(2)}) copy-start(bf16[2,64,512]{2,1,0:T(8,128)(2,1)S(1)} %get-tuple-element.14.refs_2_) | copy-start | bytes 393220
  52.0 32.1 %copy-start.6 = (bf16[2,64,512]{2,1,0:T(8,128)(2,1)}, bf16[2,64,512]{2,1,0:T(8,128)(2,1)S(1)}, u32[]{:S(2)}) copy-start(bf16[2,64,512]{2,1,0:T(8,128)(2,1)S(1)} %get-tuple-element.15.refs_3_) | copy-start | bytes 393220
  52.0 13.8 %collective-permute-start = (bf16[2,64,512]{2,1,0:T(8,128)(2,1)S(1)}, bf16[2,64,512]{2,1,0:T(8,128)(2,1)S(1)}, u32[]{:S(2)}, u32[]{:S(2)}) collective-permute-start(bf16[2,64,512]{2,1,0:T(8,128)(2,1)S(1)} %get-tuple-element.13.refs_1_), channel_id=1, source_target_pairs={{0,32},{32,0},{64,96},{96,64},{128,160},{160,128},{192,224},{224,1... | collective-permute-start | bytes 393224 | tf_op jit(solution)/shard_map/ppermute | solution.py:252
  52.1 20.2 %collective-permute-start.1 = (bf16[2,64,512]{2,1,0:T(8,128)(2,1)S(1)}, bf16[2,64,512]{2,1,0:T(8,128)(2,1)S(1)}, u32[]{:S(2)}, u32[]{:S(2)}) collective-permute-start(bf16[2,64,512]{2,1,0:T(8,128)(2,1)S(1)} %get-tuple-element.14.refs_2_), channel_id=1, source_target_pairs={{0,64},{32,96},{64,0},{96,32},{128,192},{160,224},{192,128},{224,1... | collective-permute-start | bytes 393224 | tf_op jit(solution)/shard_map/ppermute | solution.py:252
  55.0 17.8 %collective-permute-start.2 = (bf16[2,64,512]{2,1,0:T(8,128)(2,1)S(1)}, bf16[2,64,512]{2,1,0:T(8,128)(2,1)S(1)}, u32[]{:S(2)}, u32[]{:S(2)}) collective-permute-start(bf16[2,64,512]{2,1,0:T(8,128)(2,1)S(1)} %get-tuple-element.15.refs_3_), channel_id=1, source_target_pairs={{0,96},{32,64},{64,32},{96,0},{128,224},{160,192},{192,160},{224,1... | collective-permute-start | bytes 393224 | tf_op jit(solution)/shard_map/ppermute | solution.py:252
  55.6 17.3 %collective-permute-start.3 = (bf16[2,64,512]{2,1,0:T(8,128)(2,1)S(1)}, bf16[2,64,512]{2,1,0:T(8,128)(2,1)S(1)}, u32[]{:S(2)}, u32[]{:S(2)}) collective-permute-start(bf16[2,64,512]{2,1,0:T(8,128)(2,1)S(1)} %get-tuple-element.16.refs_4_), channel_id=1, source_target_pairs={{0,128},{32,160},{64,192},{96,224},{128,0},{160,32},{192,64},{224,... | collective-permute-start | bytes 393224 | tf_op jit(solution)/shard_map/ppermute | solution.py:252
  58.6 14.3 %collective-permute-start.4 = (bf16[2,64,512]{2,1,0:T(8,128)(2,1)S(1)}, bf16[2,64,512]{2,1,0:T(8,128)(2,1)S(1)}, u32[]{:S(2)}, u32[]{:S(2)}) collective-permute-start(bf16[2,64,512]{2,1,0:T(8,128)(2,1)S(1)} %get-tuple-element.17.refs_5_), channel_id=1, source_target_pairs={{0,160},{32,128},{64,224},{96,192},{128,32},{160,0},{192,96},{224,... | collective-permute-start | bytes 393224 | tf_op jit(solution)/shard_map/ppermute | solution.py:252
  65.8 10.2 %collective-permute-start.5 = (bf16[2,64,512]{2,1,0:T(8,128)(2,1)S(1)}, bf16[2,64,512]{2,1,0:T(8,128)(2,1)S(1)}, u32[]{:S(2)}, u32[]{:S(2)}) collective-permute-start(bf16[2,64,512]{2,1,0:T(8,128)(2,1)S(1)} %get-tuple-element.18.refs_6_), channel_id=1, source_target_pairs={{0,192},{32,224},{64,128},{96,160},{128,64},{160,96},{192,0},{224,... | collective-permute-start | bytes 393224 | tf_op jit(solution)/shard_map/ppermute | solution.py:252
  72.3 7.4 %collective-permute-start.6 = (bf16[2,64,512]{2,1,0:T(8,128)(2,1)S(1)}, bf16[2,64,512]{2,1,0:T(8,128)(2,1)S(1)}, u32[]{:S(2)}, u32[]{:S(2)}) collective-permute-start(bf16[2,64,512]{2,1,0:T(8,128)(2,1)S(1)} %get-tuple-element.19.refs_7_), channel_id=1, source_target_pairs={{0,224},{32,192},{64,160},{96,128},{128,96},{160,64},{192,32},{224... | collective-permute-start | bytes 393224 | tf_op jit(solution)/shard_map/ppermute | solution.py:252
  84.1 1.3 %collective-permute-start.7 = (f32[12,128]{1,0:T(8,128)S(1)}, f32[12,128]{1,0:T(8,128)S(1)}, u32[]{:S(2)}, u32[]{:S(2)}) collective-permute-start(f32[12,128]{1,0:T(8,128)S(1)} %reshape.25), channel_id=1, source_target_pairs={{0,1},{1,0},{2,3},{3,2},{4,5},{5,4},{6,7},{7,6},{8,9},{9,8},{10,11... | collective-permute-start | bytes 18440 | tf_op jit(solution)/shard_map/ppermute | solution.py:252
  85.4 4.3 %collective-permute-start.8 = (f32[12,128]{1,0:T(8,128)S(1)}, f32[12,128]{1,0:T(8,128)S(1)}, u32[]{:S(2)}, u32[]{:S(2)}) collective-permute-start(f32[12,128]{1,0:T(8,128)S(1)} %add.23), channel_id=1, source_target_pairs={{0,2},{2,0},{1,3},{3,1},{4,6},{6,4},{5,7},{7,5},{8,10},{10,8},{9,1... | collective-permute-start | bytes 18440 | tf_op jit(solution)/shard_map/ppermute | solution.py:252
  89.6 10.9 %collective-permute-start.11 = (f32[12,128]{1,0:T(8,128)S(1)}, f32[12,128]{1,0:T(8,128)S(1)}, u32[]{:S(2)}, u32[]{:S(2)}) collective-permute-start(f32[12,128]{1,0:T(8,128)S(1)} %add.24), channel_id=1, source_target_pairs={{0,12},{4,8},{8,4},{12,0},{1,13},{5,9},{9,5},{13,1},{2,14},{6,10},... | collective-permute-start | bytes 18440 | tf_op jit(solution)/shard_map/ppermute | solution.py:252
  91.9 8.6 %collective-permute-start.10 = (f32[12,128]{1,0:T(8,128)S(1)}, f32[12,128]{1,0:T(8,128)S(1)}, u32[]{:S(2)}, u32[]{:S(2)}) collective-permute-start(f32[12,128]{1,0:T(8,128)S(1)} %add.24), channel_id=1, source_target_pairs={{0,8},{4,12},{8,0},{12,4},{1,9},{5,13},{9,1},{13,5},{2,10},{6,14},... | collective-permute-start | bytes 18440 | tf_op jit(solution)/shard_map/ppermute | solution.py:252
  94.6 5.9 %collective-permute-start.9 = (f32[12,128]{1,0:T(8,128)S(1)}, f32[12,128]{1,0:T(8,128)S(1)}, u32[]{:S(2)}, u32[]{:S(2)}) collective-permute-start(f32[12,128]{1,0:T(8,128)S(1)} %add.24), channel_id=1, source_target_pairs={{0,4},{4,0},{8,12},{12,8},{1,5},{5,1},{9,13},{13,9},{2,6},{6,2},{1... | collective-permute-start | bytes 18440 | tf_op jit(solution)/shard_map/ppermute | solution.py:252
  101.3 13.3 %all-to-all-start.2 = ((f32[16,1,1536]{2,1,0:T(1,128)}), f32[16,1,1536]{2,1,0:T(1,128)S(1)}, u32[]{:S(2)}, u32[]{:S(2)}) async-start(f32[16,1,1536]{2,1,0:T(1,128)} %broadcast_in_dim.8), calls=%async_computation.2 | async-start | bytes 196608 | tf_op jit(solution)/shard_map/all_to_all | solution.py:257
  108.3 1.2 %copy-start.1 = (bf16[2,512,512]{2,1,0:T(8,128)(2,1)S(1)}, bf16[2,512,512]{2,1,0:T(8,128)(2,1)}, u32[]{:S(2)}) copy-start(bf16[2,512,512]{2,1,0:T(8,128)(2,1)} %c_ref.3) | copy-start | bytes 3145732
  109.5 5.1 %copy-start.12 = (f32[2,512]{1,0:T(2,128)S(1)}, f32[2,512]{1,0:T(2,128)}, u32[]{:S(2)}) copy-start(f32[2,512]{1,0:T(2,128)} %wav_ref.1) | copy-start | bytes 12292
  109.5 5.1 %copy-start.13 = (f32[512]{0:T(512)S(1)}, f32[512]{0:T(512)}, u32[]{:S(2)}) copy-start(f32[512]{0:T(512)} %param.15) | copy-start | bytes 6148

commit v5 on v4

--- a/solution.py
+++ b/solution.py
@@ -168,56 +168,55 @@
         c.wait()
 
 
-def k_cross(me_ref, own_ref, c_ref, *refs):
-    mods, (sum_ref, coup, x_ref, m_ref, b_ref, csem, osem, msem) = refs[:-8], refs[-8:]
+def k_cross(me_ref, order_ref, own_ref, c_ref, *refs):
+    mods, (sum_ref, x_ref, m_ref, b_ref, sem) = refs[:-5], refs[-5:]
     me = me_ref[0]
     groups = len(mods)
-    rows = mods[0].shape[1]
-    first = pltpu.make_async_copy(c_ref, coup, csem)
-    first.start()
-    owns = [
-        pltpu.make_async_copy(
-            own_ref.at[lax.bitwise_xor(me, b)], x_ref.at[:, pl.ds(b * rows, rows)], osem.at[b]
-        )
-        for b in range(groups)
-    ]
-    for c in owns:
-        c.start()
+    rows, f = mods[0].shape[1:]
+    rb = own_ref.shape[3]
+    size = rows // rb
     copies = [
-        pltpu.make_async_copy(mods[b], m_ref.at[:, pl.ds(b * rows, rows)], msem.at[b])
+        pltpu.make_async_copy(mods[b], m_ref.at[:, pl.ds(b * rows, rows)], sem.at[b])
         for b in range(groups)
     ]
     for c in copies:
         c.start()
-    first.wait()
-    couple(coup, b_ref)
-    for c in owns:
-        c.wait()
-    wd_re = window(x_ref, b_ref, 0)
-    wd_im = window(x_ref, b_ref, 1)
+    def couple_rows(i, carry):
+        block = f // 4
+        upper, lower = pl.ds(pl.multiple_of(i * block, block), block), pl.ds(pl.multiple_of(f + i * block, block), block)
+        re, im = c_ref[0, upper], c_ref[1, upper]
+        b_ref[0, upper] = re
+        b_ref[0, lower] = -im
+        b_ref[1, upper] = im
+        b_ref[1, lower] = re
+        return carry
+
+    lax.fori_loop(0, 4, couple_rows, 0)
+    for b in range(groups):
+        g = lax.bitwise_xor(me, b)
+        for s in range(size):
+            n = order_ref[g * size + s]
+            j = lax.shift_right_logical(n, 1)
+            h = lax.bitwise_and(n, 1)
+            row = (b * size + s) * rb
+            for c in range(2):
+                x_ref[c, row : row + rb] = own_ref[j, h, c]
+    wd_re, wd_im = window(x_ref, b_ref, 0), window(x_ref, b_ref, 1)
     for c in copies:
         c.wait()
-    wg_re = window(m_ref, b_ref, 0)
-    wg_im = window(m_ref, b_ref, 1)
+    wg_re, wg_im = window(m_ref, b_ref, 0), window(m_ref, b_ref, 1)
     sum_ref[0:1] = fold(wg_re * wd_re + wg_im * wd_im)
     sum_ref[1:2] = fold(wg_re * wd_im - wg_im * wd_re)
     sum_ref[2:3] = fold(wg_re * wg_re + wg_im * wg_im)
 
 
-def k_final(me_ref, slot_ref, wd_ref, wg_ref, sums_ref, wav_ref, damp_ref, nw_ref, out_ref, wd, wg, buf, sem, osem):
+def k_final(me_ref, slot_ref, wd, wg_ref, sums_ref, wav_ref, damp_ref, nw_ref, out_ref, wg, buf, nw, sem, osem, nsem):
     me = me_ref[0]
-    _, lines, _, f = wd_ref.shape
+    _, lines, _, f = wg_ref.shape
     shots, rb = out_ref.shape[1], out_ref.shape[3]
-    ins = [
-        [
-            pltpu.make_async_copy(src.at[:, b], dst.at[:, b], sem.at[i, b])
-            for i, (src, dst) in enumerate(((wd_ref, wd), (wg_ref, wg)))
-        ]
-        for b in range(lines)
-    ]
-    for pair in ins:
-        for c in pair:
-            c.start()
+    ins = [pltpu.make_async_copy(wg_ref.at[:, b], wg.at[:, b], sem.at[b]) for b in range(lines)]
+    for c in ins:
+        c.start()
     outs = [
         pltpu.make_async_copy(
             buf.at[b], out_ref.at[:, :, slot_ref[lax.bitwise_xor(me, b)]], osem.at[b]
@@ -230,21 +229,24 @@
     scale = den + damp_ref[...]
     nw_re = wav_re + (cross_re - wav_re * den) / scale
     nw_im = wav_im + (cross_im - wav_im * den) / scale
-    nw_ref[0:1] = nw_re
-    nw_ref[1:2] = nw_im
+    nw[0:1] = nw_re
+    nw[1:2] = nw_im
     for b in range(lines):
-        for c in ins[b]:
-            c.wait()
+        ins[b].wait()
         wg_re, wg_im = wg[0, b], wg[1, b]
         out_re = wd[0, b] - (nw_re * wg_re - nw_im * wg_im)
         out_im = wd[1, b] - (nw_re * wg_im + nw_im * wg_re)
         buf[b, 0] = out_re.reshape(shots, rb, f).astype(BF16)
         buf[b, 1] = out_im.reshape(shots, rb, f).astype(BF16)
-        if b:
+        if b == 0:
+            last = pltpu.make_async_copy(nw, nw_ref, nsem)
+            last.start()
+        else:
             outs[b - 1].start()
     outs[-1].start()
     for c in outs:
         c.wait()
+    last.wait()
 
 
 def swapped(x, axis, bit):
@@ -305,10 +307,10 @@
     )(shot_order, own_natural.reshape(pieces, held, 2, rb, f))
     own_here = lax.all_to_all(own_group, SHOT, 0, 0, tiled=True)
     sums = call(
-        k_cross, jax.ShapeDtypeStruct((3, f), F32), [SM] + [ANY] * (slots + 2),
-        scratch=[coup, x_block, x_block, b_block, dma, dma((slots,)), dma((slots,))],
+        k_cross, jax.ShapeDtypeStruct((3, f), F32), [SM, SM, VM, VM] + [ANY] * slots,
+        scratch=[x_block, x_block, b_block, dma((slots,))],
         limit=CRS, flops=2 * flops,
-    )(me, own_group, coupling, *[arrived[b] for b in range(slots)])
+    )(me, shot_order, own_natural.reshape(pieces, held, 2, rb, f), coupling, *[arrived[b] for b in range(slots)])
     sums = sums.reshape(3 * f // 128, 128)
     for axis in ("c", "zl"):
         sums = sums + swapped(sums, axis, 1)
@@ -328,13 +330,10 @@
     new_wavelet, residual = call(
         k_final,
         (jax.ShapeDtypeStruct((2, f), F32), jax.ShapeDtypeStruct(modeled.shape, BF16)),
-        [SM, SM, HBM, HBM, VM, VM, VM], [VM, HBM],
+        [SM, SM, VM, HBM, VM, VM, VM], [HBM, HBM],
         scratch=[
-            pltpu.VMEM((2, slots, rows, f), F32),
-            pltpu.VMEM((2, slots, rows, f), F32),
-            pltpu.VMEM((slots, 2, shots, rb, f), BF16),
-            pltpu.SemaphoreType.DMA((2, slots)),
-            pltpu.SemaphoreType.DMA((slots,)),
+            w_block, pltpu.VMEM((slots, 2, shots, rb, f), BF16), pltpu.VMEM((2, f), F32),
+            dma((slots,)), dma((slots,)), dma,
         ],
         limit=FIN,
     )(me, line_of_slot, wd_here, wg_here, parts, wavelet, damping.reshape(1, f))

time: 120 us -> 120 us (level)
  local copies, waits for them, and re-layouts: 3.2 us -> 4.41 us
    unnamed x32, local copies, waits for them, and re-layouts: 2.5 us -> 3.71 us
where the time goes in v5:
time: 120 us; the launch traced here: 118 us
  blocking collectives  38.3 us (32%)
  starting transfers between devices  38 us (32%)
  waiting for transfers between devices  18.6 us (16%)
  Pallas kernels  17.8 us (15%)
  local copies, waits for them, and re-layouts  4.41 us (4%)
    all_to_all x1, blocking collectives, update(): own_natural = lax.all_to_all(own_spread, RCV, 0, 0, tiled=True)  38.3 us
    ppermute x12, starting transfers between devices, swapped(): return lax.ppermute(x, axis, [(i, i ^ bit) for i in range(size)])  23.8 us
    ppermute x12, waiting for transfers between devices, swapped(): return lax.ppermute(x, axis, [(i, i ^ bit) for i in range(size)])  15.2 us
    all_to_all x1, starting transfers between devices, update(): own_here = lax.all_to_all(own_group, SHOT, 0, 0, tiled=True)  7.23 us
    all_to_all x1, starting transfers between devices, sent_to_all(): lax.all_to_all(jnp.broadcast_to(array[None], (size, *array.shape)), axis,...  6.99 us
    pallas_call x1, Pallas kernels, update(): call(k_window, wide, [ANY] * (slots + 1), HBM, flops=flops, scratch=windo...  4.39 us
    pallas_call x1, Pallas kernels, update(): call(k_cross, jax.ShapeDtypeStruct((3, f), F32), [SM, SM, VM, VM] + [ANY]...  4.25 us
    unnamed x32, local copies, waits for them, and re-layouts  3.71 us
  transfers between devices with their start and end apart: 14, of which 6 were waited for; matrix products, arithmetic and copies ran while one was open for 0% of the time, Pallas kernels for 9%

profile of v5, /device:TPU:8, one launch (start us, length us, event | category | flops | bytes accessed | tf_op | source)
XLA Modules:
  0.0 117.9 jit_solution(4571684984544862901)
XLA Ops:
  0.6 2.1 %shard_map.95 = bf16[32,4,8,512]{3,2,1,0:T(8,128)(2,1)} custom-call(bf16[4,32,8,512]{3,2,1,0:T(8,128)(2,1)} %bitcast.9), custom_call_target="tpu_custom_call" | custom-call | bytes 1048576 | tf_op jit(solution)/shard_map/pallas_call | solution.py:274
  2.8 38.3 %all_to_all.15 = bf16[32,4,8,512]{3,2,1,0:T(8,128)(2,1)S(1)} all-to-all(bf16[32,4,8,512]{3,2,1,0:T(8,128)(2,1)} %shard_map.95), channel_id=1, replica_groups=mesh['xh'=2,'yh'=2,'yl'=2,'xl'=2,'zh'=2,'zm'=2,'zl'=2,'c'=2] {'xl','zh',..., dimensions={0} | all-to-all | bytes 2097152 | tf_op jit(solution)/shard_map/all_to_all | solution.py:283
  41.0 1.6 %shard_map.96 = bf16[8,2,64,512]{3,2,1,0:T(8,128)(2,1)} custom-call(s32[64]{0:T(128)S(1)} %copy-done.15, bf16[32,2,2,8,512]{4,3,2,1,0:T(8,128)(2,1)S(1)} %bitcast.6), custom_call_target="tpu_custom_call" | custom-call | bytes 1048576 | tf_op jit(solution)/shard_map/pallas_call | solution.py:304
  42.7 7.2 %all-to-all-start.1 = ((bf16[8,2,64,512]{3,2,1,0:T(8,128)(2,1)}), bf16[8,2,64,512]{3,2,1,0:T(8,128)(2,1)S(1)}, u32[]{:S(2)}, u32[]{:S(2)}) async-start(bf16[8,2,64,512]{3,2,1,0:T(8,128)(2,1)} %shard_map.96), calls=%async_computation.1 | async-start | bytes 2097152 | tf_op jit(solution)/shard_map/all_to_all | solution.py:308
  49.9 1.2 %copy-done.2 = bf16[2,8,8,8,512]{4,3,2,1,0:T(8,128)(2,1)S(1)} copy-done((bf16[2,8,8,8,512]{4,3,2,1,0:T(8,128)(2,1)S(1)}, bf16[2,8,8,8,512]{4,3,2,1,0:T(8,128)(2,1)}, u32[]{:S(2)}) %copy-start.2) | copy-done | bytes 1048600
  51.1 0.8 shard_map.97
  52.0 0.6 copy-done.4
  52.6 0.0 collective-permute-start
  52.6 2.9 %collective-permute-start.1 = (bf16[2,64,512]{2,1,0:T(8,128)(2,1)S(1)}, bf16[2,64,512]{2,1,0:T(8,128)(2,1)S(1)}, u32[]{:S(2)}, u32[]{:S(2)}) collective-permute-start(bf16[2,64,512]{2,1,0:T(8,128)(2,1)S(1)} %get-tuple-element.14.refs_2_), channel_id=1, source_target_pairs={{0,64},{32,96},{64,0},{96,32},{128,192},{160,224},{192,128},{224,1... | collective-permute-start | bytes 393224 | tf_op jit(solution)/shard_map/ppermute | solution.py:254
  55.5 0.6 collective-permute-start.2
  56.1 3.0 %collective-permute-start.3 = (bf16[2,64,512]{2,1,0:T(8,128)(2,1)S(1)}, bf16[2,64,512]{2,1,0:T(8,128)(2,1)S(1)}, u32[]{:S(2)}, u32[]{:S(2)}) collective-permute-start(bf16[2,64,512]{2,1,0:T(8,128)(2,1)S(1)} %get-tuple-element.16.refs_4_), channel_id=1, source_target_pairs={{0,128},{32,160},{64,192},{96,224},{128,0},{160,32},{192,64},{224,... | collective-permute-start | bytes 393224 | tf_op jit(solution)/shard_map/ppermute | solution.py:254
  59.0 1.2 %collective-permute-start.4 = (bf16[2,64,512]{2,1,0:T(8,128)(2,1)S(1)}, bf16[2,64,512]{2,1,0:T(8,128)(2,1)S(1)}, u32[]{:S(2)}, u32[]{:S(2)}) collective-permute-start(bf16[2,64,512]{2,1,0:T(8,128)(2,1)S(1)} %get-tuple-element.17.refs_5_), channel_id=1, source_target_pairs={{0,160},{32,128},{64,224},{96,192},{128,32},{160,0},{192,96},{224,... | collective-permute-start | bytes 393224 | tf_op jit(solution)/shard_map/ppermute | solution.py:254
  60.3 5.6 %collective-permute-done.refs_1_ = bf16[2,64,512]{2,1,0:T(8,128)(2,1)S(1)} collective-permute-done((bf16[2,64,512]{2,1,0:T(8,128)(2,1)S(1)}, bf16[2,64,512]{2,1,0:T(8,128)(2,1)S(1)}, u32[]{:S(2)}, u32[]{:S(2)}) %collective-permute-start) | collective-permute-done | bytes 131104 | tf_op jit(solution)/shard_map/ppermute | solution.py:254
  65.8 6.5 %collective-permute-start.5 = (bf16[2,64,512]{2,1,0:T(8,128)(2,1)S(1)}, bf16[2,64,512]{2,1,0:T(8,128)(2,1)S(1)}, u32[]{:S(2)}, u32[]{:S(2)}) collective-permute-start(bf16[2,64,512]{2,1,0:T(8,128)(2,1)S(1)} %get-tuple-element.18.refs_6_), channel_id=1, source_target_pairs={{0,192},{32,224},{64,128},{96,160},{128,64},{160,96},{192,0},{224,... | collective-permute-start | bytes 393224 | tf_op jit(solution)/shard_map/ppermute | solution.py:254
  72.4 0.5 collective-permute-start.6
  72.9 3.1 %collective-permute-done.5.refs_6_ = bf16[2,64,512]{2,1,0:T(8,128)(2,1)S(1)} collective-permute-done((bf16[2,64,512]{2,1,0:T(8,128)(2,1)S(1)}, bf16[2,64,512]{2,1,0:T(8,128)(2,1)S(1)}, u32[]{:S(2)}, u32[]{:S(2)}) %collective-permute-start.5) | collective-permute-done | bytes 131104 | tf_op jit(solution)/shard_map/ppermute | solution.py:254
  76.0 3.7 %collective-permute-done.6.refs_7_ = bf16[2,64,512]{2,1,0:T(8,128)(2,1)S(1)} collective-permute-done((bf16[2,64,512]{2,1,0:T(8,128)(2,1)S(1)}, bf16[2,64,512]{2,1,0:T(8,128)(2,1)S(1)}, u32[]{:S(2)}, u32[]{:S(2)}) %collective-permute-start.6) | collective-permute-done | bytes 131104 | tf_op jit(solution)/shard_map/ppermute | solution.py:254
  79.7 4.3 %shard_map.100 = f32[3,512]{1,0:T(4,128)S(1)} custom-call(s32[1]{0:T(128)} %bitcast.me_ref, s32[64]{0:T(128)S(1)} %copy-done.15, bf16[32,2,2,8,512]{4,3,2,1,0:T(8,128)(2,1)S(1)} %bitcast.7, bf16[2,512,512]{2,1,0:T(8,128)(2,1)S(1)} %copy-done, bf16[2,64,512]{2,1,0:T(8,128)(2,1)S(1)} %get-tuple-element.12.refs_0_, ...), custom_call_target="tpu_custom_call" | custom-call | flops 2147483648 | bytes 1048576 | tf_op jit(solution)/shard_map/pallas_call | solution.py:309
  84.0 0.6 copy-done.3
  84.6 1.2 collective-permute-done.7
  85.8 2.6 %collective-permute-start.8 = (f32[12,128]{1,0:T(8,128)S(1)}, f32[12,128]{1,0:T(8,128)S(1)}, u32[]{:S(2)}, u32[]{:S(2)}) collective-permute-start(f32[12,128]{1,0:T(8,128)S(1)} %add.23), channel_id=1, source_target_pairs={{0,2},{2,0},{1,3},{3,1},{4,6},{6,4},{5,7},{7,5},{8,10},{10,8},{9,1... | collective-permute-start | bytes 18440 | tf_op jit(solution)/shard_map/ppermute | solution.py:254
  88.4 1.6 %collective-permute-done.8 = f32[12,128]{1,0:T(8,128)S(1)} collective-permute-done((f32[12,128]{1,0:T(8,128)S(1)}, f32[12,128]{1,0:T(8,128)S(1)}, u32[]{:S(2)}, u32[]{:S(2)}) %collective-permute-start.8) | collective-permute-done | bytes 6176 | tf_op jit(solution)/shard_map/ppermute | solution.py:254
  90.1 2.3 %collective-permute-start.11 = (f32[12,128]{1,0:T(8,128)S(1)}, f32[12,128]{1,0:T(8,128)S(1)}, u32[]{:S(2)}, u32[]{:S(2)}) collective-permute-start(f32[12,128]{1,0:T(8,128)S(1)} %add.24), channel_id=1, source_target_pairs={{0,12},{4,8},{8,4},{12,0},{1,13},{5,9},{9,5},{13,1},{2,14},{6,10},... | collective-permute-start | bytes 18440 | tf_op jit(solution)/shard_map/ppermute | solution.py:254
  92.4 2.7 %collective-permute-start.10 = (f32[12,128]{1,0:T(8,128)S(1)}, f32[12,128]{1,0:T(8,128)S(1)}, u32[]{:S(2)}, u32[]{:S(2)}) collective-permute-start(f32[12,128]{1,0:T(8,128)S(1)} %add.24), channel_id=1, source_target_pairs={{0,8},{4,12},{8,0},{12,4},{1,9},{5,13},{9,1},{13,5},{2,10},{6,14},... | collective-permute-start | bytes 18440 | tf_op jit(solution)/shard_map/ppermute | solution.py:254
  95.1 1.5 %collective-permute-start.9 = (f32[12,128]{1,0:T(8,128)S(1)}, f32[12,128]{1,0:T(8,128)S(1)}, u32[]{:S(2)}, u32[]{:S(2)}) collective-permute-start(f32[12,128]{1,0:T(8,128)S(1)} %add.24), channel_id=1, source_target_pairs={{0,4},{4,0},{8,12},{12,8},{1,5},{5,1},{9,13},{13,9},{2,6},{6,2},{1... | collective-permute-start | bytes 18440 | tf_op jit(solution)/shard_map/ppermute | solution.py:254
  96.6 4.4 %shard_map.99.wg_ref = f32[2,8,64,512]{3,2,1,0:T(8,128)} custom-call(bf16[2,64,512]{2,1,0:T(8,128)(2,1)} %copy-done.3, bf16[2,64,512]{2,1,0:T(8,128)(2,1)} %copy-done.4, bf16[2,64,512]{2,1,0:T(8,128)(2,1)} %copy-done.5, bf16[2,64,512]{2,1,0:T(8,128)(2,1)} %copy-done.6, bf16[2,64,512]{2,1,0:T(8,128)(2,1)} %copy-done.7, bf16[2,64,512]{2,1,0:T(8,128)(2,1)} %copy-done.8, ...), custom_call_target="tpu_custom_call" | custom-call | flops 1073741824 | bytes 1048576 | tf_op jit(solution)/shard_map/pallas_call | solution.py:300
  101.0 0.7 broadcast_in_dim.8
  101.7 7.0 %all-to-all-start.2 = ((f32[16,1,1536]{2,1,0:T(1,128)}), f32[16,1,1536]{2,1,0:T(1,128)S(1)}, u32[]{:S(2)}, u32[]{:S(2)}) async-start(f32[16,1,1536]{2,1,0:T(1,128)} %broadcast_in_dim.8), calls=%async_computation.2 | async-start | bytes 196608 | tf_op jit(solution)/shard_map/all_to_all | solution.py:259
  108.7 1.2 %copy-done.1 = bf16[2,512,512]{2,1,0:T(8,128)(2,1)S(1)} copy-done((bf16[2,512,512]{2,1,0:T(8,128)(2,1)S(1)}, bf16[2,512,512]{2,1,0:T(8,128)(2,1)}, u32[]{:S(2)}) %copy-start.1) | copy-done | bytes 1048600
  109.9 1.7 %shard_map.98.wd = f32[2,8,64,512]{3,2,1,0:T(8,128)S(1)} custom-call(s32[1]{0:T(128)} %bitcast.me_ref, bf16[8,2,64,512]{3,2,1,0:T(8,128)(2,1)S(1)} %all-to-all-done.1.own_ref, f32[8,64,128]{2,1,0:T(8,128)S(1)} %get-tuple-element.11.live_ref, bf16[2,512,512]{2,1,0:T(8,128)(2,1)S(1)} %copy-done.1), custom_call_target="tpu_custom_call" | custom-call | flops 1073741824 | bytes 1048576 | tf_op jit(solution)/shard_map/pallas_call | solution.py:322
  111.6 3.4 %all-to-all-done.2.sums_ref = f32[16,1,1536]{2,1,0:T(1,128)S(1)} async-done(((f32[16,1,1536]{2,1,0:T(1,128)}), f32[16,1,1536]{2,1,0:T(1,128)S(1)}, u32[]{:S(2)}, u32[]{:S(2)}) %all-to-all-start.2) | async-done | bytes 98336 | tf_op jit(solution)/shard_map/all_to_all | solution.py:259
  115.0 2.9 %shard_map.101 = (f32[2,512]{1,0:T(2,128)}, bf16[2,8,8,8,512]{4,3,2,1,0:T(8,128)(2,1)}) custom-call(s32[1]{0:T(128)} %bitcast.me_ref, s32[8]{0:T(128)S(1)} %copy-done.14, f32[2,8,64,512]{3,2,1,0:T(8,128)S(1)} %shard_map.98.wd, f32[2,8,64,512]{3,2,1,0:T(8,128)} %shard_map.99.wg_ref, f32[16,1,1536]{2,1,0:T(1,128)S(1)} %all-to-all-done.2.sums_ref, ...), custom_call_target="tpu_custom_call" | custom-call | bytes 1048576 | tf_op jit(solution)/shard_map/pallas_call | solution.py:330
  (41 shorter events, 0.1 us)
Async XLA Ops:
  0.6 40.4 %copy-start.15 = (s32[64]{0:T(128)S(1)}, s32[64]{0:T(128)}, u32[]{:S(2)}) copy-start(s32[64]{0:T(128)} %order_ref.3) | copy-start | bytes 772
  41.0 8.9 %copy-start.11 = (s32[8,8,8]{2,1,0:T(8,128)S(1)}, s32[8,8,8]{2,1,0:T(8,128)}, u32[]{:S(2)}) copy-start(s32[8,8,8]{2,1,0:T(8,128)} %mask_ref.1) | copy-start | bytes 6148
  41.0 8.9 %copy-start.14 = (s32[8]{0:T(128)S(1)}, s32[8]{0:T(128)}, u32[]{:S(2)}) copy-start(s32[8]{0:T(128)} %slot_ref.3) | copy-start | bytes 100
  42.7 37.1 %copy-start = (bf16[2,512,512]{2,1,0:T(8,128)(2,1)S(1)}, bf16[2,512,512]{2,1,0:T(8,128)(2,1)}, u32[]{:S(2)}) copy-start(bf16[2,512,512]{2,1,0:T(8,128)(2,1)} %c_ref.3) | copy-start | bytes 3145732
  42.7 58.4 %all-to-all-start.1 = ((bf16[8,2,64,512]{3,2,1,0:T(8,128)(2,1)}), bf16[8,2,64,512]{3,2,1,0:T(8,128)(2,1)S(1)}, u32[]{:S(2)}, u32[]{:S(2)}) async-start(bf16[8,2,64,512]{3,2,1,0:T(8,128)(2,1)} %shard_map.96), calls=%async_computation.1 | async-start | bytes 2097152 | tf_op jit(solution)/shard_map/all_to_all | solution.py:308
  49.9 1.2 %copy-start.2 = (bf16[2,8,8,8,512]{4,3,2,1,0:T(8,128)(2,1)S(1)}, bf16[2,8,8,8,512]{4,3,2,1,0:T(8,128)(2,1)}, u32[]{:S(2)}) copy-start(bf16[2,8,8,8,512]{4,3,2,1,0:T(8,128)(2,1)} %mod_ref.1) | copy-start | bytes 3145732
  51.9 0.6 copy-start.4
  51.9 13.9 %copy-start.5 = (bf16[2,64,512]{2,1,0:T(8,128)(2,1)}, bf16[2,64,512]{2,1,0:T(8,128)(2,1)S(1)}, u32[]{:S(2)}) copy-start(bf16[2,64,512]{2,1,0:T(8,128)(2,1)S(1)} %get-tuple-element.14.refs_2_) | copy-start | bytes 393220
  52.0 20.4 %copy-start.6 = (bf16[2,64,512]{2,1,0:T(8,128)(2,1)}, bf16[2,64,512]{2,1,0:T(8,128)(2,1)S(1)}, u32[]{:S(2)}) copy-start(bf16[2,64,512]{2,1,0:T(8,128)(2,1)S(1)} %get-tuple-element.15.refs_3_) | copy-start | bytes 393220
  52.0 20.9 %copy-start.7 = (bf16[2,64,512]{2,1,0:T(8,128)(2,1)}, bf16[2,64,512]{2,1,0:T(8,128)(2,1)S(1)}, u32[]{:S(2)}) copy-start(bf16[2,64,512]{2,1,0:T(8,128)(2,1)S(1)} %get-tuple-element.16.refs_4_) | copy-start | bytes 393220
  52.0 20.9 %copy-start.8 = (bf16[2,64,512]{2,1,0:T(8,128)(2,1)}, bf16[2,64,512]{2,1,0:T(8,128)(2,1)S(1)}, u32[]{:S(2)}) copy-start(bf16[2,64,512]{2,1,0:T(8,128)(2,1)S(1)} %get-tuple-element.17.refs_5_) | copy-start | bytes 393220
  52.0 20.9 %copy-start.9 = (bf16[2,64,512]{2,1,0:T(8,128)(2,1)}, bf16[2,64,512]{2,1,0:T(8,128)(2,1)S(1)}, u32[]{:S(2)}) copy-start(bf16[2,64,512]{2,1,0:T(8,128)(2,1)S(1)} %get-tuple-element.18.refs_6_) | copy-start | bytes 393220
  52.0 24.0 %copy-start.10 = (bf16[2,64,512]{2,1,0:T(8,128)(2,1)}, bf16[2,64,512]{2,1,0:T(8,128)(2,1)S(1)}, u32[]{:S(2)}) copy-start(bf16[2,64,512]{2,1,0:T(8,128)(2,1)S(1)} %get-tuple-element.19.refs_7_) | copy-start | bytes 393220
  52.6 13.3 %collective-permute-start = (bf16[2,64,512]{2,1,0:T(8,128)(2,1)S(1)}, bf16[2,64,512]{2,1,0:T(8,128)(2,1)S(1)}, u32[]{:S(2)}, u32[]{:S(2)}) collective-permute-start(bf16[2,64,512]{2,1,0:T(8,128)(2,1)S(1)} %get-tuple-element.13.refs_1_), channel_id=1, source_target_pairs={{0,32},{32,0},{64,96},{96,64},{128,160},{160,128},{192,224},{224,1... | collective-permute-start | bytes 393224 | tf_op jit(solution)/shard_map/ppermute | solution.py:254
  52.6 19.8 %collective-permute-start.1 = (bf16[2,64,512]{2,1,0:T(8,128)(2,1)S(1)}, bf16[2,64,512]{2,1,0:T(8,128)(2,1)S(1)}, u32[]{:S(2)}, u32[]{:S(2)}) collective-permute-start(bf16[2,64,512]{2,1,0:T(8,128)(2,1)S(1)} %get-tuple-element.14.refs_2_), channel_id=1, source_target_pairs={{0,64},{32,96},{64,0},{96,32},{128,192},{160,224},{192,128},{224,1... | collective-permute-start | bytes 393224 | tf_op jit(solution)/shard_map/ppermute | solution.py:254
  55.5 17.3 %collective-permute-start.2 = (bf16[2,64,512]{2,1,0:T(8,128)(2,1)S(1)}, bf16[2,64,512]{2,1,0:T(8,128)(2,1)S(1)}, u32[]{:S(2)}, u32[]{:S(2)}) collective-permute-start(bf16[2,64,512]{2,1,0:T(8,128)(2,1)S(1)} %get-tuple-element.15.refs_3_), channel_id=1, source_target_pairs={{0,96},{32,64},{64,32},{96,0},{128,224},{160,192},{192,160},{224,1... | collective-permute-start | bytes 393224 | tf_op jit(solution)/shard_map/ppermute | solution.py:254
  56.1 16.8 %collective-permute-start.3 = (bf16[2,64,512]{2,1,0:T(8,128)(2,1)S(1)}, bf16[2,64,512]{2,1,0:T(8,128)(2,1)S(1)}, u32[]{:S(2)}, u32[]{:S(2)}) collective-permute-start(bf16[2,64,512]{2,1,0:T(8,128)(2,1)S(1)} %get-tuple-element.16.refs_4_), channel_id=1, source_target_pairs={{0,128},{32,160},{64,192},{96,224},{128,0},{160,32},{192,64},{224,... | collective-permute-start | bytes 393224 | tf_op jit(solution)/shard_map/ppermute | solution.py:254
  59.0 13.8 %collective-permute-start.4 = (bf16[2,64,512]{2,1,0:T(8,128)(2,1)S(1)}, bf16[2,64,512]{2,1,0:T(8,128)(2,1)S(1)}, u32[]{:S(2)}, u32[]{:S(2)}) collective-permute-start(bf16[2,64,512]{2,1,0:T(8,128)(2,1)S(1)} %get-tuple-element.17.refs_5_), channel_id=1, source_target_pairs={{0,160},{32,128},{64,224},{96,192},{128,32},{160,0},{192,96},{224,... | collective-permute-start | bytes 393224 | tf_op jit(solution)/shard_map/ppermute | solution.py:254
  65.8 10.2 %collective-permute-start.5 = (bf16[2,64,512]{2,1,0:T(8,128)(2,1)S(1)}, bf16[2,64,512]{2,1,0:T(8,128)(2,1)S(1)}, u32[]{:S(2)}, u32[]{:S(2)}) collective-permute-start(bf16[2,64,512]{2,1,0:T(8,128)(2,1)S(1)} %get-tuple-element.18.refs_6_), channel_id=1, source_target_pairs={{0,192},{32,224},{64,128},{96,160},{128,64},{160,96},{192,0},{224,... | collective-permute-start | bytes 393224 | tf_op jit(solution)/shard_map/ppermute | solution.py:254
  72.4 7.4 %collective-permute-start.6 = (bf16[2,64,512]{2,1,0:T(8,128)(2,1)S(1)}, bf16[2,64,512]{2,1,0:T(8,128)(2,1)S(1)}, u32[]{:S(2)}, u32[]{:S(2)}) collective-permute-start(bf16[2,64,512]{2,1,0:T(8,128)(2,1)S(1)} %get-tuple-element.19.refs_7_), channel_id=1, source_target_pairs={{0,224},{32,192},{64,160},{96,128},{128,96},{160,64},{192,32},{224... | collective-permute-start | bytes 393224 | tf_op jit(solution)/shard_map/ppermute | solution.py:254
  84.0 0.6 copy-start.3
  84.6 1.2 collective-permute-start.7
  85.8 4.3 %collective-permute-start.8 = (f32[12,128]{1,0:T(8,128)S(1)}, f32[12,128]{1,0:T(8,128)S(1)}, u32[]{:S(2)}, u32[]{:S(2)}) collective-permute-start(f32[12,128]{1,0:T(8,128)S(1)} %add.23), channel_id=1, source_target_pairs={{0,2},{2,0},{1,3},{3,1},{4,6},{6,4},{5,7},{7,5},{8,10},{10,8},{9,1... | collective-permute-start | bytes 18440 | tf_op jit(solution)/shard_map/ppermute | solution.py:254
  90.1 10.9 %collective-permute-start.11 = (f32[12,128]{1,0:T(8,128)S(1)}, f32[12,128]{1,0:T(8,128)S(1)}, u32[]{:S(2)}, u32[]{:S(2)}) collective-permute-start(f32[12,128]{1,0:T(8,128)S(1)} %add.24), channel_id=1, source_target_pairs={{0,12},{4,8},{8,4},{12,0},{1,13},{5,9},{9,5},{13,1},{2,14},{6,10},... | collective-permute-start | bytes 18440 | tf_op jit(solution)/shard_map/ppermute | solution.py:254
  92.4 8.6 %collective-permute-start.10 = (f32[12,128]{1,0:T(8,128)S(1)}, f32[12,128]{1,0:T(8,128)S(1)}, u32[]{:S(2)}, u32[]{:S(2)}) collective-permute-start(f32[12,128]{1,0:T(8,128)S(1)} %add.24), channel_id=1, source_target_pairs={{0,8},{4,12},{8,0},{12,4},{1,9},{5,13},{9,1},{13,5},{2,10},{6,14},... | collective-permute-start | bytes 18440 | tf_op jit(solution)/shard_map/ppermute | solution.py:254
  95.1 5.9 %collective-permute-start.9 = (f32[12,128]{1,0:T(8,128)S(1)}, f32[12,128]{1,0:T(8,128)S(1)}, u32[]{:S(2)}, u32[]{:S(2)}) collective-permute-start(f32[12,128]{1,0:T(8,128)S(1)} %add.24), channel_id=1, source_target_pairs={{0,4},{4,0},{8,12},{12,8},{1,5},{5,1},{9,13},{13,9},{2,6},{6,2},{1... | collective-permute-start | bytes 18440 | tf_op jit(solution)/shard_map/ppermute | solution.py:254
  101.7 13.3 %all-to-all-start.2 = ((f32[16,1,1536]{2,1,0:T(1,128)}), f32[16,1,1536]{2,1,0:T(1,128)S(1)}, u32[]{:S(2)}, u32[]{:S(2)}) async-start(f32[16,1,1536]{2,1,0:T(1,128)} %broadcast_in_dim.8), calls=%async_computation.2 | async-start | bytes 196608 | tf_op jit(solution)/shard_map/all_to_all | solution.py:259
  108.7 1.2 %copy-start.1 = (bf16[2,512,512]{2,1,0:T(8,128)(2,1)S(1)}, bf16[2,512,512]{2,1,0:T(8,128)(2,1)}, u32[]{:S(2)}) copy-start(bf16[2,512,512]{2,1,0:T(8,128)(2,1)} %c_ref.3) | copy-start | bytes 3145732
  109.9 5.1 %copy-start.12 = (f32[2,512]{1,0:T(2,128)S(1)}, f32[2,512]{1,0:T(2,128)}, u32[]{:S(2)}) copy-start(f32[2,512]{1,0:T(2,128)} %wav_ref.1) | copy-start | bytes 12292
  109.9 5.1 %copy-start.13 = (f32[512]{0:T(512)S(1)}, f32[512]{0:T(512)}, u32[]{:S(2)}) copy-start(f32[512]{0:T(512)} %param.15) | copy-start | bytes 6148
